TPU v7x, 32 devices: a whole 2x2x4 slice. The times are simulated.
32 devices in a mesh: parts: 2 (over x), frame: 2 (over core), tile: 8 (over z, y).
Axes of the slice: x: 2, y: 2, z: 4, core: 2. Of those that a mesh axis runs over, the one named last changes fastest.
Arguments:
- decoded_refs: bfloat16 [64, 96, 64, 256], P(('parts', 'frame'), None, 'tile'), parts along dimension 0, may hold values from -6 to 6
- current_frames: bfloat16 [16, 96, 64, 256], P(('parts', 'frame'), None, 'tile'), parts along dimension 0, may hold values from -6 to 6
- ref_pairs: int32 [16, 2], P('parts'), parts along dimension 0, may hold values from 0 to 31
- ref_slots: int32 [64], P('parts'), parts along dimension 0, may hold values from 0 to 31, each once
- frame_numbers: int32 [16], P('parts'), parts along dimension 0, may hold values from 0 to 31
- rate_weights: float32 [64], P('parts'), parts along dimension 0, may hold values from 0.5 to 4
- join_kernel: bfloat16 [3, 3, 96, 288], replicated, may hold values from -0.125 to 0.125
- out_kernel: bfloat16 [3, 3, 96, 96], replicated, may hold values from -0.21875 to 0.21875
Outputs:
- reconstruction: bfloat16 [16, 96, 64, 256], P(('parts', 'frame'), None, 'tile'), parts along dimension 0
- join_grad: float32 [6, 3, 96, 288], P('parts'), parts along dimension 0
- output_grad: float32 [6, 3, 96, 96], P('parts'), parts along dimension 0
There are 2 independent parts, one for each index of `parts`. A program takes and returns all parts, laid end to end along the dimension named above; an argument that names none is the same for every part. Nothing has to cross between parts.
Inputs may be any that keep to these rules, and one draw needn't show every extreme that they name: `ref_pairs`: each B-frame names two decoded frames, possibly the same one. `ref_slots`: each slot holds exactly one decoded frame.
All inputs are finite; a program needn't handle non-finite values.
Results may differ from a plain program's by a relative error of at most 0.005.
Values may be sent and summed in bfloat16 or wider, within the bound.
No kernel may reach another device: no remote copies, remote signals or barrier semaphores. Data moves between devices by JAX's collectives and lax.ppermute only.
A program may use at most 128 MiB of HBM per device.

v0:
```python
import jax
import jax.numpy as jnp
from jax import lax
from jax.sharding import PartitionSpec as P


def partner(array, axis, stride):
    return lax.ppermute(array, axis, [(i, i ^ 1 << stride) for i in range(lax.axis_size(axis))])


def with_halo(cells, sides, width):
    for axis, dim in sides:
        count = lax.axis_size(axis)
        ends = count - 1
        head = lax.slice_in_dim(cells, 0, width, axis=dim)
        tail = lax.slice_in_dim(cells, cells.shape[dim] - width, cells.shape[dim], axis=dim)
        cells = jnp.concatenate(
            [
                lax.ppermute(tail, axis, [(i, (i + 1) % count) for i in range(ends)]),
                cells,
                lax.ppermute(head, axis, [((i + 1) % count, i) for i in range(ends)]),
            ],
            axis=dim,
        )
    return cells


def pad_cols(field):
    return jnp.pad(field, ((0, 0), (0, 0), (0, 0), (1, 1)))


def apply_taps(padded, kernel, row_count, col_count):
    running = None
    for row_tap in range(3):
        for col_tap in range(3):
            window = padded[:, :, row_tap : row_tap + row_count, col_tap : col_tap + col_count]
            partial_sum = jnp.einsum(
                "oi,bihw->bohw",
                kernel[row_tap, col_tap],
                window,
                preferred_element_type=jnp.float32,
            )
            running = partial_sum if running is None else running + partial_sum
    return running


def tap_grads(upstream, padded, row_count, col_count):
    pieces = []
    for row_tap in range(3):
        for col_tap in range(3):
            window = padded[:, :, row_tap : row_tap + row_count, col_tap : col_tap + col_count]
            pieces.append(
                jnp.einsum("bohw,bihw->oi", upstream, window, preferred_element_type=jnp.float32)
            )
    stacked = jnp.stack(pieces)
    return stacked.reshape((3, 3) + stacked.shape[1:])


def transpose_taps(padded, kernel, row_count, col_count):
    running = None
    for row_tap in range(3):
        for col_tap in range(3):
            window = padded[
                :, :, 2 - row_tap : 2 - row_tap + row_count, 2 - col_tap : 2 - col_tap + col_count
            ]
            partial_sum = jnp.einsum(
                "oi,bohw->bihw",
                kernel[row_tap, col_tap],
                window,
                preferred_element_type=jnp.float32,
            )
            running = partial_sum if running is None else running + partial_sum
    return running


def on_device(
    decoded_refs,
    current_frames,
    ref_pairs,
    ref_slots,
    frame_numbers,
    rate_weights,
    join_kernel,
    out_kernel,
):
    local_refs = decoded_refs.shape[0]
    local_frames, channels, tile_rows, col_count = current_frames.shape
    group = lax.axis_index("frame")
    frame_range = jnp.arange(ref_slots.shape[0], dtype=jnp.int32)

    def pair_slots(which):
        pairs = lax.dynamic_slice_in_dim(ref_pairs, which * local_frames, local_frames, 0)
        return jnp.sum(jnp.where(pairs[:, :, None] == frame_range, ref_slots, 0), axis=-1).reshape(
            -1
        )

    mine = pair_slots(group)
    other = pair_slots(1 - group) - group * local_refs
    other_held = (other >= 0) & (other < local_refs)
    outgoing = jnp.take(decoded_refs, jnp.clip(other, 0, local_refs - 1), axis=0)
    outgoing = jnp.where(other_held[:, None, None, None], outgoing, jnp.zeros((), jnp.bfloat16))
    incoming = partner(outgoing, "frame", 0)
    mine_local = mine - group * local_refs
    mine_held = (mine_local >= 0) & (mine_local < local_refs)
    own_tiles = jnp.take(decoded_refs, jnp.clip(mine_local, 0, local_refs - 1), axis=0)
    picked = jnp.where(mine_held[:, None, None, None], own_tiles, incoming)
    picked = picked.reshape(local_frames, 2 * channels, tile_rows, col_count)
    stacked = jnp.concatenate([picked, current_frames], axis=1)
    height = tile_rows * lax.axis_size("tile")
    stacked_pad = pad_cols(with_halo(stacked, (("tile", 2),), 1))
    preact = apply_taps(stacked_pad, join_kernel, tile_rows, col_count)
    hidden = jax.nn.silu(preact).astype(jnp.bfloat16)
    hidden_pad = pad_cols(with_halo(hidden, (("tile", 2),), 1))
    recon = apply_taps(hidden_pad, out_kernel, tile_rows, col_count)
    frames_here = lax.dynamic_slice_in_dim(frame_numbers, group * local_frames, local_frames, 0)
    gop_range = jnp.arange(rate_weights.shape[0], dtype=jnp.int32)
    weight_here = jnp.sum(jnp.where(frames_here[:, None] == gop_range, rate_weights, 0.0), axis=-1)
    residual = (
        2.0
        * weight_here[:, None, None, None]
        * (recon - current_frames.astype(jnp.float32))
        / (height * col_count)
    ).astype(jnp.bfloat16)
    output_part = tap_grads(residual, hidden_pad, tile_rows, col_count)
    residual_pad = pad_cols(with_halo(residual, (("tile", 2),), 1))
    hidden_grad = transpose_taps(residual_pad, out_kernel, tile_rows, col_count)
    sigma = jax.nn.sigmoid(preact)
    preact_grad = (hidden_grad * (sigma * (1.0 + preact * (1.0 - sigma)))).astype(jnp.bfloat16)
    join_part = tap_grads(preact_grad, stacked_pad, tile_rows, col_count)
    join_total, output_total = lax.psum((join_part, output_part), ("frame", "tile"))
    return (recon.astype(jnp.bfloat16), join_total, output_total)


def solution(mesh):
    placed = (
        P(("parts", "frame"), None, "tile", None),
        P(("parts", "frame"), None, "tile", None),
        P("parts", None),
        P("parts"),
        P("parts"),
        P("parts"),
        P(),
        P(),
    )
    return jax.shard_map(
        on_device,
        mesh=mesh,
        in_specs=placed,
        out_specs=(
            P(("parts", "frame"), None, "tile", None),
            P("parts", None, None, None),
            P("parts", None, None, None),
        ),
        check_vma=False,
    )
```

profile of v0, /device:TPU:0, one launch (start us, length us, event | category | flops | bytes accessed | tf_op | source)
XLA Modules:
  0.0 316.3 jit_solution(6652373692335212695)
XLA Ops:
  9.5 3.5 %gather_fusion.1 = bf16[8,96,8,256]{3,2,1,0:T(8,128)(2,1)S(1)} fusion(bf16[16,96,8,256]{3,2,1,0:T(8,128)(2,1)} %param.10, s32[1024]{0:T(1024)S(1)} %pad_clamp_fusion), kind=kCustom, calls=%fused_computation.1.clone | custom fusion | bytes 6291488 | tf_op jit(solution)/shard_map/jit(_take)/gather | solution.py:100
  15.9 3.5 %gather_fusion = bf16[8,96,8,256]{3,2,1,0:T(8,128)(2,1)S(1)} fusion(bf16[16,96,8,256]{3,2,1,0:T(8,128)(2,1)} %param.10, s32[1024]{0:T(1024)S(1)} %pad_clamp_fusion.1), kind=kCustom, calls=%fused_computation.clone | custom fusion | bytes 6291488 | tf_op jit(solution)/shard_map/jit(_take)/gather | solution.py:105
  25.4 4.8 %collective-permute-start.1 = (bf16[4,288,1,256]{3,1,2,0:T(8,128)(2,1)S(1)}, bf16[4,288,1,256]{3,1,2,0:T(8,128)(2,1)S(1)}, u32[]{:S(2)}, u32[]{:S(2)}) collective-permute-start(bf16[4,288,1,256]{3,1,2,0:T(8,128)(2,1)S(1)} %get-tuple-element.17), channel_id=1, source_target_pairs={{0,1},{1,2},{2,3},{3,4},{4,5},{5,6},{6,7},{8,9},{9,10},{10,11},{11... | collective-permute-start | bytes 1769480 | tf_op jit(solution)/shard_map/ppermute | solution.py:19
  31.9 3.0 fusion.184
  34.9 20.8 %collective-permute-done.1 = bf16[4,288,1,256]{3,1,2,0:T(8,128)(2,1)S(1)} collective-permute-done((bf16[4,288,1,256]{3,1,2,0:T(8,128)(2,1)S(1)}, bf16[4,288,1,256]{3,1,2,0:T(8,128)(2,1)S(1)}, u32[]{:S(2)}, u32[]{:S(2)}) %collective-permute-start.1) | collective-permute-done | bytes 589856 | tf_op jit(solution)/shard_map/ppermute | solution.py:19
  55.8 5.9 %fusion.5 = bf16[4,288,10,258]{3,1,2,0:T(8,128)(2,1)S(1)} fusion(bf16[4,288,1,256]{3,1,2,0:T(8,128)(2,1)S(1)} %collective-permute-done.2, bf16[4,288,8,256]{3,1,2,0:T(8,128)(2,1)S(1)} %copy_dynamic-update-slice_fusion.1, bf16[4,288,1,256]{3,1,2,0:T(8,128)(2,1)S(1)} %collective-permute-done.1), kind=kLoop, calls=%fused_computation.9 | loop fusion | flops 35665920 | bytes 11842560 | tf_op jit(solution)/shard_map/concatenate | solution.py:17
  61.7 3.0 fusion.13
  64.7 3.3 %fusion.17 = f32[4,8,256,96]{2,3,1,0:T(8,128)} fusion(bf16[4,288,10,258]{3,1,2,0:T(8,128)(2,1)S(1)} %fusion.5, bf16[3,3,96,288]{3,2,1,0:T(8,128)(2,1)S(1)} %copy-done.8), kind=kOutput, calls=%fused_computation.25 | convolution fusion | flops 452984832 | bytes 7938048 | tf_op jit(solution)/shard_map/oi,bihw->bohw/dot_general | solution.py:37
  68.0 3.0 fusion.21
  71.0 3.3 %fusion.25 = f32[4,8,256,96]{2,3,1,0:T(8,128)} fusion(bf16[4,288,10,258]{3,1,2,0:T(8,128)(2,1)S(1)} %fusion.5, bf16[3,3,96,288]{3,2,1,0:T(8,128)(2,1)S(1)} %copy-done.8), kind=kOutput, calls=%fused_computation.33 | convolution fusion | flops 452984832 | bytes 7938048 | tf_op jit(solution)/shard_map/oi,bihw->bohw/dot_general | solution.py:37
  74.3 3.0 fusion.29
  77.2 3.0 fusion.44
  80.3 3.0 fusion.42
  83.2 11.2 %fusion.38 = (bf16[4,96,8,256]{3,1,2,0:T(8,128)(2,1)}, f32[4,8,256,96]{2,3,1,0:T(8,128)}) fusion(bf16[4,288,10,258]{3,1,2,0:T(8,128)(2,1)S(1)} %fusion.5, bf16[3,3,96,288]{3,2,1,0:T(8,128)(2,1)} %param.16, f32[4,8,256,96]{2,3,1,0:T(8,128)} %fusion.44, f32[4,8,256,96]{2,3,1,0:T(8,128)} %fusion.13, f32[4,8,256,96]{2,3,1,0:T(8,128)} %fusion.17, ...), kind=kOutput, calls=%fused_computation.52 | convolution fusion | flops 463208448 | bytes 34676736 | tf_op jit(solution)/shard_map/oi,bihw->bohw/dot_general | solution.py:37
  95.6 4.4 %collective-permute-start.3 = (bf16[4,96,1,256]{3,1,2,0:T(8,128)(2,1)S(1)}, bf16[4,96,1,256]{3,1,2,0:T(8,128)(2,1)S(1)}, u32[]{:S(2)}, u32[]{:S(2)}) collective-permute-start(bf16[4,96,1,256]{3,1,2,0:T(8,128)(2,1)S(1)} %get-tuple-element.21), channel_id=1, source_target_pairs={{0,1},{1,2},{2,3},{3,4},{4,5},{5,6},{6,7},{8,9},{9,10},{10,11},{11... | collective-permute-start | bytes 589832 | tf_op jit(solution)/shard_map/ppermute | solution.py:19
  101.8 3.7 %fusion.209 = f32[4,8,256,96]{2,3,1,0:T(8,128)} fusion(bf16[4,96,8,256]{3,1,2,0:T(8,128)(2,1)} %get-tuple-element.25, bf16[3,3,96,96]{3,2,1,0:T(8,128)(2,1)S(1)} %copy-done.4), kind=kOutput, calls=%fused_computation.183 | convolution fusion | flops 150994944 | bytes 4743168 | tf_op jit(solution)/shard_map/oi,bihw->bohw/dot_general | solution.py:37
  105.5 3.6 %collective-permute-done.4 = bf16[4,96,1,256]{3,1,2,0:T(8,128)(2,1)S(1)} collective-permute-done((bf16[4,96,1,256]{3,1,2,0:T(8,128)(2,1)S(1)}, bf16[4,96,1,256]{3,1,2,0:T(8,128)(2,1)S(1)}, u32[]{:S(2)}, u32[]{:S(2)}) %collective-permute-start.4) | collective-permute-done | bytes 196640 | tf_op jit(solution)/shard_map/ppermute | solution.py:21
  126.9 12.3 %bitcast_convert_fusion = (bf16[4,96,8,256]{3,1,2,0:T(8,128)(2,1)}, f32[4,8,256,96]{2,3,1,0:T(8,128)}) fusion(bf16[4,96,10,258]{3,1,2,0:T(8,128)(2,1)S(1)} %select_maximum_fusion.2, bf16[3,3,96,96]{3,2,1,0:T(8,128)(2,1)S(1)} %copy-done.4, f32[4,8,256,96]{2,3,1,0:T(8,128)} %fusion.175, f32[4,8,256,96]{2,3,1,0:T(8,128)} %fusion.76, ...), kind=kOutput, calls=%fused_computation.42 | convolution fusion | flops 158072832 | bytes 31481856 | tf_op jit(solution)/shard_map/oi,bihw->bohw/dot_general | solution.py:37
  139.2 2.6 fusion.34
  146.0 5.4 %collective-permute-start.5 = (bf16[4,96,1,256]{3,1,2,0:T(8,128)(2,1)S(1)}, bf16[4,96,1,256]{3,1,2,0:T(8,128)(2,1)S(1)}, u32[]{:S(2)}, u32[]{:S(2)}) collective-permute-start(bf16[4,96,1,256]{3,1,2,0:T(8,128)(2,1)S(1)} %get-tuple-element.20), channel_id=1, source_target_pairs={{0,1},{1,2},{2,3},{3,4},{4,5},{5,6},{6,7},{8,9},{9,10},{10,11},{11... | collective-permute-start | bytes 589832 | tf_op jit(solution)/shard_map/ppermute | solution.py:19
  177.1 10.6 %fusion.31 = bf16[4,96,8,256]{3,1,2,0:T(8,128)(2,1)S(1)} fusion(f32[4,8,256,96]{2,3,1,0:T(8,128)} %get-tuple-element.26, f32[4,8,256,96]{2,3,1,0:T(8,128)} %fusion.50, f32[4,8,256,96]{2,3,1,0:T(8,128)} %fusion.58, f32[4,8,256,96]{2,3,1,0:T(8,128)} %fusion.60, f32[4,8,256,96]{2,3,1,0:T(8,128)} %fusion.207, f32[4,8,256,96]{2,3,1,0:T(8,128)} %fusion.62, ...), kind=kOutput, calls=%fused_computation.40 | convolution fusion | flops 164364288 | bytes 31481856 | tf_op jit(solution)/shard_map/oi,bohw->bihw/dot_general | solution.py:66
  206.3 3.4 %copy.56 = bf16[4,96,8,256]{3,2,1,0:T(8,128)(2,1)} copy(bf16[4,96,8,256]{3,1,2,0:T(8,128)(2,1)} %get-tuple-element.27) | data formatting | bytes 3145728
  209.7 95.2 %all-reduce.6.cloned.1.call-done = (f32[3,3,96,288]{3,2,1,0:T(8,128)}, f32[3,3,96,96]{3,2,1,0:T(8,128)}) async-done(((f32[3,3,96,288]{3,2,1,0:T(8,128)}, f32[3,3,96,96]{3,2,1,0:T(8,128)}), (f32[3,3,96,288]{3,2,1,0:T(8,128)}, f32[3,3,96,96]{3,2,1,0:T(8,128)})) %all-reduce.6.cloned.1.call-update) | async-done | bytes 1327120 | tf_op jit(solution)/shard_map/psum | solution.py:130
  304.9 2.5 copy.133
  (97 shorter events, 83.5 us)
Async XLA Ops:
  7.2 297.8 %all-reduce.6.cloned.1.call-start = ((), (), s32[]{:S(2)}) async-start(), calls=%async_computation | async-start | bytes 3538944 | tf_op jit(solution)/shard_map/psum | solution.py:130
  13.1 2.6 copy-start.9
  15.2 6.1 %collective-permute-start = (bf16[8,96,8,256]{3,2,1,0:T(8,128)(2,1)}, bf16[8,96,8,256]{3,2,1,0:T(8,128)(2,1)}, u32[]{:S(2)}, u32[]{:S(2)}) collective-permute-start(bf16[8,96,8,256]{3,2,1,0:T(8,128)(2,1)} %select_select_fusion), channel_id=1, source_target_pairs={{0,8},{8,0},{1,9},{9,1},{2,10},{10,2},{3,11},{11,3},{4,12},{12,4},... | collective-permute-start | bytes 9437192 | tf_op jit(solution)/shard_map/ppermute | solution.py:8
  15.9 3.6 %copy-start.10 = (f32[32]{0:T(128)S(1)}, f32[32]{0:T(128)}, u32[]{:S(2)}) copy-start(f32[32]{0:T(128)} %param.15) | copy-start | bytes 388
  23.6 1.4 copy-start.1
  25.0 6.9 %copy-start.8 = (bf16[3,3,96,288]{3,2,1,0:T(8,128)(2,1)S(1)}, bf16[3,3,96,288]{3,2,1,0:T(8,128)(2,1)}, u32[]{:S(2)}) copy-start(bf16[3,3,96,288]{3,2,1,0:T(8,128)(2,1)} %param.16) | copy-start | bytes 1492996
  25.4 30.3 %collective-permute-start.1 = (bf16[4,288,1,256]{3,1,2,0:T(8,128)(2,1)S(1)}, bf16[4,288,1,256]{3,1,2,0:T(8,128)(2,1)S(1)}, u32[]{:S(2)}, u32[]{:S(2)}) collective-permute-start(bf16[4,288,1,256]{3,1,2,0:T(8,128)(2,1)S(1)} %get-tuple-element.17), channel_id=1, source_target_pairs={{0,1},{1,2},{2,3},{3,4},{4,5},{5,6},{6,7},{8,9},{9,10},{10,11},{11... | collective-permute-start | bytes 1769480 | tf_op jit(solution)/shard_map/ppermute | solution.py:19
  30.3 25.5 %collective-permute-start.2 = (bf16[4,288,1,256]{3,1,2,0:T(8,128)(2,1)S(1)}, bf16[4,288,1,256]{3,1,2,0:T(8,128)(2,1)S(1)}, u32[]{:S(2)}, u32[]{:S(2)}) collective-permute-start(bf16[4,288,1,256]{3,1,2,0:T(8,128)(2,1)S(1)} %get-tuple-element.18), channel_id=1, source_target_pairs={{1,0},{2,1},{3,2},{4,3},{5,4},{6,5},{7,6},{9,8},{10,9},{11,10},{12... | collective-permute-start | bytes 1769480 | tf_op jit(solution)/shard_map/ppermute | solution.py:21
  55.7 24.5 %copy-start.5 = (bf16[4,288,1,256]{3,1,2,0:T(8,128)(2,1)}, bf16[4,288,1,256]{3,1,2,0:T(8,128)(2,1)S(1)}, u32[]{:S(2)}) copy-start(bf16[4,288,1,256]{3,1,2,0:T(8,128)(2,1)S(1)} %collective-permute-done.1) | copy-start | bytes 1769476
  83.2 18.6 %copy-start.4 = (bf16[3,3,96,96]{3,2,1,0:T(8,128)(2,1)S(1)}, bf16[3,3,96,96]{3,2,1,0:T(8,128)(2,1)}, u32[]{:S(2)}) copy-start(bf16[3,3,96,96]{3,2,1,0:T(8,128)(2,1)} %param.17) | copy-start | bytes 497668
  94.4 14.7 %copy-start = (bf16[4,96,8,256]{3,1,2,0:T(8,128)(2,1)S(1)}, bf16[4,96,8,256]{3,1,2,0:T(8,128)(2,1)}, u32[]{:S(2)}) copy-start(bf16[4,96,8,256]{3,1,2,0:T(8,128)(2,1)} %get-tuple-element.25) | copy-start | bytes 4718596
  95.6 9.9 %collective-permute-start.3 = (bf16[4,96,1,256]{3,1,2,0:T(8,128)(2,1)S(1)}, bf16[4,96,1,256]{3,1,2,0:T(8,128)(2,1)S(1)}, u32[]{:S(2)}, u32[]{:S(2)}) collective-permute-start(bf16[4,96,1,256]{3,1,2,0:T(8,128)(2,1)S(1)} %get-tuple-element.21), channel_id=1, source_target_pairs={{0,1},{1,2},{2,3},{3,4},{4,5},{5,6},{6,7},{8,9},{9,10},{10,11},{11... | collective-permute-start | bytes 589832 | tf_op jit(solution)/shard_map/ppermute | solution.py:19
  100.0 9.1 %collective-permute-start.4 = (bf16[4,96,1,256]{3,1,2,0:T(8,128)(2,1)S(1)}, bf16[4,96,1,256]{3,1,2,0:T(8,128)(2,1)S(1)}, u32[]{:S(2)}, u32[]{:S(2)}) collective-permute-start(bf16[4,96,1,256]{3,1,2,0:T(8,128)(2,1)S(1)} %get-tuple-element.22), channel_id=1, source_target_pairs={{1,0},{2,1},{3,2},{4,3},{5,4},{6,5},{7,6},{9,8},{10,9},{11,10},{12... | collective-permute-start | bytes 589832 | tf_op jit(solution)/shard_map/ppermute | solution.py:21
  126.9 12.3 %copy-start.2 = (bf16[4,96,8,256]{3,2,1,0:T(8,128)(2,1)S(1)}, bf16[4,96,8,256]{3,2,1,0:T(8,128)(2,1)}, u32[]{:S(2)}) copy-start(bf16[4,96,8,256]{3,2,1,0:T(8,128)(2,1)} %param.11) | copy-start | bytes 4718596
  144.8 11.9 %collective-permute-start.6 = (bf16[4,96,1,256]{3,1,2,0:T(8,128)(2,1)S(1)}, bf16[4,96,1,256]{3,1,2,0:T(8,128)(2,1)S(1)}, u32[]{:S(2)}, u32[]{:S(2)}) collective-permute-start(bf16[4,96,1,256]{3,1,2,0:T(8,128)(2,1)S(1)} %get-tuple-element.19), channel_id=1, source_target_pairs={{1,0},{2,1},{3,2},{4,3},{5,4},{6,5},{7,6},{9,8},{10,9},{11,10},{12... | collective-permute-start | bytes 589832 | tf_op jit(solution)/shard_map/ppermute | solution.py:21
  146.0 12.6 %collective-permute-start.5 = (bf16[4,96,1,256]{3,1,2,0:T(8,128)(2,1)S(1)}, bf16[4,96,1,256]{3,1,2,0:T(8,128)(2,1)S(1)}, u32[]{:S(2)}, u32[]{:S(2)}) collective-permute-start(bf16[4,96,1,256]{3,1,2,0:T(8,128)(2,1)S(1)} %get-tuple-element.20), channel_id=1, source_target_pairs={{0,1},{1,2},{2,3},{3,4},{4,5},{5,6},{6,7},{8,9},{9,10},{10,11},{11... | collective-permute-start | bytes 589832 | tf_op jit(solution)/shard_map/ppermute | solution.py:19
  156.6 6.4 %copy-start.7 = (f32[9,96,96]{2,1,0:T(8,128)}, f32[9,96,96]{2,1,0:T(8,128)S(1)}, u32[]{:S(2)}) copy-start(f32[9,96,96]{2,1,0:T(8,128)S(1)} %fusion.168) | copy-start | bytes 995332
  187.7 1.8 copy-start.6
  205.2 1.1 copy-start.3
Sparse Core Ops, SparseCore 0:
  206.4 98.4 all-reduce.5
where the time goes:
time: 320 us; the launch traced here: 316 us
  waiting for transfers between devices  123 us (38%)
  matrix products  120 us (38%)
  local copies, waits for them, and re-layouts  20.6 us (6%)
  starting transfers between devices  19.8 us (6%)
  other arithmetic  18 us (6%)
  between operations  14.7 us (5%)
    psum x1, waiting for transfers between devices, on_device(): lax.psum((join_part, output_part), ('frame', 'tile'))  95.2 us
    dot_general x18, matrix products, apply_taps(): jnp.einsum('oi,bihw->bohw', kernel[row_tap, col_tap], window, preferred_e...  67.6 us
    dot_general x9, matrix products, transpose_taps(): jnp.einsum('oi,bohw->bihw', kernel[row_tap, col_tap], window, preferred_e...  29.4 us
    dot_general x18, matrix products, tap_grads(): jnp.einsum('bohw,bihw->oi', upstream, window, preferred_element_type=jnp....  23.1 us
    ppermute x3, waiting for transfers between devices, with_halo(): lax.ppermute(tail, axis, [(i, (i + 1) % count) for i in range(ends)])  22.8 us
    ppermute x3, starting transfers between devices, with_halo(): lax.ppermute(tail, axis, [(i, (i + 1) % count) for i in range(ends)])  14.6 us
    unnamed x26, local copies, waits for them, and re-layouts  10.2 us
    concatenate x3, other arithmetic, with_halo(): jnp.concatenate([lax.ppermute(tail, axis, [(i, (i + 1) % count) for i in...  9.9 us
  transfers between devices with their start and end apart: 8, of which 5 were waited for; matrix products, arithmetic and copies ran while one was open for 6% of the time, Pallas kernels for 0%

commit v1 on v0

v1 whole, which is shorter than its diff:
```python
import functools

import jax
import jax.numpy as jnp
from jax import lax
from jax.experimental import pallas as pl
from jax.experimental.pallas import tpu as pltpu
from jax.sharding import PartitionSpec as P

F32 = jnp.float32
BF16 = jnp.bfloat16
LANES = 128


def call(body, name, flops, nbytes, **kw):
    return pl.pallas_call(
        body,
        name=name,
        cost_estimate=pl.CostEstimate(flops=flops, bytes_accessed=nbytes, transcendentals=0),
        compiler_params=pltpu.CompilerParams(vmem_limit_bytes=40 * 1024 * 1024),
        **kw,
    )


def frame_spec(shape):
    return pl.BlockSpec((1,) + shape[1:], lambda b: (b,) + (0,) * (len(shape) - 1))


def whole_spec(shape):
    return pl.BlockSpec(shape, lambda *_: (0,) * len(shape))


def from_left(x):
    lane = lax.broadcasted_iota(jnp.int32, x.shape, 1)
    return jnp.where(lane == 0, jnp.zeros((), x.dtype), pltpu.roll(x, 1, 1))


def from_right(x):
    lane = lax.broadcasted_iota(jnp.int32, x.shape, 1)
    w = x.shape[1]
    return jnp.where(lane == w - 1, jnp.zeros((), x.dtype), pltpu.roll(x, w - 1, 1))


def shift_sum(y):
    c = y.shape[0] // 3
    return y[c : 2 * c] + from_left(y[:c]) + from_right(y[2 * c :])


def conv_rows(weights, rows, width, group=2):
    zero = jnp.zeros_like(rows[0])
    padded = [zero] + rows + [zero]
    sums = []
    for r0 in range(0, len(rows), group):
        columns = [
            jnp.concatenate(padded[r : r + 3], 0) for r in range(r0, min(r0 + group, len(rows)))
        ]
        y = jnp.dot(weights, jnp.concatenate(columns, 1), preferred_element_type=F32)
        for j in range(len(columns)):
            sums.append(shift_sum(y[:, j * width : (j + 1) * width]))
    return sums


def gather_body(pairs, slots, group, refs, out):
    out[...] = refs[...]


def edge_taps_body(xr0, xc0, xr1, xc1, w, up, down):
    frames = up.shape[0]
    for xr, xc, tap, out in ((xr0, xc0, 1, up), (xr1, xc1, 0, down)):
        for b in range(frames):
            x = jnp.concatenate([xr[b, 0], xc[b, 0]], 0)
            y = jnp.dot(w[tap], x, preferred_element_type=F32)
            out[b] = shift_sum(y).astype(BF16)


def silu_and_slope(v):
    s = jax.nn.sigmoid(v)
    return (v * s).astype(BF16), s * (1.0 + v * (1.0 - s))


def join_body(xr, xc, w, hidden, slope, edge):
    rows, width = xr.shape[1], xr.shape[3]
    stacked = [jnp.concatenate([xr[0, r], xc[0, r]], 0) for r in range(rows)]
    sums = conv_rows(w[...], stacked, width)
    edge[0, 0] = sums[0]
    edge[0, 1] = sums[-1]
    for r in range(1, rows - 1):
        hidden[0, r - 1], slope[0, r - 1] = silu_and_slope(sums[r])


def join_edge_body(edge, above, below, hidden, slope):
    for b in range(edge.shape[0]):
        for k, got in enumerate((above, below)):
            hidden[b, k], slope[b, k] = silu_and_slope(edge[b, k] + got[b].astype(F32))


def frame_scale(pairs, cells, b, frames):
    numbers, rates, group = pairs
    return rates[numbers[group[0] * frames + b]] * (2.0 / cells)


def output_body(numbers, rates, group, hm, he, xc, w, recon, residual, edge, *, cells, frames):
    rows, width = hm.shape[1] + 2, hm.shape[3]
    hidden = [he[0, 0]] + [hm[0, r] for r in range(rows - 2)] + [he[0, 1]]
    sums = conv_rows(w[...], hidden, width)
    scale = frame_scale((numbers, rates, group), cells, pl.program_id(0), frames)
    edge[0, 0] = sums[0]
    edge[0, 1] = sums[-1]
    for r in range(1, rows - 1):
        recon[0, r - 1] = sums[r].astype(BF16)
        residual[0, r - 1] = ((sums[r] - xc[0, r].astype(F32)) * scale).astype(BF16)


def output_edge_body(
    numbers, rates, group, edge, above, below, xc0, xc1, w, recon, residual, *, cells, frames
):
    for b in range(edge.shape[0]):
        scale = frame_scale((numbers, rates, group), cells, b, frames)
        for k, (got, xc) in enumerate(((above, xc0), (below, xc1))):
            y = jnp.dot(w[k], got[b], preferred_element_type=F32)
            total = edge[b, k] + shift_sum(y)
            recon[b, k] = total.astype(BF16)
            residual[b, k] = ((total - xc[b, 0].astype(F32)) * scale).astype(BF16)


def slope_body(rm, re, slope, w, grad, edge):
    rows, width = rm.shape[1] + 2, rm.shape[3]
    residual = [re[0, 0]] + [rm[0, r] for r in range(rows - 2)] + [re[0, 1]]
    sums = conv_rows(w[...], residual, width)
    edge[0, 0] = sums[0]
    edge[0, 1] = sums[-1]
    for r in range(1, rows - 1):
        grad[0, r - 1] = (sums[r] * slope[0, r - 1]).astype(BF16)


def slope_edge_body(edge, above, below, slope, w, grad):
    for b in range(edge.shape[0]):
        for k, got in enumerate((above, below)):
            y = jnp.dot(w[k], got[b], preferred_element_type=F32)
            grad[b, k] = ((edge[b, k] + shift_sum(y)) * slope[b, k]).astype(BF16)


def contract(left, right):
    return lax.dot_general(left, right, (((1,), (1,)), ((), ())), preferred_element_type=F32)


def lane_blocks(x):
    return [x[:, k : k + LANES] for k in range(0, x.shape[1], LANES)]


def grads_body(gm, ge, xr, xc, hm, he, rm, re, above, below, packed):
    rows, width = gm.shape[1] + 2, gm.shape[3]
    channels = gm.shape[2]
    joined = xr.shape[2] + xc.shape[2]
    rest = joined % 256
    head = joined - rest
    zero = jnp.zeros((channels, width), BF16)
    grad = [ge[0, 0]] + [gm[0, r] for r in range(rows - 2)] + [ge[0, 1]]
    turned = [[from_right(g) for g in grad], grad, [from_left(g) for g in grad]]
    stacked = [jnp.concatenate([xr[0, r], xc[0, r]], 0) for r in range(rows)]
    taps = []
    for p in range(3):
        for q in range(3):
            taps.append(
                jnp.concatenate(
                    [turned[q][r - p + 1] if 0 <= r - p + 1 < rows else zero for r in range(rows)],
                    1,
                )
            )
    main = contract(
        jnp.concatenate(taps, 0), jnp.concatenate([s[:head] for s in stacked], 1)
    )
    tails = [s[head:] for s in stacked]
    tail_zero = jnp.zeros_like(tails[0])
    tail = contract(
        jnp.concatenate([jnp.concatenate(turned[q], 1) for q in range(3)], 0),
        jnp.concatenate(
            [
                jnp.concatenate(
                    [tails[r + p - 1] if 0 <= r + p - 1 < rows else tail_zero for r in range(rows)],
                    1,
                )
                for p in range(3)
            ],
            0,
        ),
    )
    hidden = [he[0, 0]] + [hm[0, r] for r in range(rows - 2)] + [he[0, 1]]
    shifted = [[from_left(h) for h in hidden], hidden, [from_right(h) for h in hidden]]
    residual = (
        [above[0], re[0, 0]] + [rm[0, r] for r in range(rows - 2)] + [re[0, 1], below[0]]
    )
    out = contract(
        jnp.concatenate(
            [jnp.concatenate([residual[r - p + 2] for r in range(rows)], 1) for p in range(3)], 0
        ),
        jnp.concatenate([jnp.concatenate(shifted[q], 1) for q in range(3)], 0),
    )
    blocks = lane_blocks(main) + lane_blocks(jnp.concatenate([out, tail], 1))
    first = pl.program_id(0) == 0

    @pl.when(first)
    def _():
        at = 0
        for block in blocks:
            packed[at : at + block.shape[0], :] = block
            at += block.shape[0]
        if at < packed.shape[0]:
            packed[at:, :] = jnp.zeros((packed.shape[0] - at, LANES), F32)

    @pl.when(jnp.logical_not(first))
    def _():
        at = 0
        for block in blocks:
            packed[at : at + block.shape[0], :] += block
            at += block.shape[0]


def grads_edge_body(packed_in, above, below, xr0, xc0, xr1, xc1, packed):
    frames, channels, _ = above.shape
    joined = xr0.shape[2] + xc0.shape[2]
    rest = joined % 256
    head = joined - rest
    taps = 3 * channels
    packed[...] = packed_in[...]
    tail_at = 3 * taps * (head // LANES)
    tail_lane = taps
    for p, got, xr, xc in ((2, above, xr0, xc0), (0, below, xr1, xc1)):
        rows = [got[b] for b in range(frames)]
        left = jnp.concatenate(
            [
                jnp.concatenate([move(g) for g in rows], 1)
                for move in (from_right, lambda g: g, from_left)
            ],
            0,
        )
        right = jnp.concatenate(
            [jnp.concatenate([xr[b, 0], xc[b, 0]], 0) for b in range(frames)], 1
        )
        extra = contract(left, right)
        for k, block in enumerate(lane_blocks(extra[:, :head])):
            at = 3 * taps * k + taps * p
            packed[at : at + taps, :] += block
        lane = tail_lane + rest * p
        at = tail_at + taps * (lane // LANES)
        lane = lane % LANES
        packed[at : at + taps, lane : lane + rest] += extra[:, head:]


def unpack_body(packed, join, out):
    channels = out.shape[2]
    joined = join.shape[3]
    rest = joined % 256
    head = joined - rest
    taps = 3 * channels
    tail_at = 3 * taps * (head // LANES)
    tail = jnp.concatenate(
        [
            packed[tail_at + taps * k : tail_at + taps * (k + 1), :]
            for k in range((taps + 3 * rest) // LANES)
        ],
        1,
    )
    for p in range(3):
        for q in range(3):
            rows = slice(q * channels, (q + 1) * channels)
            pieces = [
                packed[
                    3 * taps * k + taps * p + q * channels : 3 * taps * k
                    + taps * p
                    + (q + 1) * channels,
                    :,
                ]
                for k in range(head // LANES)
            ]
            pieces.append(tail[rows, taps + rest * p : taps + rest * (p + 1)])
            join[p, q] = jnp.concatenate(pieces, 1)
            out[p, q] = tail[p * channels : (p + 1) * channels, q * channels : (q + 1) * channels]


def swap_edges(up, down, axis):
    count = lax.axis_size(axis)
    ends = count - 1
    below = lax.ppermute(up, axis, [(i + 1, i) for i in range(ends)])
    above = lax.ppermute(down, axis, [(i, i + 1) for i in range(ends)])
    return above, below


def reduce_all(packed, steps):
    part = packed
    for axis, stride in steps:
        count = lax.axis_size(axis)
        bit = (lax.axis_index(axis) // stride) % 2
        half = part.shape[0] // 2
        send = lax.dynamic_slice_in_dim(part, (1 - bit) * half, half, 0)
        keep = lax.dynamic_slice_in_dim(part, bit * half, half, 0)
        part = keep + lax.ppermute(send, axis, [(i, i ^ stride) for i in range(count)])
    for axis, stride in reversed(steps):
        count = lax.axis_size(axis)
        bit = (lax.axis_index(axis) // stride) % 2
        got = lax.ppermute(part, axis, [(i, i ^ stride) for i in range(count)])
        part = jnp.concatenate(
            [jnp.where(bit == 0, part, got), jnp.where(bit == 0, got, part)], 0
        )
    return part


def on_device(
    decoded_refs,
    current_frames,
    ref_pairs,
    ref_slots,
    frame_numbers,
    rate_weights,
    join_kernel,
    out_kernel,
):
    local_refs = decoded_refs.shape[0]
    frames, channels, rows, width = current_frames.shape
    joined = join_kernel.shape[3]
    cells = rows * lax.axis_size("tile") * width
    group = lax.axis_index("frame")
    group_id = group.reshape(1).astype(jnp.int32)
    picks = 2 * frames
    taps = 3 * channels
    conv_flops = 2 * frames * rows * width * 3 * taps

    def gathered(owner, name):
        tile = decoded_refs.shape[1:]

        def tile_at(i, pairs, slots, ids):
            wanted = (ids[0] if owner == 0 else 1 - ids[0]) * frames + i // 2
            slot = slots[pairs[wanted * 2 + i % 2]] - ids[0] * local_refs
            return (jnp.clip(slot, 0, local_refs - 1), 0, 0, 0)

        return call(
            gather_body,
            name,
            0,
            4 * picks * channels * rows * width,
            grid_spec=pltpu.PrefetchScalarGridSpec(
                num_scalar_prefetch=3,
                grid=(picks,),
                in_specs=[pl.BlockSpec((1,) + tile, tile_at)],
                out_specs=pl.BlockSpec((1,) + tile, lambda i, *_: (i, 0, 0, 0)),
            ),
            out_shape=jax.ShapeDtypeStruct((picks,) + tile, BF16),
        )(ref_pairs.reshape(-1), ref_slots, group_id, decoded_refs)

    outgoing = gathered(1, "gather_out")
    incoming = lax.ppermute(outgoing, "frame", [(0, 1), (1, 0)])
    own = gathered(0, "gather_own")
    pairs = lax.dynamic_slice_in_dim(ref_pairs, group * frames, frames, 0)
    slot_range = jnp.arange(ref_slots.shape[0], dtype=jnp.int32)
    slots = jnp.sum(jnp.where(pairs[:, :, None] == slot_range, ref_slots, 0), axis=-1)
    held = slots // local_refs == group
    picked = jnp.where(
        held[:, :, None, None, None],
        own.reshape(frames, 2, channels, rows, width),
        incoming.reshape(frames, 2, channels, rows, width),
    )
    xr = picked.transpose(0, 3, 1, 2, 4).reshape(frames, rows, 2 * channels, width)
    xc = current_frames.transpose(0, 2, 1, 3)

    join_w = join_kernel.transpose(1, 2, 0, 3).reshape(taps, 3 * joined)
    join_edge_w = join_kernel[0::2].reshape(2, taps, joined)
    out_w = out_kernel.transpose(1, 2, 0, 3).reshape(taps, taps)
    out_edge_w = out_kernel[0::2].reshape(2, taps, channels)
    back = out_kernel[::-1, ::-1].transpose(0, 1, 3, 2)
    back_w = back.transpose(1, 2, 0, 3).reshape(taps, taps)
    back_edge_w = back[0::2].reshape(2, taps, channels)

    mid = (frames, rows - 2, channels, width)
    ends = (frames, 2, channels, width)
    line = (frames, channels, width)

    def struct(shape, dtype):
        return jax.ShapeDtypeStruct(shape, dtype)

    def row_spec(x, r):
        shape = (frames, 1) + x.shape[2:]
        return pl.BlockSpec(shape, lambda *_: (0, r, 0, 0))

    up, down = call(
        edge_taps_body,
        "edge_taps",
        conv_flops * joined // (3 * rows) * 2,
        8 * frames * joined * width,
        grid=(1,),
        in_specs=[
            row_spec(xr, 0),
            row_spec(xc, 0),
            row_spec(xr, rows - 1),
            row_spec(xc, rows - 1),
            whole_spec(join_edge_w.shape),
        ],
        out_specs=[whole_spec(line)] * 2,
        out_shape=[struct(line, BF16)] * 2,
    )(xr, xc, xr, xc, join_edge_w)
    above, below = swap_edges(up, down, "tile")

    hm, sm, pe = call(
        join_body,
        "join_conv",
        conv_flops * joined,
        frames * rows * width * (2 * joined + 6 * channels),
        grid=(frames,),
        in_specs=[frame_spec(xr.shape), frame_spec(xc.shape), whole_spec(join_w.shape)],
        out_specs=[frame_spec(mid), frame_spec(mid), frame_spec(ends)],
        out_shape=[struct(mid, BF16), struct(mid, F32), struct(ends, F32)],
    )(xr, xc, join_w)

    he, se = call(
        join_edge_body,
        "join_edge",
        10 * frames * 2 * channels * width,
        14 * frames * 2 * channels * width,
        grid=(1,),
        in_specs=[whole_spec(ends), whole_spec(line), whole_spec(line)],
        out_specs=[whole_spec(ends)] * 2,
        out_shape=[struct(ends, BF16), struct(ends, F32)],
    )(pe, above, below)
    h_above, h_below = swap_edges(he[:, 0], he[:, 1], "tile")

    rated = (frame_numbers, rate_weights, group_id)
    cm, rm, ce = call(
        functools.partial(output_body, cells=cells, frames=frames),
        "out_conv",
        conv_flops * channels,
        frames * rows * width * 8 * channels,
        grid_spec=pltpu.PrefetchScalarGridSpec(
            num_scalar_prefetch=3,
            grid=(frames,),
            in_specs=[
                pl.BlockSpec((1,) + s[1:], lambda b, *_: (b, 0, 0, 0))
                for s in (mid, ends, xc.shape)
            ]
            + [whole_spec(out_w.shape)],
            out_specs=[
                pl.BlockSpec((1,) + s[1:], lambda b, *_: (b, 0, 0, 0)) for s in (mid, mid, ends)
            ],
        ),
        out_shape=[struct(mid, BF16), struct(mid, BF16), struct(ends, F32)],
    )(*rated, hm, he, xc, out_w)

    ce, re = call(
        functools.partial(output_edge_body, cells=cells, frames=frames),
        "out_edge",
        conv_flops * channels // (3 * rows) * 2,
        14 * frames * 2 * channels * width,
        grid_spec=pltpu.PrefetchScalarGridSpec(
            num_scalar_prefetch=3,
            grid=(1,),
            in_specs=[
                whole_spec(ends),
                whole_spec(line),
                whole_spec(line),
                row_spec(xc, 0),
                row_spec(xc, rows - 1),
                whole_spec(out_edge_w.shape),
            ],
            out_specs=[whole_spec(ends)] * 2,
        ),
        out_shape=[struct(ends, BF16)] * 2,
    )(*rated, ce, h_above, h_below, xc, xc, out_edge_w)
    r_above, r_below = swap_edges(re[:, 0], re[:, 1], "tile")

    gm, de = call(
        slope_body,
        "back_conv",
        conv_flops * channels,
        frames * rows * width * 8 * channels,
        grid=(frames,),
        in_specs=[frame_spec(mid), frame_spec(ends), frame_spec(mid), whole_spec(back_w.shape)],
        out_specs=[frame_spec(mid), frame_spec(ends)],
        out_shape=[struct(mid, BF16), struct(ends, F32)],
    )(rm, re, sm, back_w)

    ge = call(
        slope_edge_body,
        "back_edge",
        conv_flops * channels // (3 * rows) * 2,
        14 * frames * 2 * channels * width,
        grid=(1,),
        in_specs=[
            whole_spec(ends),
            whole_spec(line),
            whole_spec(line),
            whole_spec(ends),
            whole_spec(back_edge_w.shape),
        ],
        out_specs=whole_spec(ends),
        out_shape=struct(ends, BF16),
    )(de, r_above, r_below, se, back_edge_w)
    g_above, g_below = swap_edges(ge[:, 0], ge[:, 1], "tile")

    steps = [("frame", 1)]
    stride = 1
    while stride < lax.axis_size("tile"):
        steps.append(("tile", stride))
        stride *= 2
    unit = 8 << len(steps)
    packed_rows = 3 * taps * (joined + channels) // LANES
    packed_shape = (pl.cdiv(packed_rows, unit) * unit, LANES)
    packed = call(
        grads_body,
        "grads",
        conv_flops * (joined + channels),
        frames * rows * width * (2 * joined + 6 * channels),
        grid=(frames,),
        in_specs=[
            frame_spec(x.shape) for x in (gm, ge, xr, xc, hm, he, rm, re, r_above, r_below)
        ],
        out_specs=whole_spec(packed_shape),
        out_shape=struct(packed_shape, F32),
    )(gm, ge, xr, xc, hm, he, rm, re, r_above, r_below)
    packed = call(
        grads_edge_body,
        "grads_edge",
        conv_flops * joined // (3 * rows) * 2,
        8 * packed_shape[0] * LANES,
        grid=(1,),
        in_specs=[
            whole_spec(packed_shape),
            whole_spec(line),
            whole_spec(line),
            row_spec(xr, 0),
            row_spec(xc, 0),
            row_spec(xr, rows - 1),
            row_spec(xc, rows - 1),
        ],
        out_specs=whole_spec(packed_shape),
        out_shape=struct(packed_shape, F32),
        input_output_aliases={0: 0},
    )(packed, g_above, g_below, xr, xc, xr, xc)
    total = reduce_all(packed, steps)
    join_total, out_total = call(
        unpack_body,
        "unpack",
        0,
        8 * packed_shape[0] * LANES,
        grid=(1,),
        in_specs=[whole_spec(packed_shape)],
        out_specs=[whole_spec(join_kernel.shape), whole_spec(out_kernel.shape)],
        out_shape=[struct(join_kernel.shape, F32), struct(out_kernel.shape, F32)],
    )(total)
    recon = jnp.concatenate([ce[:, :1], cm, ce[:, 1:]], 1).transpose(0, 2, 1, 3)
    return recon, join_total, out_total


def solution(mesh):
    placed = (
        P(("parts", "frame"), None, "tile", None),
        P(("parts", "frame"), None, "tile", None),
        P("parts", None),
        P("parts"),
        P("parts"),
        P("parts"),
        P(),
        P(),
    )
    return jax.shard_map(
        on_device,
        mesh=mesh,
        in_specs=placed,
        out_specs=(
            P(("parts", "frame"), None, "tile", None),
            P("parts", None, None, None),
            P("parts", None, None, None),
        ),
        check_vma=False,
    )
```

time: 320 us -> 149 us (0.47)
  matrix products: 120 us -> 0 us
  waiting for transfers between devices: 123 us -> 30.1 us
  Pallas kernels: 0 us -> 32.3 us
  starting transfers between devices: 19.8 us -> 39.9 us
  local copies, waits for them, and re-layouts: 20.6 us -> 38.2 us
  between operations: 14.7 us -> 1.28 us
  other arithmetic: 18 us -> 6.08 us
    dot_general x45 -> x0, matrix products: 120 us -> none  [the longest x18 67.6 us: apply_taps(): jnp.einsum('oi,bihw->bohw', kernel[row_tap, col_tap], window, preferred_e...]
    psum x1 -> x0, waiting for transfers between devices: 95.2 us -> none  [on_device(): lax.psum((join_part, output_part), ('frame', 'tile'))]
    pallas_call x0 -> x12, Pallas kernels: none -> 32.3 us  [the longest x1 9.51 us: on_device(): call(grads_body, 'grads', conv_flops * (joined + channels), frames * rows...]
    ppermute x7 -> x17, starting transfers between devices: 19.8 us -> 39.9 us  [the longest x4 20.7 us: swap_edges(): above = lax.ppermute(down, axis, [(i, i + 1) for i in range(ends)])]
    unnamed x26 -> x75, local copies, waits for them, and re-layouts: 10.2 us -> 23.1 us
    concatenate x3 -> x4, other arithmetic: 9.9 us -> 1.02 us  [reduce_all(): jnp.concatenate([jnp.where(bit == 0, part, got), jnp.where(bit == 0, got,...]
    gather x2 -> x0, local copies, waits for them, and re-layouts: 7.07 us -> none  [the longest x1 3.54 us: on_device(): jnp.take(decoded_refs, jnp.clip(mine_local, 0, local_refs - 1), axis=0)]
    reshape x0 -> x4, local copies, waits for them, and re-layouts: none -> 5.29 us  [the longest x1 2.88 us: on_device(): join_w = join_kernel.transpose(1, 2, 0, 3).reshape(taps, 3 * joined)]
  transfers between devices with their start and end apart: 8 -> 17, of which waited for: 5 -> 9; matrix products, arithmetic and copies ran while one was open for 6% -> 12% of each run, Pallas kernels for 0% -> 16%
where the time goes in v1:
time: 149 us; the launch traced here: 148 us
  starting transfers between devices  39.9 us (27%)
  local copies, waits for them, and re-layouts  38.2 us (26%)
  Pallas kernels  32.3 us (22%)
  waiting for transfers between devices  30.1 us (20%)
  other arithmetic  6.08 us (4%)
    unnamed x75, local copies, waits for them, and re-layouts  23.1 us
    ppermute x4, starting transfers between devices, swap_edges(): above = lax.ppermute(down, axis, [(i, i + 1) for i in range(ends)])  20.7 us
    ppermute x4, waiting for transfers between devices, reduce_all(): lax.ppermute(send, axis, [(i, i ^ stride) for i in range(count)])  17.5 us
    ppermute x4, waiting for transfers between devices, reduce_all(): got = lax.ppermute(part, axis, [(i, i ^ stride) for i in range(count)])  12.2 us
    pallas_call x1, Pallas kernels, on_device(): call(grads_body, 'grads', conv_flops * (joined + channels), frames * rows...  9.51 us
    ppermute x4, starting transfers between devices, reduce_all(): lax.ppermute(send, axis, [(i, i ^ stride) for i in range(count)])  7.34 us
    ppermute x4, starting transfers between devices, reduce_all(): got = lax.ppermute(part, axis, [(i, i ^ stride) for i in range(count)])  6.17 us
    pallas_call x1, Pallas kernels, on_device(): call(join_body, 'join_conv', conv_flops * joined, frames * rows * width *...  5.83 us
  transfers between devices with their start and end apart: 17, of which 9 were waited for; matrix products, arithmetic and copies ran while one was open for 12% of the time, Pallas kernels for 16%

profile of v1, /device:TPU:0, one launch (start us, length us, event | category | flops | bytes accessed | tf_op | source)
XLA Modules:
  0.0 147.9 jit_solution(6120911353986035635)
XLA Ops:
  1.5 2.8 %copy-done.3 = bf16[16,96,8,256]{3,2,1,0:T(8,128)(2,1)S(1)} copy-done((bf16[16,96,8,256]{3,2,1,0:T(8,128)(2,1)S(1)}, bf16[16,96,8,256]{3,2,1,0:T(8,128)(2,1)}, u32[]{:S(2)}) %copy-start.3) | copy-done | bytes 6291480
  11.4 2.5 %copy.49 = bf16[3,96,3,288]{3,2,1,0:T(4,128)(2,1)} copy(bf16[3,96,3,288]{3,1,0,2:T(8,128)(2,1)} %bitcast.55) | data formatting | bytes 995328 | tf_op jit(solution)/shard_map/transpose | solution.py:365
  13.9 2.9 %reshape.64.w = bf16[288,864]{1,0:T(8,128)(2,1)} reshape(bf16[3,96,3,288]{3,2,1,0:T(4,128)(2,1)} %copy.49) | data formatting | bytes 995328 | tf_op jit(solution)/shard_map/reshape | solution.py:365
  19.1 3.2 %copy_select_fusion = bf16[4,2,96,8,256]{4,2,1,3,0:T(8,128)(2,1)S(1)} fusion(bf16[4,2,96,8,256]{4,3,2,1,0:T(8,128)(2,1)} %bitcast.2, bf16[4,2,96,8,256]{4,3,2,1,0:T(8,128)(2,1)S(1)} %bitcast.51, pred[4,2]{1,0:T(4,128)(4,1)S(1)} %copy.44), kind=kLoop, calls=%fused_computation | loop fusion | flops 1572864 | bytes 9437192 | tf_op jit(solution)/shard_map/jit(_where)/select_n | solution.py:357
  23.2 4.4 %collective-permute-start.1 = (bf16[4,96,256]{2,1,0:T(8,128)(2,1)S(1)}, bf16[4,96,256]{2,1,0:T(8,128)(2,1)S(1)}, u32[]{:S(2)}, u32[]{:S(2)}) collective-permute-start(bf16[4,96,256]{2,1,0:T(8,128)(2,1)S(1)} %get-tuple-element.21), channel_id=1, source_target_pairs={{0,1},{1,2},{2,3},{3,4},{4,5},{5,6},{6,7},{8,9},{9,10},{10,11},{11... | collective-permute-start | bytes 589832 | tf_op jit(solution)/shard_map/ppermute | solution.py:285
  29.0 5.8 %join_conv.1 = (bf16[4,6,96,256]{3,2,1,0:T(8,128)(2,1)S(1)}, f32[4,6,96,256]{3,2,1,0:T(8,128)S(1)}, f32[4,2,96,256]{3,2,1,0:T(8,128)S(1)}) custom-call(bf16[4,8,192,256]{3,2,1,0:T(8,128)(2,1)S(1)} %bitcast.38, bf16[4,8,96,256]{3,2,1,0:T(8,128)(2,1)S(1)} %bitcast.44, bf16[288,864]{1,0:T(8,128)(2,1)S(1)} %copy-done.12), custom_call_target="tpu_custom_call" | custom-call | flops 4076863488 | bytes 9437184 | tf_op jit(solution)/shard_map/join_conv/pallas_call | solution.py:402
  40.6 5.8 %collective-permute-start.3 = (bf16[4,96,256]{2,1,0:T(8,128)(2,1)}, bf16[4,96,256]{2,1,0:T(8,128)(2,1)}, u32[]{:S(2)}, u32[]{:S(2)}) collective-permute-start(bf16[4,96,256]{2,1,0:T(8,128)(2,1)} %get-tuple-element.55), channel_id=1, source_target_pairs={{0,1},{1,2},{2,3},{3,4},{4,5},{5,6},{6,7},{8,9},{9,10},{10,11},{11... | collective-permute-start | bytes 589832 | tf_op jit(solution)/shard_map/ppermute | solution.py:285
  52.2 3.9 %out_conv.1 = (bf16[4,6,96,256]{3,2,1,0:T(8,128)(2,1)S(1)}, bf16[4,6,96,256]{3,2,1,0:T(8,128)(2,1)S(1)}, f32[4,2,96,256]{3,2,1,0:T(8,128)S(1)}) custom-call(s32[8]{0:T(128)S(1)} %copy-done.23, f32[32]{0:T(128)S(1)} %copy-done.24, s32[1]{0:T(128)} %bitcast.group, bf16[4,6,96,256]{3,2,1,0:T(8,128)(2,1)S(1)} %copy-done.31, ...), custom_call_target="tpu_custom_call" | custom-call | flops 1358954496 | bytes 6291456 | tf_op jit(solution)/shard_map/out_conv/pallas_call | solution.py:426
  57.1 2.2 %out_edge.1 = (bf16[4,2,96,256]{3,2,1,0:T(8,128)(2,1)S(1)}, bf16[4,2,96,256]{3,2,1,0:T(8,128)(2,1)S(1)}) custom-call(s32[8]{0:T(128)S(1)} %copy-done.23, f32[32]{0:T(128)S(1)} %copy-done.24, s32[1]{0:T(128)} %bitcast.group, f32[4,2,96,256]{3,2,1,0:T(8,128)S(1)} %get-tuple-element.24.edge, bf16[4,96,256]{2,1,0:T(8,128)(2,1)} %collective-permute-done.3.above, ...), custom_call_target="tpu_custom_call" | custom-call | flops 113246208 | bytes 2752512 | tf_op jit(solution)/shard_map/out_edge/pallas_call | solution.py:446
  61.5 5.5 %collective-permute-start.5 = (bf16[4,96,256]{2,1,0:T(8,128)(2,1)}, bf16[4,96,256]{2,1,0:T(8,128)(2,1)}, u32[]{:S(2)}, u32[]{:S(2)}) collective-permute-start(bf16[4,96,256]{2,1,0:T(8,128)(2,1)} %get-tuple-element.51), channel_id=1, source_target_pairs={{0,1},{1,2},{2,3},{3,4},{4,5},{5,6},{6,7},{8,9},{9,10},{10,11},{11... | collective-permute-start | bytes 589832 | tf_op jit(solution)/shard_map/ppermute | solution.py:285
  74.9 3.3 %back_conv.1 = (bf16[4,6,96,256]{3,2,1,0:T(8,128)(2,1)S(1)}, f32[4,2,96,256]{3,2,1,0:T(8,128)S(1)}) custom-call(bf16[4,6,96,256]{3,2,1,0:T(8,128)(2,1)S(1)} %copy-done.28, bf16[4,2,96,256]{3,2,1,0:T(8,128)(2,1)S(1)} %copy-done.19, f32[4,6,96,256]{3,2,1,0:T(8,128)S(1)} %copy-done.26, bf16[288,288]{1,0:T(8,128)(2,1)S(1)} %reshape.68.w), custom_call_target="tpu_custom_call" | custom-call | flops 1358954496 | bytes 6291456 | tf_op jit(solution)/shard_map/back_conv/pallas_call | solution.py:468
  81.4 5.0 %collective-permute-start.7 = (bf16[4,96,256]{2,1,0:T(8,128)(2,1)S(1)}, bf16[4,96,256]{2,1,0:T(8,128)(2,1)S(1)}, u32[]{:S(2)}, u32[]{:S(2)}) collective-permute-start(bf16[4,96,256]{2,1,0:T(8,128)(2,1)S(1)} %get-tuple-element.49), channel_id=1, source_target_pairs={{0,1},{1,2},{2,3},{3,4},{4,5},{5,6},{6,7},{8,9},{9,10},{10,11},{11... | collective-permute-start | bytes 589832 | tf_op jit(solution)/shard_map/ppermute | solution.py:285
  86.5 9.5 %grads.1.packed_in = f32[2688,128]{1,0:T(8,128)S(1)} custom-call(bf16[4,6,96,256]{3,2,1,0:T(8,128)(2,1)S(1)} %get-tuple-element.30.gm, bf16[4,2,96,256]{3,2,1,0:T(8,128)(2,1)S(1)} %back_edge.1.ge, bf16[4,8,192,256]{3,2,1,0:T(8,128)(2,1)S(1)} %bitcast.39, bf16[4,8,96,256]{3,2,1,0:T(8,128)(2,1)S(1)} %bitcast.48, bf16[4,6,96,256]{3,2,1,0:T(8,128)(2,1)S(1)} %copy-done.32, ...), custom_call_target="tpu_custom_call" | custom-call | flops 5435817984 | bytes 9437184 | tf_op jit(solution)/shard_map/grads/pallas_call | solution.py:505
  98.3 2.1 %collective-permute-done.9 = f32[1344,128]{1,0:T(8,128)S(1)} collective-permute-done((f32[1344,128]{1,0:T(8,128)S(1)}, f32[1344,128]{1,0:T(8,128)S(1)}, u32[]{:S(2)}, u32[]{:S(2)}) %collective-permute-start.9) | collective-permute-done | bytes 688160 | tf_op jit(solution)/shard_map/ppermute | solution.py:297
  101.7 3.0 %collective-permute-start.10 = (f32[672,128]{1,0:T(8,128)S(1)}, f32[672,128]{1,0:T(8,128)S(1)}, u32[]{:S(2)}, u32[]{:S(2)}) collective-permute-start(f32[672,128]{1,0:T(8,128)S(1)} %constant_dynamic-slice_fusion.2), channel_id=1, source_target_pairs={{0,1},{1,0},{2,3},{3,2},{4,5},{5,4},{6,7},{7,6},{8,9},{9,8},{10,11... | collective-permute-start | bytes 1032200 | tf_op jit(solution)/shard_map/ppermute | solution.py:297
  104.6 8.4 %collective-permute-done.10 = f32[672,128]{1,0:T(8,128)S(1)} collective-permute-done((f32[672,128]{1,0:T(8,128)S(1)}, f32[672,128]{1,0:T(8,128)S(1)}, u32[]{:S(2)}, u32[]{:S(2)}) %collective-permute-start.10) | collective-permute-done | bytes 344096 | tf_op jit(solution)/shard_map/ppermute | solution.py:297
  114.7 4.3 %collective-permute-done.11 = f32[336,128]{1,0:T(8,128)S(1)} collective-permute-done((f32[336,128]{1,0:T(8,128)S(1)}, f32[336,128]{1,0:T(8,128)S(1)}, u32[]{:S(2)}, u32[]{:S(2)}) %collective-permute-start.11) | collective-permute-done | bytes 172064 | tf_op jit(solution)/shard_map/ppermute | solution.py:297
  119.0 2.7 %collective-permute-start.12 = (f32[168,128]{1,0:T(8,128)S(1)}, f32[168,128]{1,0:T(8,128)S(1)}, u32[]{:S(2)}, u32[]{:S(2)}) collective-permute-start(f32[168,128]{1,0:T(8,128)S(1)} %constant_dynamic-slice_fusion), channel_id=1, source_target_pairs={{0,4},{1,5},{2,6},{3,7},{4,0},{5,1},{6,2},{7,3},{8,12},{9,13},{10,... | collective-permute-start | bytes 258056 | tf_op jit(solution)/shard_map/ppermute | solution.py:297
  121.7 2.8 %collective-permute-done.12 = f32[168,128]{1,0:T(8,128)S(1)} collective-permute-done((f32[168,128]{1,0:T(8,128)S(1)}, f32[168,128]{1,0:T(8,128)S(1)}, u32[]{:S(2)}, u32[]{:S(2)}) %collective-permute-start.12) | collective-permute-done | bytes 86048 | tf_op jit(solution)/shard_map/ppermute | solution.py:297
  124.5 2.8 %collective-permute-start.13 = (f32[168,128]{1,0:T(8,128)S(1)}, f32[168,128]{1,0:T(8,128)S(1)}, u32[]{:S(2)}, u32[]{:S(2)}) collective-permute-start(f32[168,128]{1,0:T(8,128)S(1)} %dynamic-slice_add_fusion.3), channel_id=1, source_target_pairs={{0,4},{1,5},{2,6},{3,7},{4,0},{5,1},{6,2},{7,3},{8,12},{9,13},{10,... | collective-permute-start | bytes 258056 | tf_op jit(solution)/shard_map/ppermute | solution.py:301
  127.2 2.8 %collective-permute-done.13 = f32[168,128]{1,0:T(8,128)S(1)} collective-permute-done((f32[168,128]{1,0:T(8,128)S(1)}, f32[168,128]{1,0:T(8,128)S(1)}, u32[]{:S(2)}, u32[]{:S(2)}) %collective-permute-start.13) | collective-permute-done | bytes 86048 | tf_op jit(solution)/shard_map/ppermute | solution.py:301
  131.9 3.6 %collective-permute-done.14 = f32[336,128]{1,0:T(8,128)S(1)} collective-permute-done((f32[336,128]{1,0:T(8,128)S(1)}, f32[336,128]{1,0:T(8,128)S(1)}, u32[]{:S(2)}, u32[]{:S(2)}) %collective-permute-start.14) | collective-permute-done | bytes 172064 | tf_op jit(solution)/shard_map/ppermute | solution.py:301
  137.2 5.7 %collective-permute-done.15 = f32[672,128]{1,0:T(8,128)S(1)} collective-permute-done((f32[672,128]{1,0:T(8,128)S(1)}, f32[672,128]{1,0:T(8,128)S(1)}, u32[]{:S(2)}, u32[]{:S(2)}) %collective-permute-start.15) | collective-permute-done | bytes 344096 | tf_op jit(solution)/shard_map/ppermute | solution.py:301
  144.1 2.0 %copy.59 = bf16[4,96,8,256]{3,2,1,0:T(8,128)(2,1)} copy(bf16[4,96,8,256]{3,1,2,0:T(8,128)(2,1)S(1)} %maximum_bitcast_fusion) | data formatting | bytes 3145728
  (135 shorter events, 49.7 us)
Async XLA Ops:
  5.9 12.8 %collective-permute-start = (bf16[8,96,8,256]{3,2,1,0:T(8,128)(2,1)S(1)}, bf16[8,96,8,256]{3,2,1,0:T(8,128)(2,1)}, u32[]{:S(2)}, u32[]{:S(2)}) collective-permute-start(bf16[8,96,8,256]{3,2,1,0:T(8,128)(2,1)S(1)} %gather_out.1), channel_id=1, source_target_pairs={{0,8},{8,0},{1,9},{9,1},{2,10},{10,2},{3,11},{11,3},{4,12},{12,4},... | collective-permute-start | bytes 9437192 | tf_op jit(solution)/shard_map/ppermute | solution.py:351
  18.7 10.3 %copy-start = (bf16[4,96,8,256]{3,1,2,0:T(8,128)(2,1)}, bf16[4,96,8,256]{3,1,2,0:T(8,128)(2,1)S(1)}, u32[]{:S(2)}) copy-start(bf16[4,96,8,256]{3,1,2,0:T(8,128)(2,1)S(1)} %copy.69) | copy-start | bytes 4718596
  23.2 13.0 %collective-permute-start.1 = (bf16[4,96,256]{2,1,0:T(8,128)(2,1)S(1)}, bf16[4,96,256]{2,1,0:T(8,128)(2,1)S(1)}, u32[]{:S(2)}, u32[]{:S(2)}) collective-permute-start(bf16[4,96,256]{2,1,0:T(8,128)(2,1)S(1)} %get-tuple-element.21), channel_id=1, source_target_pairs={{0,1},{1,2},{2,3},{3,4},{4,5},{5,6},{6,7},{8,9},{9,10},{10,11},{11... | collective-permute-start | bytes 589832 | tf_op jit(solution)/shard_map/ppermute | solution.py:285
  27.7 8.9 %collective-permute-start.2 = (bf16[4,96,256]{2,1,0:T(8,128)(2,1)S(1)}, bf16[4,96,256]{2,1,0:T(8,128)(2,1)S(1)}, u32[]{:S(2)}, u32[]{:S(2)}) collective-permute-start(bf16[4,96,256]{2,1,0:T(8,128)(2,1)S(1)} %get-tuple-element.22), channel_id=1, source_target_pairs={{1,0},{2,1},{3,2},{4,3},{5,4},{6,5},{7,6},{9,8},{10,9},{11,10},{12... | collective-permute-start | bytes 589832 | tf_op jit(solution)/shard_map/ppermute | solution.py:284
  36.3 10.1 %copy-start.33 = (bf16[3,3,96,96]{3,2,1,0:T(8,128)(2,1)S(1)}, bf16[3,3,96,96]{3,2,1,0:T(8,128)(2,1)}, u32[]{:S(2)}) copy-start(bf16[3,3,96,96]{3,2,1,0:T(8,128)(2,1)} %param.15) | copy-start | bytes 497668
  36.6 11.9 %copy-start.23 = (s32[8]{0:T(128)S(1)}, s32[8]{0:T(128)}, u32[]{:S(2)}) copy-start(s32[8]{0:T(128)} %numbers.3) | copy-start | bytes 100
  36.6 11.9 %copy-start.24 = (f32[32]{0:T(128)S(1)}, f32[32]{0:T(128)}, u32[]{:S(2)}) copy-start(f32[32]{0:T(128)} %rates.3) | copy-start | bytes 388
  39.3 17.8 %collective-permute-start.4 = (bf16[4,96,256]{2,1,0:T(8,128)(2,1)}, bf16[4,96,256]{2,1,0:T(8,128)(2,1)}, u32[]{:S(2)}, u32[]{:S(2)}) collective-permute-start(bf16[4,96,256]{2,1,0:T(8,128)(2,1)} %get-tuple-element.54), channel_id=1, source_target_pairs={{1,0},{2,1},{3,2},{4,3},{5,4},{6,5},{7,6},{9,8},{10,9},{11,10},{12... | collective-permute-start | bytes 589832 | tf_op jit(solution)/shard_map/ppermute | solution.py:284
  40.6 16.5 %collective-permute-start.3 = (bf16[4,96,256]{2,1,0:T(8,128)(2,1)}, bf16[4,96,256]{2,1,0:T(8,128)(2,1)}, u32[]{:S(2)}, u32[]{:S(2)}) collective-permute-start(bf16[4,96,256]{2,1,0:T(8,128)(2,1)} %get-tuple-element.55), channel_id=1, source_target_pairs={{0,1},{1,2},{2,3},{3,4},{4,5},{5,6},{6,7},{8,9},{9,10},{10,11},{11... | collective-permute-start | bytes 589832 | tf_op jit(solution)/shard_map/ppermute | solution.py:285
  57.1 9.9 %copy-start.34 = (bf16[3,3,96,96]{3,2,1,0:T(8,128)(2,1)S(1)}, bf16[3,3,96,96]{3,2,1,0:T(8,128)(2,1)}, u32[]{:S(2)}) copy-start(bf16[3,3,96,96]{3,2,1,0:T(8,128)(2,1)} %param.15) | copy-start | bytes 497668
  60.3 18.0 %collective-permute-start.6 = (bf16[4,96,256]{2,1,0:T(8,128)(2,1)}, bf16[4,96,256]{2,1,0:T(8,128)(2,1)}, u32[]{:S(2)}, u32[]{:S(2)}) collective-permute-start(bf16[4,96,256]{2,1,0:T(8,128)(2,1)} %get-tuple-element.50), channel_id=1, source_target_pairs={{1,0},{2,1},{3,2},{4,3},{5,4},{6,5},{7,6},{9,8},{10,9},{11,10},{12... | collective-permute-start | bytes 589832 | tf_op jit(solution)/shard_map/ppermute | solution.py:284
  61.5 16.7 %collective-permute-start.5 = (bf16[4,96,256]{2,1,0:T(8,128)(2,1)}, bf16[4,96,256]{2,1,0:T(8,128)(2,1)}, u32[]{:S(2)}, u32[]{:S(2)}) collective-permute-start(bf16[4,96,256]{2,1,0:T(8,128)(2,1)} %get-tuple-element.51), channel_id=1, source_target_pairs={{0,1},{1,2},{2,3},{3,4},{4,5},{5,6},{6,7},{8,9},{9,10},{10,11},{11... | collective-permute-start | bytes 589832 | tf_op jit(solution)/shard_map/ppermute | solution.py:285
  74.9 11.5 %copy-start.29 = (bf16[4,6,96,256]{3,2,1,0:T(8,128)(2,1)S(1)}, bf16[4,6,96,256]{3,2,1,0:T(8,128)(2,1)}, u32[]{:S(2)}) copy-start(bf16[4,6,96,256]{3,2,1,0:T(8,128)(2,1)} %copy-done.27) | copy-start | bytes 3538948
  74.9 11.5 %copy-start.32 = (bf16[4,6,96,256]{3,2,1,0:T(8,128)(2,1)S(1)}, bf16[4,6,96,256]{3,2,1,0:T(8,128)(2,1)}, u32[]{:S(2)}) copy-start(bf16[4,6,96,256]{3,2,1,0:T(8,128)(2,1)} %copy-done.30) | copy-start | bytes 3538948
  80.1 15.9 %collective-permute-start.8 = (bf16[4,96,256]{2,1,0:T(8,128)(2,1)S(1)}, bf16[4,96,256]{2,1,0:T(8,128)(2,1)S(1)}, u32[]{:S(2)}, u32[]{:S(2)}) collective-permute-start(bf16[4,96,256]{2,1,0:T(8,128)(2,1)S(1)} %get-tuple-element.48), channel_id=1, source_target_pairs={{1,0},{2,1},{3,2},{4,3},{5,4},{6,5},{7,6},{9,8},{10,9},{11,10},{12... | collective-permute-start | bytes 589832 | tf_op jit(solution)/shard_map/ppermute | solution.py:284
  81.4 14.6 %collective-permute-start.7 = (bf16[4,96,256]{2,1,0:T(8,128)(2,1)S(1)}, bf16[4,96,256]{2,1,0:T(8,128)(2,1)S(1)}, u32[]{:S(2)}, u32[]{:S(2)}) collective-permute-start(bf16[4,96,256]{2,1,0:T(8,128)(2,1)S(1)} %get-tuple-element.49), channel_id=1, source_target_pairs={{0,1},{1,2},{2,3},{3,4},{4,5},{5,6},{6,7},{8,9},{9,10},{10,11},{11... | collective-permute-start | bytes 589832 | tf_op jit(solution)/shard_map/ppermute | solution.py:285
  98.2 2.2 %collective-permute-start.9 = (f32[1344,128]{1,0:T(8,128)S(1)}, f32[1344,128]{1,0:T(8,128)S(1)}, u32[]{:S(2)}, u32[]{:S(2)}) collective-permute-start(f32[1344,128]{1,0:T(8,128)S(1)} %constant_dynamic-slice_fusion.3), channel_id=1, source_target_pairs={{0,8},{8,0},{1,9},{9,1},{2,10},{10,2},{3,11},{11,3},{4,12},{12,4},... | collective-permute-start | bytes 2064392 | tf_op jit(solution)/shard_map/ppermute | solution.py:297
  101.7 11.3 %collective-permute-start.10 = (f32[672,128]{1,0:T(8,128)S(1)}, f32[672,128]{1,0:T(8,128)S(1)}, u32[]{:S(2)}, u32[]{:S(2)}) collective-permute-start(f32[672,128]{1,0:T(8,128)S(1)} %constant_dynamic-slice_fusion.2), channel_id=1, source_target_pairs={{0,1},{1,0},{2,3},{3,2},{4,5},{5,4},{6,7},{7,6},{8,9},{9,8},{10,11... | collective-permute-start | bytes 1032200 | tf_op jit(solution)/shard_map/ppermute | solution.py:297
  113.1 5.9 %collective-permute-start.11 = (f32[336,128]{1,0:T(8,128)S(1)}, f32[336,128]{1,0:T(8,128)S(1)}, u32[]{:S(2)}, u32[]{:S(2)}) collective-permute-start(f32[336,128]{1,0:T(8,128)S(1)} %constant_dynamic-slice_fusion.1), channel_id=1, source_target_pairs={{0,2},{1,3},{2,0},{3,1},{4,6},{5,7},{6,4},{7,5},{8,10},{9,11},{10,... | collective-permute-start | bytes 516104 | tf_op jit(solution)/shard_map/ppermute | solution.py:297
  119.0 5.4 %collective-permute-start.12 = (f32[168,128]{1,0:T(8,128)S(1)}, f32[168,128]{1,0:T(8,128)S(1)}, u32[]{:S(2)}, u32[]{:S(2)}) collective-permute-start(f32[168,128]{1,0:T(8,128)S(1)} %constant_dynamic-slice_fusion), channel_id=1, source_target_pairs={{0,4},{1,5},{2,6},{3,7},{4,0},{5,1},{6,2},{7,3},{8,12},{9,13},{10,... | collective-permute-start | bytes 258056 | tf_op jit(solution)/shard_map/ppermute | solution.py:297
  124.5 5.5 %collective-permute-start.13 = (f32[168,128]{1,0:T(8,128)S(1)}, f32[168,128]{1,0:T(8,128)S(1)}, u32[]{:S(2)}, u32[]{:S(2)}) collective-permute-start(f32[168,128]{1,0:T(8,128)S(1)} %dynamic-slice_add_fusion.3), channel_id=1, source_target_pairs={{0,4},{1,5},{2,6},{3,7},{4,0},{5,1},{6,2},{7,3},{8,12},{9,13},{10,... | collective-permute-start | bytes 258056 | tf_op jit(solution)/shard_map/ppermute | solution.py:301
  130.0 5.5 %collective-permute-start.14 = (f32[336,128]{1,0:T(8,128)S(1)}, f32[336,128]{1,0:T(8,128)S(1)}, u32[]{:S(2)}, u32[]{:S(2)}) collective-permute-start(f32[336,128]{1,0:T(8,128)S(1)} %pad_maximum_fusion.3), channel_id=1, source_target_pairs={{0,2},{1,3},{2,0},{3,1},{4,6},{5,7},{6,4},{7,5},{8,10},{9,11},{10,... | collective-permute-start | bytes 516104 | tf_op jit(solution)/shard_map/ppermute | solution.py:301
  135.6 7.3 %collective-permute-start.15 = (f32[672,128]{1,0:T(8,128)S(1)}, f32[672,128]{1,0:T(8,128)S(1)}, u32[]{:S(2)}, u32[]{:S(2)}) collective-permute-start(f32[672,128]{1,0:T(8,128)S(1)} %pad_maximum_fusion.2), channel_id=1, source_target_pairs={{0,1},{1,0},{2,3},{3,2},{4,5},{5,4},{6,7},{7,6},{8,9},{9,8},{10,11... | collective-permute-start | bytes 1032200 | tf_op jit(solution)/shard_map/ppermute | solution.py:301
  143.8 2.4 %collective-permute-start.16 = (f32[1344,128]{1,0:T(8,128)}, f32[1344,128]{1,0:T(8,128)S(1)}, u32[]{:S(2)}, u32[]{:S(2)}) collective-permute-start(f32[1344,128]{1,0:T(8,128)} %pad_maximum_fusion.1), channel_id=1, source_target_pairs={{0,8},{8,0},{1,9},{9,1},{2,10},{10,2},{3,11},{11,3},{4,12},{12,4},... | collective-permute-start | bytes 2064392 | tf_op jit(solution)/shard_map/ppermute | solution.py:301
  (29 other events, 99.7 us)

commit v2 on v0

v2 whole, which is shorter than its diff:
```python
import functools

import jax
import jax.numpy as jnp
from jax import lax
from jax.experimental.layout import Layout, with_layout_constraint
from jax.experimental import pallas as pl
from jax.experimental.pallas import tpu as pltpu
from jax.sharding import PartitionSpec as P

F32 = jnp.float32
BF16 = jnp.bfloat16
LANES = 128
VMEM_LIMIT = 16 * 1024 * 1024


def call(body, name, flops, nbytes, vmem, **kw):
    return pl.pallas_call(
        body,
        name=name,
        cost_estimate=pl.CostEstimate(flops=flops, bytes_accessed=nbytes, transcendentals=0),
        compiler_params=pltpu.CompilerParams(vmem_limit_bytes=vmem),
        **kw,
    )


def whole_spec(shape):
    return pl.BlockSpec(shape, lambda *_: (0,) * len(shape))


def from_left(x):
    lane = lax.broadcasted_iota(jnp.int32, x.shape, 1)
    return jnp.where(lane == 0, jnp.zeros((), x.dtype), pltpu.roll(x, 1, 1))


def from_right(x):
    lane = lax.broadcasted_iota(jnp.int32, x.shape, 1)
    w = x.shape[1]
    return jnp.where(lane == w - 1, jnp.zeros((), x.dtype), pltpu.roll(x, w - 1, 1))


def shift_sum(y):
    c = y.shape[0] // 3
    return y[c : 2 * c] + from_left(y[:c]) + from_right(y[2 * c :])


def conv_rows(weights, rows, width, group=2):
    zero = jnp.zeros_like(rows[0])
    padded = [zero] + rows + [zero]
    sums = []
    for r0 in range(0, len(rows), group):
        columns = [
            jnp.concatenate(padded[r : r + 3], 0) for r in range(r0, min(r0 + group, len(rows)))
        ]
        y = jnp.dot(weights, jnp.concatenate(columns, 1), preferred_element_type=F32)
        for j in range(len(columns)):
            sums.append(shift_sum(y[:, j * width : (j + 1) * width]))
    return sums


def gather_body(pairs, slots, group, refs, out, *scratch, owner, frames):
    local_refs = refs.shape[0]
    picks = out.shape[0]
    g = group[0]
    wanted = (g if owner == 0 else 1 - g) * frames
    tiles, sems = (out, scratch[0]) if owner == 0 else scratch[:2]

    def fetch(i):
        slot = slots[pairs[i % 2, wanted + i // 2]] - g * local_refs
        slot = jnp.clip(slot, 0, local_refs - 1)
        return pltpu.make_async_copy(refs.at[slot], tiles.at[i], sems.at[i])

    def put(i):
        return pltpu.make_async_copy(tiles.at[i], out.at[i], scratch[2].at[i])

    for i in range(picks):
        fetch(i).start()
    for i in range(picks):
        fetch(i).wait()
        if owner:
            put(i).start()
    if owner:
        for i in range(picks):
            put(i).wait()


def prepare_body(jk, ok, w1, w2, w3, back):
    channels = ok.shape[1]
    taps = 3 * channels
    w1[...] = jnp.concatenate([jk[p * taps : (p + 1) * taps, :] for p in range(3)], 1)
    w2[...] = jnp.concatenate([ok[p * taps : (p + 1) * taps, :] for p in range(3)], 1)
    blocks = []
    for p in range(3):
        rows = []
        for q in range(3):
            at = ((2 - p) * 3 + 2 - q) * channels
            rows.append(ok[at : at + channels, :].astype(F32).T.astype(BF16))
        blocks.append(jnp.concatenate(rows, 0))
        back[p * taps : (p + 1) * taps, :] = blocks[-1]
    w3[...] = jnp.concatenate(blocks, 1)


def inside(tile, count, above, below):
    t = tile[0]
    return jnp.where(t > 0, above, jnp.zeros_like(above)), jnp.where(
        t < count - 1, below, jnp.zeros_like(below)
    )


def edge_sums(w, p, cells):
    taps = w.shape[0] // 3
    width = cells[0].shape[1]
    y = jnp.dot(
        w[p * taps : (p + 1) * taps, :],
        jnp.concatenate(cells, 1),
        preferred_element_type=F32,
    )
    return [shift_sum(y[:, k * width : (k + 1) * width]) for k in range(len(cells))]


def edge_taps_body(xr0, xc0, xr1, xc1, w, up, down):
    frames = up.shape[0]
    for xr, xc, p, out in ((xr0, xc0, 2, up), (xr1, xc1, 0, down)):
        cells = [jnp.concatenate([xr[b, 0], xc[b, 0]], 0) for b in range(frames)]
        for b, x in enumerate(edge_sums(w, p, cells)):
            out[b] = x.astype(BF16)


def silu_and_slope(v):
    s = jax.nn.sigmoid(v)
    return (v * s).astype(BF16), s * (1.0 + v * (1.0 - s))


def join_body(xr, xc, w, hidden, slope, top, bottom):
    rows, width = xr.shape[1], xr.shape[3]
    stacked = [jnp.concatenate([xr[0, r], xc[0, r]], 0) for r in range(rows)]
    sums = conv_rows(w[...], stacked, width)
    top[0] = sums[0]
    bottom[0] = sums[-1]
    for r in range(1, rows - 1):
        hidden[0, r - 1], slope[0, r - 1] = silu_and_slope(sums[r])


def join_edge_body(tile, top, bottom, above, below, ht, hb, st, sb, *, count):
    for b in range(top.shape[0]):
        got_a, got_b = inside(tile, count, above[b].astype(F32), below[b].astype(F32))
        ht[b], st[b] = silu_and_slope(top[b] + got_a)
        hb[b], sb[b] = silu_and_slope(bottom[b] + got_b)


def frame_scale(numbers, rates, group, cells, b, frames):
    return rates[numbers[group[0] * frames + b]] * (2.0 / cells)


def column(first, mid, last):
    return [first[0]] + [mid[0, r] for r in range(mid.shape[1])] + [last[0]]


def output_body(
    numbers, rates, group, hm, ht, hb, xc, w, recon, residual, top, bottom, *, cells, frames
):
    hidden = column(ht, hm, hb)
    sums = conv_rows(w[...], hidden, hm.shape[3])
    scale = frame_scale(numbers, rates, group, cells, pl.program_id(0), frames)
    top[0] = sums[0]
    bottom[0] = sums[-1]
    for r in range(1, len(sums) - 1):
        recon[0, r - 1] = sums[r].astype(BF16)
        residual[0, r - 1] = ((sums[r] - xc[0, r].astype(F32)) * scale).astype(BF16)


def output_edge_body(
    numbers, rates, group, tile, top, bottom, above, below, xc0, xc1, w, ct, cb, rt, rb,
    *, cells, frames, count
):
    frames = top.shape[0]
    got = inside(tile, count, above[...], below[...])
    for g, p, part, xc, c, r in (
        (got[0], 0, top, xc0, ct, rt),
        (got[1], 2, bottom, xc1, cb, rb),
    ):
        for b, x in enumerate(edge_sums(w, p, [g[b] for b in range(frames)])):
            scale = frame_scale(numbers, rates, group, cells, b, frames)
            total = part[b] + x
            c[b] = total.astype(BF16)
            r[b] = ((total - xc[b, 0].astype(F32)) * scale).astype(BF16)


def slope_body(rm, rt, rb, slope, w, grad, top, bottom):
    sums = conv_rows(w[...], column(rt, rm, rb), rm.shape[3])
    top[0] = sums[0]
    bottom[0] = sums[-1]
    for r in range(1, len(sums) - 1):
        grad[0, r - 1] = (sums[r] * slope[0, r - 1]).astype(BF16)


def slope_edge_body(tile, top, bottom, above, below, st, sb, w, gt, gb, *, count):
    got = inside(tile, count, above[...], below[...])
    for g, p, part, slope, grad in ((got[0], 0, top, st, gt), (got[1], 2, bottom, sb, gb)):
        for b, x in enumerate(edge_sums(w, p, [g[b] for b in range(g.shape[0])])):
            grad[b] = ((part[b] + x) * slope[b]).astype(BF16)


def contract(left, right):
    return lax.dot_general(left, right, (((1,), (1,)), ((), ())), preferred_element_type=F32)


def lane_blocks(x):
    return [x[:, k : k + LANES] for k in range(0, x.shape[1], LANES)]


def add_up(out, value):
    first = pl.program_id(0) == 0

    @pl.when(first)
    def _():
        out[...] = value

    @pl.when(jnp.logical_not(first))
    def _():
        out[...] += value


def side_taps(rows):
    return [[from_left(x) for x in rows], rows, [from_right(x) for x in rows]]


def out_grad_body(hm, ht, hb, rm, rt, rb, out):
    hidden = side_taps(column(ht, hm, hb))
    residual = column(rt, rm, rb)
    zero = jnp.zeros_like(residual[0])
    padded = [zero] + residual + [zero]
    rows = len(residual)
    value = contract(
        jnp.concatenate(
            [jnp.concatenate(padded[2 - p : 2 - p + rows], 1) for p in range(3)], 0
        ),
        jnp.concatenate([jnp.concatenate(h, 1) for h in hidden], 0),
    )
    add_up(out, value)


def grads_body(tile, gm, gt, gb, xr, xc, ht, hb, above, below, og, packed, *, count):
    rows, width = xr.shape[1], xr.shape[3]
    channels = gm.shape[2]
    joined = xr.shape[2] + xc.shape[2]
    rest = joined % 256
    head = joined - rest
    zero = jnp.zeros((channels, width), BF16)
    turned = side_taps(column(gt, gm, gb))[::-1]
    stacked = [jnp.concatenate([xr[0, r], xc[0, r]], 0) for r in range(rows)]
    taps = []
    for p in range(3):
        for q in range(3):
            taps.append(
                jnp.concatenate(
                    [turned[q][r - p + 1] if 0 <= r - p + 1 < rows else zero for r in range(rows)],
                    1,
                )
            )
    main = contract(jnp.concatenate(taps, 0), jnp.concatenate([s[:head] for s in stacked], 1))
    tails = [s[head:] for s in stacked]
    tail_zero = jnp.zeros_like(tails[0])
    tail = contract(
        jnp.concatenate([jnp.concatenate(turned[q], 1) for q in range(3)], 0),
        jnp.concatenate(
            [
                jnp.concatenate(
                    [tails[r + p - 1] if 0 <= r + p - 1 < rows else tail_zero for r in range(rows)],
                    1,
                )
                for p in range(3)
            ],
            0,
        ),
    )
    got = inside(tile, count, above[0], below[0])
    out = jnp.concatenate(
        [
            contract(got[1], jnp.concatenate([x[0] for x in side_taps([hb[0]])], 0)),
            jnp.zeros((channels, 3 * channels), F32),
            contract(got[0], jnp.concatenate([x[0] for x in side_taps([ht[0]])], 0)),
        ],
        0,
    )
    first = pl.program_id(0) == 0
    out = out + jnp.where(first, og[...], 0.0)
    blocks = lane_blocks(main) + lane_blocks(jnp.concatenate([out, tail], 1))

    @pl.when(first)
    def _():
        at = 0
        for block in blocks:
            packed[at : at + block.shape[0], :] = block
            at += block.shape[0]
        if at < packed.shape[0]:
            packed[at:, :] = jnp.zeros((packed.shape[0] - at, LANES), F32)

    @pl.when(jnp.logical_not(first))
    def _():
        at = 0
        for block in blocks:
            packed[at : at + block.shape[0], :] += block
            at += block.shape[0]


def grads_edge_body(
    tile, group, packed_in, above, below, xr0, xc0, xr1, xc1, send, keep, packed, *, count
):
    frames, channels, _ = above.shape
    joined = xr0.shape[2] + xc0.shape[2]
    rest = joined % 256
    head = joined - rest
    taps = 3 * channels
    half = send.shape[0]
    packed[...] = packed_in[...]
    tail_at = 3 * taps * (head // LANES)
    got = inside(tile, count, above[...], below[...])
    for p, edge, xr, xc in ((2, got[0], xr0, xc0), (0, got[1], xr1, xc1)):
        rows = [edge[b] for b in range(frames)]
        left = jnp.concatenate(
            [
                jnp.concatenate([move(g) for g in rows], 1)
                for move in (from_right, lambda g: g, from_left)
            ],
            0,
        )
        right = jnp.concatenate(
            [jnp.concatenate([xr[b, 0], xc[b, 0]], 0) for b in range(frames)], 1
        )
        extra = contract(left, right)
        for k, block in enumerate(lane_blocks(extra[:, :head])):
            at = 3 * taps * k + taps * p
            packed[at : at + taps, :] += block
        lane = taps + rest * p
        at = tail_at + taps * (lane // LANES)
        lane = lane % LANES
        packed[at : at + taps, lane : lane + rest] += extra[:, head:]
    g = group[0]
    send[...] = packed[pl.ds(pl.multiple_of((1 - g) * half, 8), half), :]
    keep[...] = packed[pl.ds(pl.multiple_of(g * half, 8), half), :]


def unpack_body(group, own, got, join, out, packed):
    channels = out.shape[2]
    joined = join.shape[3]
    rest = joined % 256
    head = joined - rest
    taps = 3 * channels
    half = own.shape[0]
    g = group[0]
    packed[pl.ds(pl.multiple_of(g * half, 8), half), :] = own[...].astype(F32)
    packed[pl.ds(pl.multiple_of((1 - g) * half, 8), half), :] = got[...].astype(F32)
    tail_at = 3 * taps * (head // LANES)
    tail = jnp.concatenate(
        [
            packed[tail_at + taps * k : tail_at + taps * (k + 1), :]
            for k in range((taps + 3 * rest) // LANES)
        ],
        1,
    )
    for p in range(3):
        for q in range(3):
            rows = slice(q * channels, (q + 1) * channels)
            at = taps * p + q * channels
            pieces = [
                packed[3 * taps * k + at : 3 * taps * k + at + channels, :]
                for k in range(head // LANES)
            ]
            pieces.append(tail[rows, taps + rest * p : taps + rest * (p + 1)])
            join[p, q] = jnp.concatenate(pieces, 1)
            out[p, q] = tail[p * channels : (p + 1) * channels, q * channels : (q + 1) * channels]


def swap_edges(up, down, axis):
    count = lax.axis_size(axis)
    below = lax.ppermute(up, axis, [((i + 1) % count, i) for i in range(count)])
    above = lax.ppermute(down, axis, [(i, (i + 1) % count) for i in range(count)])
    return above, below


def halves(part, axis, stride):
    bit = (lax.axis_index(axis) // stride) % 2
    half = part.shape[0] // 2
    send = lax.dynamic_slice_in_dim(part, (1 - bit) * half, half, 0)
    return send, lax.dynamic_slice_in_dim(part, bit * half, half, 0)


def on_device(
    decoded_refs,
    current_frames,
    ref_pairs,
    ref_slots,
    frame_numbers,
    rate_weights,
    join_kernel,
    out_kernel,
):
    local_refs = decoded_refs.shape[0]
    frames, channels, rows, width = current_frames.shape
    joined = join_kernel.shape[3]
    count = lax.axis_size("tile")
    cells = rows * count * width
    group = lax.axis_index("frame")
    group_id = group.reshape(1).astype(jnp.int32)
    tile_id = lax.axis_index("tile").reshape(1).astype(jnp.int32)
    picks = 2 * frames
    taps = 3 * channels
    conv_flops = 2 * frames * rows * width * 3 * taps

    def struct(shape, dtype):
        return jax.ShapeDtypeStruct(shape, dtype)

    def run(
        body, name, scalars, args, specs, outs, out_specs, grid, flops, nbytes, scratch=(),
        vmem=VMEM_LIMIT,
    ):
        return call(
            body,
            name,
            flops,
            nbytes,
            vmem,
            grid_spec=pltpu.PrefetchScalarGridSpec(
                num_scalar_prefetch=len(scalars),
                grid=grid,
                in_specs=specs,
                out_specs=out_specs,
                scratch_shapes=scratch,
            ),
            out_shape=outs,
        )(*scalars, *args)

    def each(x):
        return pl.BlockSpec((1,) + x.shape[1:], lambda b, *_: (b,) + (0,) * (len(x.shape) - 1))

    def whole(x):
        return whole_spec(x.shape)

    def row(x, r):
        return pl.BlockSpec((frames, 1) + x.shape[2:], lambda *_: (0, r, 0, 0))

    pairs_of = ref_pairs.T
    tile_shape = decoded_refs.shape[1:]

    def gathered(owner, name):
        return run(
            functools.partial(gather_body, owner=owner, frames=frames),
            name,
            (pairs_of, ref_slots, group_id),
            (pltpu.with_memory_space_constraint(decoded_refs, pltpu.HBM),),
            [pl.BlockSpec(memory_space=pltpu.HBM)],
            struct((picks,) + tile_shape, BF16),
            pl.BlockSpec(memory_space=pltpu.HBM if owner else pltpu.VMEM),
            (1,),
            0,
            4 * picks * channels * rows * width,
            ((pltpu.VMEM((picks,) + tile_shape, BF16),) if owner else ())
            + (pltpu.SemaphoreType.DMA((picks,)),) * (1 + owner),
            60 * 1024 * 1024 if owner else VMEM_LIMIT,
        )

    incoming = lax.ppermute(gathered(1, "gather_out"), "frame", [(0, 1), (1, 0)])
    own = gathered(0, "gather_own")
    pairs = lax.dynamic_slice_in_dim(ref_pairs, group * frames, frames, 0)
    slot_range = jnp.arange(ref_slots.shape[0], dtype=jnp.int32)
    slots = jnp.sum(jnp.where(pairs[:, :, None] == slot_range, ref_slots, 0), axis=-1)
    held = slots // local_refs == group
    picked = jnp.where(
        held[:, :, None, None, None],
        own.reshape(frames, 2, channels, rows, width),
        incoming.reshape(frames, 2, channels, rows, width),
    )
    xr = picked.transpose(0, 3, 1, 2, 4).reshape(frames, rows, 2 * channels, width)
    xc = current_frames.transpose(0, 2, 1, 3)

    jk = join_kernel.reshape(3 * taps, joined)
    ok = out_kernel.reshape(3 * taps, channels)
    prepared = [
        struct((taps, 3 * joined), BF16),
        struct((taps, taps), BF16),
        struct((taps, taps), BF16),
        struct((3 * taps, channels), BF16),
    ]
    w1, w2, w3, back = run(
        prepare_body, "prepare", (), (jk, ok), [whole(jk), whole(ok)], prepared,
        [whole(x) for x in prepared], (1,), 4 * jk.size, 4 * (jk.size + 3 * ok.size),
    )

    mid = (frames, rows - 2, channels, width)
    line = (frames, channels, width)
    mid_b, mid_f = struct(mid, BF16), struct(mid, F32)
    line_b, line_f = struct(line, BF16), struct(line, F32)
    edge_bytes = 24 * frames * channels * width
    mid_bytes = 10 * frames * rows * channels * width
    edge_flops = conv_flops * channels // (3 * rows) * 2

    up, down = run(
        edge_taps_body, "edge_taps", (), (xr, xc, xr, xc, jk),
        [row(xr, 0), row(xc, 0), row(xr, rows - 1), row(xc, rows - 1), whole(jk)],
        [line_b] * 2, [whole(line_b)] * 2, (1,), 3 * edge_flops, edge_bytes,
    )
    above, below = swap_edges(up, down, "tile")

    outs = [mid_b, mid_f, line_f, line_f]
    hm, sm, top, bottom = run(
        join_body, "join_conv", (), (xr, xc, w1), [each(xr), each(xc), whole(w1)],
        outs, [each(x) for x in outs], (frames,), conv_flops * joined, mid_bytes,
    )
    ht, hb, st, sb = run(
        functools.partial(join_edge_body, count=count), "join_edge", (tile_id,),
        (top, bottom, above, below), [whole(line_f)] * 4,
        [line_b, line_b, line_f, line_f], [whole(line_f)] * 4, (1,), edge_bytes, edge_bytes,
    )
    h_above, h_below = swap_edges(ht, hb, "tile")

    rated = (frame_numbers, rate_weights, group_id)
    outs = [mid_b, mid_b, line_f, line_f]
    cm, rm, top, bottom = run(
        functools.partial(output_body, cells=cells, frames=frames), "out_conv", rated,
        (hm, ht, hb, xc, w2), [each(x) for x in (hm, ht, hb, xc)] + [whole(w2)],
        outs, [each(x) for x in outs], (frames,), conv_flops * channels, mid_bytes,
    )
    ct, cb, rt, rb = run(
        functools.partial(output_edge_body, cells=cells, frames=frames, count=count),
        "out_edge", rated + (tile_id,), (top, bottom, h_above, h_below, xc, xc, ok),
        [whole(line_f)] * 4 + [row(xc, 0), row(xc, rows - 1), whole(ok)],
        [line_b] * 4, [whole(line_b)] * 4, (1,), edge_flops, edge_bytes,
    )
    r_above, r_below = swap_edges(rt, rb, "tile")

    outs = [mid_b, line_f, line_f]
    gm, top, bottom = run(
        slope_body, "back_conv", (), (rm, rt, rb, sm, w3),
        [each(x) for x in (rm, rt, rb, sm)] + [whole(w3)],
        outs, [each(x) for x in outs], (frames,), conv_flops * channels, mid_bytes,
    )
    og_s = struct((taps, taps), F32)
    og = run(
        out_grad_body, "out_grad", (), (hm, ht, hb, rm, rt, rb),
        [each(x) for x in (hm, ht, hb, rm, rt, rb)], og_s, whole(og_s), (frames,),
        conv_flops * channels, mid_bytes,
    )
    recon = jnp.concatenate([ct[:, None], cm, cb[:, None]], 1).transpose(0, 2, 1, 3)
    recon = with_layout_constraint(recon, Layout((0, 1, 2, 3)))
    gt, gb = run(
        functools.partial(slope_edge_body, count=count), "back_edge", (tile_id,),
        (top, bottom, r_above, r_below, st, sb, back), [whole(line_f)] * 6 + [whole(back)],
        [line_b] * 2, [whole(line_b)] * 2, (1,), edge_flops, edge_bytes,
    )
    g_above, g_below = swap_edges(gt, gb, "tile")

    strides = []
    while 1 << len(strides) < count:
        strides.append(1 << len(strides))
    unit = 8 * 2 * count
    packed_rows = 3 * taps * (joined + channels) // LANES
    packed_s = struct((pl.cdiv(packed_rows, unit) * unit, LANES), F32)
    half_s = struct((packed_s.shape[0] // 2, LANES), F32)
    args = (gm, gt, gb, xr, xc, ht, hb, r_above, r_below)
    packed = run(
        functools.partial(grads_body, count=count), "grads", (tile_id,), args + (og,),
        [each(x) for x in args] + [whole(og)], packed_s, whole(packed_s), (frames,),
        conv_flops * joined, 2 * mid_bytes,
    )
    send, part = run(
        functools.partial(grads_edge_body, count=count), "grads_edge", (tile_id, group_id),
        (packed, g_above, g_below, xr, xc, xr, xc),
        [whole(packed_s), whole(line_b), whole(line_b)]
        + [row(xr, 0), row(xc, 0), row(xr, rows - 1), row(xc, rows - 1)],
        [half_s] * 2, [whole(half_s)] * 2, (1,), 3 * edge_flops, edge_bytes,
        (pltpu.VMEM(packed_s.shape, F32),),
    )
    part = part + lax.ppermute(send, "frame", [(0, 1), (1, 0)])
    for stride in strides[:-1]:
        send, keep = halves(part, "tile", stride)
        pairs = [(i, i ^ stride) for i in range(count)]
        part = keep + lax.ppermute(send.astype(BF16), "tile", pairs).astype(F32)
    part = part.astype(BF16)
    pairs = [(i, i ^ strides[-1]) for i in range(count)]
    got = lax.ppermute(part, "tile", pairs)
    part = (part.astype(F32) + got.astype(F32)).astype(BF16)
    part, recon = lax.optimization_barrier((part, recon))
    for stride in reversed(strides[:-1]):
        bit = (lax.axis_index("tile") // stride) % 2
        got = lax.ppermute(part, "tile", [(i, i ^ stride) for i in range(count)])
        part = jnp.concatenate(
            [jnp.where(bit == 0, part, got), jnp.where(bit == 0, got, part)], 0
        )
    got = lax.ppermute(part, "frame", [(0, 1), (1, 0)])
    outs = [struct(join_kernel.shape, F32), struct(out_kernel.shape, F32)]
    join_total, out_total = run(
        unpack_body, "unpack", (group_id,), (part, got), [whole(half_s)] * 2,
        outs, [whole(x) for x in outs], (1,), 0, 8 * packed_s.size,
        (pltpu.VMEM(packed_s.shape, F32),),
    )
    return recon, join_total, out_total


def solution(mesh):
    placed = (
        P(("parts", "frame"), None, "tile", None),
        P(("parts", "frame"), None, "tile", None),
        P("parts", None),
        P("parts"),
        P("parts"),
        P("parts"),
        P(),
        P(),
    )
    return jax.shard_map(
        on_device,
        mesh=mesh,
        in_specs=placed,
        out_specs=(
            P(("parts", "frame"), None, "tile", None),
            P("parts", None, None, None),
            P("parts", None, None, None),
        ),
        check_vma=False,
    )
```

time: 320 us -> 103 us (0.32)
  matrix products: 120 us -> 0 us
  waiting for transfers between devices: 123 us -> 34.6 us
  Pallas kernels: 0 us -> 36.9 us
  local copies, waits for them, and re-layouts: 20.6 us -> 3.42 us
  between operations: 14.7 us -> 0.99 us
  other arithmetic: 18 us -> 7.14 us
    dot_general x45 -> x0, matrix products: 120 us -> none  [the longest x18 67.6 us: apply_taps(): jnp.einsum('oi,bihw->bohw', kernel[row_tap, col_tap], window, preferred_e...]
    psum x1 -> x0, waiting for transfers between devices: 95.2 us -> none  [on_device(): lax.psum((join_part, output_part), ('frame', 'tile'))]
    pallas_call x0 -> x14, Pallas kernels: none -> 36.9 us  [run(): call(body, name, flops, nbytes, vmem, grid_spec=pltpu.PrefetchScalarGridS...]
    concatenate x3 -> x2, other arithmetic: 9.9 us -> 0.04 us  [on_device(): jnp.concatenate([jnp.where(bit == 0, part, got), jnp.where(bit == 0, got,...]
    unnamed x26 -> x13, local copies, waits for them, and re-layouts: 10.2 us -> 1.87 us
    gather x2 -> x0, local copies, waits for them, and re-layouts: 7.07 us -> none  [the longest x1 3.54 us: on_device(): jnp.take(decoded_refs, jnp.clip(mine_local, 0, local_refs - 1), axis=0)]
    ppermute x7 -> x16, waiting for transfers between devices: 28 us -> 34.6 us  [the longest x2 9.3 us: on_device(): part = keep + lax.ppermute(send.astype(BF16), 'tile', pairs).astype(F32)]
    ppermute x7 -> x16, starting transfers between devices: 19.8 us -> 19.1 us  [the longest x4 13.6 us: swap_edges(): below = lax.ppermute(up, axis, [((i + 1) % count, i) for i in range(count)])]
  transfers between devices with their start and end apart: 8 -> 16, of which waited for: 5 -> 12; matrix products, arithmetic and copies ran while one was open for 6% -> 6% of each run, Pallas kernels for 0% -> 26%
where the time goes in v2:
time: 103 us; the launch traced here: 102 us
  Pallas kernels  36.9 us (36%)
  waiting for transfers between devices  34.6 us (34%)
  starting transfers between devices  19.1 us (19%)
  other arithmetic  7.14 us (7%)
  local copies, waits for them, and re-layouts  3.42 us (3%)
    pallas_call x14, Pallas kernels, run(): call(body, name, flops, nbytes, vmem, grid_spec=pltpu.PrefetchScalarGridS...  36.9 us
    ppermute x4, starting transfers between devices, swap_edges(): below = lax.ppermute(up, axis, [((i + 1) % count, i) for i in range(count)])  13.6 us
    ppermute x2, waiting for transfers between devices, on_device(): part = keep + lax.ppermute(send.astype(BF16), 'tile', pairs).astype(F32)  9.3 us
    ppermute x2, waiting for transfers between devices, on_device(): got = lax.ppermute(part, 'tile', [(i, i ^ stride) for i in range(count)])  9 us
    ppermute x4, waiting for transfers between devices, swap_edges(): lax.ppermute(down, axis, [(i, (i + 1) % count) for i in range(count)])  7.56 us
    select_n x1, other arithmetic, on_device(): jnp.where(held[:, :, None, None, None], own.reshape(frames, 2, channels,...  3.09 us
    ppermute x4, starting transfers between devices, swap_edges(): lax.ppermute(down, axis, [(i, (i + 1) % count) for i in range(count)])  3.06 us
    ppermute x1, waiting for transfers between devices, on_device(): got = lax.ppermute(part, 'tile', pairs)  2.85 us
  transfers between devices with their start and end apart: 16, of which 12 were waited for; matrix products, arithmetic and copies ran while one was open for 6% of the time, Pallas kernels for 26%

profile of v2, /device:TPU:0, one launch (start us, length us, event | category | flops | bytes accessed | tf_op | source)
XLA Modules:
  0.0 102.2 jit_solution(15337575809659928692)
XLA Ops:
  0.7 4.6 %gather_out.1 = bf16[8,96,8,256]{3,2,1,0:T(8,128)(2,1)} custom-call(s32[2,8]{1,0:T(2,128)} %bitcast.39, s32[32]{0:T(128)} %slots.3, s32[1]{0:T(128)} %bitcast.1.group, bf16[16,96,8,256]{3,2,1,0:T(8,128)(2,1)} %refs.3), custom_call_target="tpu_custom_call" | custom-call | bytes 6291456 | tf_op jit(solution)/shard_map/gather_out/pallas_call | solution.py:418
  5.7 2.8 %gather_own.1 = bf16[8,96,8,256]{3,2,1,0:T(8,128)(2,1)S(1)} custom-call(s32[2,8]{1,0:T(2,128)S(1)} %bitcast.40, s32[32]{0:T(128)S(1)} %copy-done.3, s32[1]{0:T(128)} %bitcast.1.group, bf16[16,96,8,256]{3,2,1,0:T(8,128)(2,1)} %refs.3), custom_call_target="tpu_custom_call" | custom-call | bytes 6291456 | tf_op jit(solution)/shard_map/gather_own/pallas_call | solution.py:418
  9.0 1.8 %copy.33 = bf16[4,96,8,256]{3,1,2,0:T(8,128)(2,1)S(1)} copy(bf16[4,96,8,256]{3,2,1,0:T(8,128)(2,1)} %param.9) | data formatting | bytes 3145728 | tf_op args[1]
  11.3 3.1 %copy_select_fusion = bf16[4,2,96,8,256]{4,2,1,3,0:T(8,128)(2,1)S(1)} fusion(bf16[4,2,96,8,256]{4,3,2,1,0:T(8,128)(2,1)} %bitcast.4, bf16[4,2,96,8,256]{4,3,2,1,0:T(8,128)(2,1)S(1)} %bitcast.32, pred[4,2]{1,0:T(4,128)(4,1)S(1)} %copy.23), kind=kLoop, calls=%fused_computation | loop fusion | flops 1572864 | bytes 9437192 | tf_op jit(solution)/shard_map/jit(_where)/select_n | solution.py:469
  15.3 3.0 %collective-permute-start.1 = (bf16[4,96,256]{2,1,0:T(8,128)(2,1)S(1)}, bf16[4,96,256]{2,1,0:T(8,128)(2,1)S(1)}, u32[]{:S(2)}, u32[]{:S(2)}) collective-permute-start(bf16[4,96,256]{2,1,0:T(8,128)(2,1)S(1)} %get-tuple-element.40), channel_id=1, source_target_pairs={{0,1},{1,2},{2,3},{3,4},{4,5},{5,6},{6,7},{7,0},{8,9},{9,10},{10,1... | collective-permute-start | bytes 589832 | tf_op jit(solution)/shard_map/ppermute | solution.py:378
  18.3 3.1 %collective-permute-start.2 = (bf16[4,96,256]{2,1,0:T(8,128)(2,1)S(1)}, bf16[4,96,256]{2,1,0:T(8,128)(2,1)S(1)}, u32[]{:S(2)}, u32[]{:S(2)}) collective-permute-start(bf16[4,96,256]{2,1,0:T(8,128)(2,1)S(1)} %get-tuple-element.41), channel_id=1, source_target_pairs={{1,0},{2,1},{3,2},{4,3},{5,4},{6,5},{7,6},{0,7},{9,8},{10,9},{11,1... | collective-permute-start | bytes 589832 | tf_op jit(solution)/shard_map/ppermute | solution.py:377
  21.4 5.9 %join_conv.1 = (bf16[4,6,96,256]{3,2,1,0:T(8,128)(2,1)S(1)}, f32[4,6,96,256]{3,2,1,0:T(8,128)S(1)}, f32[4,96,256]{2,1,0:T(8,128)S(1)}, f32[4,96,256]{2,1,0:T(8,128)S(1)}) custom-call(bf16[4,8,192,256]{3,2,1,0:T(8,128)(2,1)S(1)} %bitcast.19, bf16[4,8,96,256]{3,2,1,0:T(8,128)(2,1)S(1)} %bitcast.25, bf16[288,864]{1,0:T(8,128)(2,1)S(1)} %get-tuple-element.36.w), custom_call_target="tpu_custom_call" | custom-call | flops 4076863488 | bytes 7864320 | tf_op jit(solution)/shard_map/join_conv/pallas_call | solution.py:418
  27.3 1.9 %collective-permute-done.2.below = bf16[4,96,256]{2,1,0:T(8,128)(2,1)S(1)} collective-permute-done((bf16[4,96,256]{2,1,0:T(8,128)(2,1)S(1)}, bf16[4,96,256]{2,1,0:T(8,128)(2,1)S(1)}, u32[]{:S(2)}, u32[]{:S(2)}) %collective-permute-start.2) | collective-permute-done | bytes 196640 | tf_op jit(solution)/shard_map/ppermute | solution.py:377
  29.5 3.4 %collective-permute-start.4 = (bf16[4,96,256]{2,1,0:T(8,128)(2,1)S(1)}, bf16[4,96,256]{2,1,0:T(8,128)(2,1)S(1)}, u32[]{:S(2)}, u32[]{:S(2)}) collective-permute-start(bf16[4,96,256]{2,1,0:T(8,128)(2,1)S(1)} %get-tuple-element.42.ht), channel_id=1, source_target_pairs={{1,0},{2,1},{3,2},{4,3},{5,4},{6,5},{7,6},{0,7},{9,8},{10,9},{11,1... | collective-permute-start | bytes 589832 | tf_op jit(solution)/shard_map/ppermute | solution.py:377
  32.9 3.9 %out_conv.1 = (bf16[4,6,96,256]{3,2,1,0:T(8,128)(2,1)S(1)}, bf16[4,6,96,256]{3,2,1,0:T(8,128)(2,1)S(1)}, f32[4,96,256]{2,1,0:T(8,128)S(1)}, f32[4,96,256]{2,1,0:T(8,128)S(1)}) custom-call(s32[8]{0:T(128)S(1)} %copy-done.4, f32[32]{0:T(128)S(1)} %copy-done.5, s32[1]{0:T(128)} %bitcast.1.group, bf16[4,6,96,256]{3,2,1,0:T(8,128)(2,1)S(1)} %get-tuple-element.37.hm, ...), custom_call_target="tpu_custom_call" | custom-call | flops 1358954496 | bytes 7864320 | tf_op jit(solution)/shard_map/out_conv/pallas_call | solution.py:418
  36.8 4.6 %collective-permute-done.3.above = bf16[4,96,256]{2,1,0:T(8,128)(2,1)S(1)} collective-permute-done((bf16[4,96,256]{2,1,0:T(8,128)(2,1)S(1)}, bf16[4,96,256]{2,1,0:T(8,128)(2,1)S(1)}, u32[]{:S(2)}, u32[]{:S(2)}) %collective-permute-start.3) | collective-permute-done | bytes 196640 | tf_op jit(solution)/shard_map/ppermute | solution.py:378
  42.6 3.7 %collective-permute-start.6 = (bf16[4,96,256]{2,1,0:T(8,128)(2,1)S(1)}, bf16[4,96,256]{2,1,0:T(8,128)(2,1)S(1)}, u32[]{:S(2)}, u32[]{:S(2)}) collective-permute-start(bf16[4,96,256]{2,1,0:T(8,128)(2,1)S(1)} %get-tuple-element.48.rt), channel_id=1, source_target_pairs={{1,0},{2,1},{3,2},{4,3},{5,4},{6,5},{7,6},{0,7},{9,8},{10,9},{11,1... | collective-permute-start | bytes 589832 | tf_op jit(solution)/shard_map/ppermute | solution.py:377
  46.3 3.7 %out_grad.1.og = f32[288,288]{1,0:T(8,128)S(1)} custom-call(bf16[4,6,96,256]{3,2,1,0:T(8,128)(2,1)S(1)} %get-tuple-element.37.hm, bf16[4,96,256]{2,1,0:T(8,128)(2,1)S(1)} %get-tuple-element.42.ht, bf16[4,96,256]{2,1,0:T(8,128)(2,1)S(1)} %get-tuple-element.43.hb, bf16[4,6,96,256]{3,2,1,0:T(8,128)(2,1)S(1)} %get-tuple-element.45.rm, ...), custom_call_target="tpu_custom_call" | custom-call | flops 1358954496 | bytes 7864320 | tf_op jit(solution)/shard_map/out_grad/pallas_call | solution.py:418
  50.0 3.4 %back_conv.1 = (bf16[4,6,96,256]{3,2,1,0:T(8,128)(2,1)S(1)}, f32[4,96,256]{2,1,0:T(8,128)S(1)}, f32[4,96,256]{2,1,0:T(8,128)S(1)}) custom-call(bf16[4,6,96,256]{3,2,1,0:T(8,128)(2,1)S(1)} %get-tuple-element.45.rm, bf16[4,96,256]{2,1,0:T(8,128)(2,1)S(1)} %get-tuple-element.48.rt, bf16[4,96,256]{2,1,0:T(8,128)(2,1)S(1)} %get-tuple-element.49.rb, ...), custom_call_target="tpu_custom_call" | custom-call | flops 1358954496 | bytes 7864320 | tf_op jit(solution)/shard_map/back_conv/pallas_call | solution.py:418
  55.4 3.5 %collective-permute-start.8 = (bf16[4,96,256]{2,1,0:T(8,128)(2,1)S(1)}, bf16[4,96,256]{2,1,0:T(8,128)(2,1)S(1)}, u32[]{:S(2)}, u32[]{:S(2)}) collective-permute-start(bf16[4,96,256]{2,1,0:T(8,128)(2,1)S(1)} %get-tuple-element.58.gt), channel_id=1, source_target_pairs={{1,0},{2,1},{3,2},{4,3},{5,4},{6,5},{7,6},{0,7},{9,8},{10,9},{11,1... | collective-permute-start | bytes 589832 | tf_op jit(solution)/shard_map/ppermute | solution.py:377
  58.8 6.7 %grads.1.packed_in = f32[2688,128]{1,0:T(8,128)S(1)} custom-call(s32[1]{0:T(128)} %bitcast.tile, bf16[4,6,96,256]{3,2,1,0:T(8,128)(2,1)S(1)} %get-tuple-element.52.gm, bf16[4,96,256]{2,1,0:T(8,128)(2,1)S(1)} %get-tuple-element.58.gt, bf16[4,96,256]{2,1,0:T(8,128)(2,1)S(1)} %get-tuple-element.59.gb, bf16[4,8,192,256]{3,2,1,0:T(8,128)(2,1)S(1)} %bitcast.20, ...), custom_call_target="tpu_custom_call" | custom-call | flops 4076863488 | bytes 15728640 | tf_op jit(solution)/shard_map/grads/pallas_call | solution.py:418
  65.6 1.7 %collective-permute-done.7.above = bf16[4,96,256]{2,1,0:T(8,128)(2,1)S(1)} collective-permute-done((bf16[4,96,256]{2,1,0:T(8,128)(2,1)S(1)}, bf16[4,96,256]{2,1,0:T(8,128)(2,1)S(1)}, u32[]{:S(2)}, u32[]{:S(2)}) %collective-permute-start.7) | collective-permute-done | bytes 196640 | tf_op jit(solution)/shard_map/ppermute | solution.py:378
  68.4 2.2 %collective-permute-done.9 = f32[1344,128]{1,0:T(8,128)} collective-permute-done((f32[1344,128]{1,0:T(8,128)S(1)}, f32[1344,128]{1,0:T(8,128)}, u32[]{:S(2)}, u32[]{:S(2)}) %collective-permute-start.9) | collective-permute-done | bytes 688160 | tf_op jit(solution)/shard_map/ppermute | solution.py:574
  72.1 6.2 %collective-permute-done.10 = bf16[672,128]{1,0:T(8,128)(2,1)S(1)} collective-permute-done((bf16[672,128]{1,0:T(8,128)(2,1)S(1)}, bf16[672,128]{1,0:T(8,128)(2,1)S(1)}, u32[]{:S(2)}, u32[]{:S(2)}) %collective-permute-start.10) | collective-permute-done | bytes 172064 | tf_op jit(solution)/shard_map/ppermute | solution.py:578
  79.8 3.1 %collective-permute-done.11 = bf16[336,128]{1,0:T(8,128)(2,1)S(1)} collective-permute-done((bf16[336,128]{1,0:T(8,128)(2,1)S(1)}, bf16[336,128]{1,0:T(8,128)(2,1)S(1)}, u32[]{:S(2)}, u32[]{:S(2)}) %collective-permute-start.11) | collective-permute-done | bytes 86048 | tf_op jit(solution)/shard_map/ppermute | solution.py:578
  83.4 2.5 %maximum_bitcast_fusion = bf16[4,96,8,256]{3,2,1,0:T(8,128)(2,1)} fusion(bf16[4,1,96,256]{3,1,2,0:T(2,128)(2,1)S(1)} %copy.29, bf16[4,6,96,256]{3,1,2,0:T(8,128)(2,1)S(1)} %copy.28, bf16[4,1,96,256]{3,1,2,0:T(2,128)(2,1)S(1)} %copy.27), kind=kLoop, calls=%fused_computation.1 | loop fusion | flops 4718592 | bytes 3145728 | tf_op jit(solution)/shard_map/transpose | solution.py:544
  85.9 2.8 %collective-permute-done.12 = bf16[336,128]{1,0:T(8,128)(2,1)S(1)} collective-permute-done((bf16[336,128]{1,0:T(8,128)(2,1)S(1)}, bf16[336,128]{1,0:T(8,128)(2,1)S(1)}, u32[]{:S(2)}, u32[]{:S(2)}) %collective-permute-start.12) | collective-permute-done | bytes 86048 | tf_op jit(solution)/shard_map/ppermute | solution.py:581
  88.9 4.5 %collective-permute-done.13 = bf16[336,128]{1,0:T(8,128)(2,1)S(1)} collective-permute-done((bf16[336,128]{1,0:T(8,128)(2,1)S(1)}, bf16[336,128]{1,0:T(8,128)(2,1)S(1)}, u32[]{:S(2)}, u32[]{:S(2)}) %collective-permute-start.13) | collective-permute-done | bytes 86048 | tf_op jit(solution)/shard_map/ppermute | solution.py:586
  94.3 4.5 %collective-permute-done.14 = bf16[672,128]{1,0:T(8,128)(2,1)S(1)} collective-permute-done((bf16[672,128]{1,0:T(8,128)(2,1)S(1)}, bf16[672,128]{1,0:T(8,128)(2,1)S(1)}, u32[]{:S(2)}, u32[]{:S(2)}) %collective-permute-start.14) | collective-permute-done | bytes 172064 | tf_op jit(solution)/shard_map/ppermute | solution.py:586
  (54 shorter events, 14.8 us)
Async XLA Ops:
  0.6 5.0 %copy-start.2 = (s32[8,2]{0,1:T(2,128)S(1)}, s32[8,2]{0,1:T(2,128)}, u32[]{:S(2)}) copy-start(s32[8,2]{0,1:T(2,128)} %param.10) | copy-start | bytes 196
  0.6 5.0 %copy-start.3 = (s32[32]{0:T(128)S(1)}, s32[32]{0:T(128)}, u32[]{:S(2)}) copy-start(s32[32]{0:T(128)} %slots.3) | copy-start | bytes 388
  5.3 6.1 %collective-permute-start = (bf16[8,96,8,256]{3,2,1,0:T(8,128)(2,1)}, bf16[8,96,8,256]{3,2,1,0:T(8,128)(2,1)}, u32[]{:S(2)}, u32[]{:S(2)}) collective-permute-start(bf16[8,96,8,256]{3,2,1,0:T(8,128)(2,1)} %gather_out.1), channel_id=1, source_target_pairs={{0,8},{8,0},{1,9},{9,1},{2,10},{10,2},{3,11},{11,3},{4,12},{12,4},... | collective-permute-start | bytes 9437192 | tf_op jit(solution)/shard_map/ppermute | solution.py:463
  8.5 2.3 %copy-start.1 = (bf16[3,3,96,96]{3,2,1,0:T(8,128)(2,1)S(1)}, bf16[3,3,96,96]{3,2,1,0:T(8,128)(2,1)}, u32[]{:S(2)}) copy-start(bf16[3,3,96,96]{3,2,1,0:T(8,128)(2,1)} %param.15) | copy-start | bytes 497668
  9.0 1.9 %copy-start = (bf16[3,3,96,288]{3,2,1,0:T(8,128)(2,1)S(1)}, bf16[3,3,96,288]{3,2,1,0:T(8,128)(2,1)}, u32[]{:S(2)}) copy-start(bf16[3,3,96,288]{3,2,1,0:T(8,128)(2,1)} %param.14) | copy-start | bytes 1492996
  15.3 12.0 %collective-permute-start.1 = (bf16[4,96,256]{2,1,0:T(8,128)(2,1)S(1)}, bf16[4,96,256]{2,1,0:T(8,128)(2,1)S(1)}, u32[]{:S(2)}, u32[]{:S(2)}) collective-permute-start(bf16[4,96,256]{2,1,0:T(8,128)(2,1)S(1)} %get-tuple-element.40), channel_id=1, source_target_pairs={{0,1},{1,2},{2,3},{3,4},{4,5},{5,6},{6,7},{7,0},{8,9},{9,10},{10,1... | collective-permute-start | bytes 589832 | tf_op jit(solution)/shard_map/ppermute | solution.py:378
  18.3 10.9 %collective-permute-start.2 = (bf16[4,96,256]{2,1,0:T(8,128)(2,1)S(1)}, bf16[4,96,256]{2,1,0:T(8,128)(2,1)S(1)}, u32[]{:S(2)}, u32[]{:S(2)}) collective-permute-start(bf16[4,96,256]{2,1,0:T(8,128)(2,1)S(1)} %get-tuple-element.41), channel_id=1, source_target_pairs={{1,0},{2,1},{3,2},{4,3},{5,4},{6,5},{7,6},{0,7},{9,8},{10,9},{11,1... | collective-permute-start | bytes 589832 | tf_op jit(solution)/shard_map/ppermute | solution.py:377
  21.4 11.5 %copy-start.4 = (s32[8]{0:T(128)S(1)}, s32[8]{0:T(128)}, u32[]{:S(2)}) copy-start(s32[8]{0:T(128)} %numbers.3) | copy-start | bytes 100
  21.4 11.5 %copy-start.5 = (f32[32]{0:T(128)S(1)}, f32[32]{0:T(128)}, u32[]{:S(2)}) copy-start(f32[32]{0:T(128)} %rates.3) | copy-start | bytes 388
  29.5 7.3 %collective-permute-start.4 = (bf16[4,96,256]{2,1,0:T(8,128)(2,1)S(1)}, bf16[4,96,256]{2,1,0:T(8,128)(2,1)S(1)}, u32[]{:S(2)}, u32[]{:S(2)}) collective-permute-start(bf16[4,96,256]{2,1,0:T(8,128)(2,1)S(1)} %get-tuple-element.42.ht), channel_id=1, source_target_pairs={{1,0},{2,1},{3,2},{4,3},{5,4},{6,5},{7,6},{0,7},{9,8},{10,9},{11,1... | collective-permute-start | bytes 589832 | tf_op jit(solution)/shard_map/ppermute | solution.py:377
  32.9 8.5 %collective-permute-start.3 = (bf16[4,96,256]{2,1,0:T(8,128)(2,1)S(1)}, bf16[4,96,256]{2,1,0:T(8,128)(2,1)S(1)}, u32[]{:S(2)}, u32[]{:S(2)}) collective-permute-start(bf16[4,96,256]{2,1,0:T(8,128)(2,1)S(1)} %get-tuple-element.43.hb), channel_id=1, source_target_pairs={{0,1},{1,2},{2,3},{3,4},{4,5},{5,6},{6,7},{7,0},{8,9},{9,10},{10,1... | collective-permute-start | bytes 589832 | tf_op jit(solution)/shard_map/ppermute | solution.py:378
  42.6 10.8 %collective-permute-start.6 = (bf16[4,96,256]{2,1,0:T(8,128)(2,1)S(1)}, bf16[4,96,256]{2,1,0:T(8,128)(2,1)S(1)}, u32[]{:S(2)}, u32[]{:S(2)}) collective-permute-start(bf16[4,96,256]{2,1,0:T(8,128)(2,1)S(1)} %get-tuple-element.48.rt), channel_id=1, source_target_pairs={{1,0},{2,1},{3,2},{4,3},{5,4},{6,5},{7,6},{0,7},{9,8},{10,9},{11,1... | collective-permute-start | bytes 589832 | tf_op jit(solution)/shard_map/ppermute | solution.py:377
  46.3 8.4 %collective-permute-start.5 = (bf16[4,96,256]{2,1,0:T(8,128)(2,1)S(1)}, bf16[4,96,256]{2,1,0:T(8,128)(2,1)S(1)}, u32[]{:S(2)}, u32[]{:S(2)}) collective-permute-start(bf16[4,96,256]{2,1,0:T(8,128)(2,1)S(1)} %get-tuple-element.49.rb), channel_id=1, source_target_pairs={{0,1},{1,2},{2,3},{3,4},{4,5},{5,6},{6,7},{7,0},{8,9},{9,10},{10,1... | collective-permute-start | bytes 589832 | tf_op jit(solution)/shard_map/ppermute | solution.py:378
  55.4 10.2 %collective-permute-start.8 = (bf16[4,96,256]{2,1,0:T(8,128)(2,1)S(1)}, bf16[4,96,256]{2,1,0:T(8,128)(2,1)S(1)}, u32[]{:S(2)}, u32[]{:S(2)}) collective-permute-start(bf16[4,96,256]{2,1,0:T(8,128)(2,1)S(1)} %get-tuple-element.58.gt), channel_id=1, source_target_pairs={{1,0},{2,1},{3,2},{4,3},{5,4},{6,5},{7,6},{0,7},{9,8},{10,9},{11,1... | collective-permute-start | bytes 589832 | tf_op jit(solution)/shard_map/ppermute | solution.py:377
  58.8 8.4 %collective-permute-start.7 = (bf16[4,96,256]{2,1,0:T(8,128)(2,1)S(1)}, bf16[4,96,256]{2,1,0:T(8,128)(2,1)S(1)}, u32[]{:S(2)}, u32[]{:S(2)}) collective-permute-start(bf16[4,96,256]{2,1,0:T(8,128)(2,1)S(1)} %get-tuple-element.59.gb), channel_id=1, source_target_pairs={{0,1},{1,2},{2,3},{3,4},{4,5},{5,6},{6,7},{7,0},{8,9},{9,10},{10,1... | collective-permute-start | bytes 589832 | tf_op jit(solution)/shard_map/ppermute | solution.py:378
  68.3 2.3 %collective-permute-start.9 = (f32[1344,128]{1,0:T(8,128)S(1)}, f32[1344,128]{1,0:T(8,128)}, u32[]{:S(2)}, u32[]{:S(2)}) collective-permute-start(f32[1344,128]{1,0:T(8,128)S(1)} %get-tuple-element.61), channel_id=1, source_target_pairs={{0,8},{8,0},{1,9},{9,1},{2,10},{10,2},{3,11},{11,3},{4,12},{12,4},... | collective-permute-start | bytes 2064392 | tf_op jit(solution)/shard_map/ppermute | solution.py:574
  71.8 6.5 %collective-permute-start.10 = (bf16[672,128]{1,0:T(8,128)(2,1)S(1)}, bf16[672,128]{1,0:T(8,128)(2,1)S(1)}, u32[]{:S(2)}, u32[]{:S(2)}) collective-permute-start(bf16[672,128]{1,0:T(8,128)(2,1)S(1)} %dynamic-slice_convert_fusion), channel_id=1, source_target_pairs={{0,1},{1,0},{2,3},{3,2},{4,5},{5,4},{6,7},{7,6},{8,9},{9,8},{10,11... | collective-permute-start | bytes 516104 | tf_op jit(solution)/shard_map/ppermute | solution.py:578
  78.4 4.6 %collective-permute-start.11 = (bf16[336,128]{1,0:T(8,128)(2,1)S(1)}, bf16[336,128]{1,0:T(8,128)(2,1)S(1)}, u32[]{:S(2)}, u32[]{:S(2)}) collective-permute-start(bf16[336,128]{1,0:T(8,128)(2,1)S(1)} %dynamic-slice_convert_fusion.1), channel_id=1, source_target_pairs={{0,2},{1,3},{2,0},{3,1},{4,6},{5,7},{6,4},{7,5},{8,10},{9,11},{10,... | collective-permute-start | bytes 258056 | tf_op jit(solution)/shard_map/ppermute | solution.py:578
  82.9 5.8 %collective-permute-start.12 = (bf16[336,128]{1,0:T(8,128)(2,1)S(1)}, bf16[336,128]{1,0:T(8,128)(2,1)S(1)}, u32[]{:S(2)}, u32[]{:S(2)}) collective-permute-start(bf16[336,128]{1,0:T(8,128)(2,1)S(1)} %add_convert_fusion.1), channel_id=1, source_target_pairs={{0,4},{1,5},{2,6},{3,7},{4,0},{5,1},{6,2},{7,3},{8,12},{9,13},{10,... | collective-permute-start | bytes 258056 | tf_op jit(solution)/shard_map/ppermute | solution.py:581
  88.8 4.6 %collective-permute-start.13 = (bf16[336,128]{1,0:T(8,128)(2,1)S(1)}, bf16[336,128]{1,0:T(8,128)(2,1)S(1)}, u32[]{:S(2)}, u32[]{:S(2)}) collective-permute-start(bf16[336,128]{1,0:T(8,128)(2,1)S(1)} %add_convert_fusion), channel_id=1, source_target_pairs={{0,2},{1,3},{2,0},{3,1},{4,6},{5,7},{6,4},{7,5},{8,10},{9,11},{10,... | collective-permute-start | bytes 258056 | tf_op jit(solution)/shard_map/ppermute | solution.py:586
  93.4 5.5 %collective-permute-start.14 = (bf16[672,128]{1,0:T(8,128)(2,1)S(1)}, bf16[672,128]{1,0:T(8,128)(2,1)S(1)}, u32[]{:S(2)}, u32[]{:S(2)}) collective-permute-start(bf16[672,128]{1,0:T(8,128)(2,1)S(1)} %pad_maximum_fusion.1), channel_id=1, source_target_pairs={{0,1},{1,0},{2,3},{3,2},{4,5},{5,4},{6,7},{7,6},{8,9},{9,8},{10,11... | collective-permute-start | bytes 516104 | tf_op jit(solution)/shard_map/ppermute | solution.py:586
  98.9 1.7 %collective-permute-start.15 = (bf16[1344,128]{1,0:T(8,128)(2,1)S(1)}, bf16[1344,128]{1,0:T(8,128)(2,1)S(1)}, u32[]{:S(2)}, u32[]{:S(2)}) collective-permute-start(bf16[1344,128]{1,0:T(8,128)(2,1)S(1)} %pad_maximum_fusion.own), channel_id=1, source_target_pairs={{0,8},{8,0},{1,9},{9,1},{2,10},{10,2},{3,11},{11,3},{4,12},{12,4},... | collective-permute-start | bytes 1032200 | tf_op jit(solution)/shard_map/ppermute | solution.py:590

commit v3 on v2

--- a/solution.py
+++ b/solution.py
@@ -141,7 +141,7 @@
         hidden[0, r - 1], slope[0, r - 1] = silu_and_slope(sums[r])
 
 
-def join_edge_body(tile, top, bottom, above, below, ht, hb, st, sb, *, count):
+def join_edge_body(tile, top, bottom, below, above, ht, hb, st, sb, *, count):
     for b in range(top.shape[0]):
         got_a, got_b = inside(tile, count, above[b].astype(F32), below[b].astype(F32))
         ht[b], st[b] = silu_and_slope(top[b] + got_a)
@@ -337,11 +337,11 @@
         lane = lane % LANES
         packed[at : at + taps, lane : lane + rest] += extra[:, head:]
     g = group[0]
-    send[...] = packed[pl.ds(pl.multiple_of((1 - g) * half, 8), half), :]
+    send[...] = packed[pl.ds(pl.multiple_of((1 - g) * half, 8), half), :].astype(BF16)
     keep[...] = packed[pl.ds(pl.multiple_of(g * half, 8), half), :]
 
 
-def unpack_body(group, own, got, join, out, packed):
+def unpack_body(group, tile, own, got, join, out, packed, *, near):
     channels = out.shape[2]
     joined = join.shape[3]
     rest = joined % 256
@@ -349,8 +349,14 @@
     taps = 3 * channels
     half = own.shape[0]
     g = group[0]
-    packed[pl.ds(pl.multiple_of(g * half, 8), half), :] = own[...].astype(F32)
-    packed[pl.ds(pl.multiple_of((1 - g) * half, 8), half), :] = got[...].astype(F32)
+    size = half // near
+    me = lax.rem(tile[0], near)
+    for k in range(near):
+        at = (me ^ k) * size
+        for held, x in ((g, own), (1 - g, got)):
+            packed[pl.ds(pl.multiple_of(held * half + at, 8), size), :] = x[
+                k * size : (k + 1) * size, :
+            ].astype(F32)
     tail_at = 3 * taps * (head // LANES)
     tail = jnp.concatenate(
         [
@@ -377,13 +383,6 @@
     below = lax.ppermute(up, axis, [((i + 1) % count, i) for i in range(count)])
     above = lax.ppermute(down, axis, [(i, (i + 1) % count) for i in range(count)])
     return above, below
-
-
-def halves(part, axis, stride):
-    bit = (lax.axis_index(axis) // stride) % 2
-    half = part.shape[0] // 2
-    send = lax.dynamic_slice_in_dim(part, (1 - bit) * half, half, 0)
-    return send, lax.dynamic_slice_in_dim(part, bit * half, half, 0)
 
 
 def on_device(
@@ -509,7 +508,7 @@
     )
     ht, hb, st, sb = run(
         functools.partial(join_edge_body, count=count), "join_edge", (tile_id,),
-        (top, bottom, above, below), [whole(line_f)] * 4,
+        (top, bottom, below, above), [whole(line_f)] * 4,
         [line_b, line_b, line_f, line_f], [whole(line_f)] * 4, (1,), edge_bytes, edge_bytes,
     )
     h_above, h_below = swap_edges(ht, hb, "tile")
@@ -550,10 +549,8 @@
     )
     g_above, g_below = swap_edges(gt, gb, "tile")
 
-    strides = []
-    while 1 << len(strides) < count:
-        strides.append(1 << len(strides))
-    unit = 8 * 2 * count
+    near = 4 if count % 4 == 0 else count
+    unit = 16 * 2 * near
     packed_rows = 3 * taps * (joined + channels) // LANES
     packed_s = struct((pl.cdiv(packed_rows, unit) * unit, LANES), F32)
     half_s = struct((packed_s.shape[0] // 2, LANES), F32)
@@ -568,29 +565,34 @@
         (packed, g_above, g_below, xr, xc, xr, xc),
         [whole(packed_s), whole(line_b), whole(line_b)]
         + [row(xr, 0), row(xc, 0), row(xr, rows - 1), row(xc, rows - 1)],
-        [half_s] * 2, [whole(half_s)] * 2, (1,), 3 * edge_flops, edge_bytes,
+        [struct(half_s.shape, BF16), half_s], [whole(half_s)] * 2, (1,), 3 * edge_flops, edge_bytes,
         (pltpu.VMEM(packed_s.shape, F32),),
     )
-    part = part + lax.ppermute(send, "frame", [(0, 1), (1, 0)])
-    for stride in strides[:-1]:
-        send, keep = halves(part, "tile", stride)
-        pairs = [(i, i ^ stride) for i in range(count)]
-        part = keep + lax.ppermute(send.astype(BF16), "tile", pairs).astype(F32)
-    part = part.astype(BF16)
-    pairs = [(i, i ^ strides[-1]) for i in range(count)]
-    got = lax.ppermute(part, "tile", pairs)
-    part = (part.astype(F32) + got.astype(F32)).astype(BF16)
-    part, recon = lax.optimization_barrier((part, recon))
-    for stride in reversed(strides[:-1]):
-        bit = (lax.axis_index("tile") // stride) % 2
-        got = lax.ppermute(part, "tile", [(i, i ^ stride) for i in range(count)])
-        part = jnp.concatenate(
-            [jnp.where(bit == 0, part, got), jnp.where(bit == 0, got, part)], 0
-        )
+    part = part + lax.ppermute(send, "frame", [(0, 1), (1, 0)]).astype(F32)
+    me = lax.axis_index("tile") % near
+    size = part.shape[0] // near
+
+    def trade(x, mask):
+        return lax.ppermute(x, "tile", [(i, i ^ mask) for i in range(count)])
+
+    def quarter(mask):
+        return lax.dynamic_slice_in_dim(part, (me ^ mask) * size, size, 0)
+
+    gots = [trade(quarter(mask).astype(BF16), mask) for mask in range(1, near)]
+    total = quarter(0)
+    for got in gots:
+        total = total + got.astype(F32)
+    total = total.astype(BF16)
+    mask = near
+    while mask < count:
+        total = (total.astype(F32) + trade(total, mask).astype(F32)).astype(BF16)
+        mask *= 2
+    total, recon = lax.optimization_barrier((total, recon))
+    part = jnp.concatenate([total] + [trade(total, mask) for mask in range(1, near)], 0)
     got = lax.ppermute(part, "frame", [(0, 1), (1, 0)])
     outs = [struct(join_kernel.shape, F32), struct(out_kernel.shape, F32)]
     join_total, out_total = run(
-        unpack_body, "unpack", (group_id,), (part, got), [whole(half_s)] * 2,
+        functools.partial(unpack_body, near=near), "unpack", (group_id, tile_id), (part, got), [whole(half_s)] * 2,
         outs, [whole(x) for x in outs], (1,), 0, 8 * packed_s.size,
         (pltpu.VMEM(packed_s.shape, F32),),
     )

time: 103 us -> 92.6 us (0.90)
  waiting for transfers between devices: 34.6 us -> 22.9 us
  starting transfers between devices: 19.1 us -> 22.3 us
  other arithmetic: 7.14 us -> 5.9 us
    ppermute x6 -> x8, waiting for transfers between devices: 23.4 us -> 9.99 us  [the longest x7 8.38 us: trade(): return lax.ppermute(x, 'tile', [(i, i ^ mask) for i in range(count)])]
    ppermute x6 -> x8, starting transfers between devices: 1.95 us -> 8.29 us  [the longest x7 8.22 us: trade(): return lax.ppermute(x, 'tile', [(i, i ^ mask) for i in range(count)])]
    ppermute x4, starting transfers between devices: 3.06 us -> 0.1 us  [swap_edges(): lax.ppermute(down, axis, [(i, (i + 1) % count) for i in range(count)])]
    ppermute x4, waiting for transfers between devices: 7.56 us -> 9.55 us  [swap_edges(): lax.ppermute(down, axis, [(i, (i + 1) % count) for i in range(count)])]
    add x2 -> x1, other arithmetic: 1.2 us -> 0.06 us  [on_device(): part = part + lax.ppermute(send, 'frame', [(0, 1), (1, 0)]).astype(F32)]
  transfers between devices with their start and end apart: 16 -> 18, of which waited for: 12 -> 12; matrix products, arithmetic and copies ran while one was open for 6% -> 7% of each run, Pallas kernels for 26% -> 29%
where the time goes in v3:
time: 92.6 us; the launch traced here: 92.2 us
  Pallas kernels  36.7 us (40%)
  waiting for transfers between devices  22.9 us (25%)
  starting transfers between devices  22.3 us (24%)
  other arithmetic  5.9 us (6%)
  local copies, waits for them, and re-layouts  3.47 us (4%)
  between operations  0.96 us (1%)
    pallas_call x14, Pallas kernels, run(): call(body, name, flops, nbytes, vmem, grid_spec=pltpu.PrefetchScalarGridS...  36.7 us
    ppermute x4, starting transfers between devices, swap_edges(): below = lax.ppermute(up, axis, [((i + 1) % count, i) for i in range(count)])  13.2 us
    ppermute x4, waiting for transfers between devices, swap_edges(): lax.ppermute(down, axis, [(i, (i + 1) % count) for i in range(count)])  9.55 us
    ppermute x7, waiting for transfers between devices, trade(): return lax.ppermute(x, 'tile', [(i, i ^ mask) for i in range(count)])  8.38 us
    ppermute x7, starting transfers between devices, trade(): return lax.ppermute(x, 'tile', [(i, i ^ mask) for i in range(count)])  8.22 us
    select_n x1, other arithmetic, on_device(): jnp.where(held[:, :, None, None, None], own.reshape(frames, 2, channels,...  3.09 us
    transpose x1, other arithmetic, on_device(): jnp.concatenate([ct[:, None], cm, cb[:, None]], 1).transpose(0, 2, 1, 3)  2.45 us
    unnamed x16, local copies, waits for them, and re-layouts  1.9 us
  transfers between devices with their start and end apart: 18, of which 12 were waited for; matrix products, arithmetic and copies ran while one was open for 7% of the time, Pallas kernels for 29%

profile of v3, /device:TPU:0, one launch (start us, length us, event | category | flops | bytes accessed | tf_op | source)
XLA Modules:
  0.0 92.2 jit_solution(3201591788389709190)
XLA Ops:
  0.7 4.5 %gather_out.1 = bf16[8,96,8,256]{3,2,1,0:T(8,128)(2,1)} custom-call(s32[2,8]{1,0:T(2,128)} %bitcast.39, s32[32]{0:T(128)} %slots.3, s32[1]{0:T(128)} %bitcast.1.group, bf16[16,96,8,256]{3,2,1,0:T(8,128)(2,1)} %refs.3), custom_call_target="tpu_custom_call" | custom-call | bytes 6291456 | tf_op jit(solution)/shard_map/gather_out/pallas_call | solution.py:417
  5.8 2.7 %gather_own.1 = bf16[8,96,8,256]{3,2,1,0:T(8,128)(2,1)S(1)} custom-call(s32[2,8]{1,0:T(2,128)S(1)} %bitcast.40, s32[32]{0:T(128)S(1)} %copy-done.3, s32[1]{0:T(128)} %bitcast.1.group, bf16[16,96,8,256]{3,2,1,0:T(8,128)(2,1)} %refs.3), custom_call_target="tpu_custom_call" | custom-call | bytes 6291456 | tf_op jit(solution)/shard_map/gather_own/pallas_call | solution.py:417
  9.0 1.8 %copy.33 = bf16[4,96,8,256]{3,1,2,0:T(8,128)(2,1)S(1)} copy(bf16[4,96,8,256]{3,2,1,0:T(8,128)(2,1)} %param.9) | data formatting | bytes 3145728 | tf_op args[1]
  11.4 3.1 %copy_select_fusion = bf16[4,2,96,8,256]{4,2,1,3,0:T(8,128)(2,1)S(1)} fusion(bf16[4,2,96,8,256]{4,3,2,1,0:T(8,128)(2,1)} %bitcast.4, bf16[4,2,96,8,256]{4,3,2,1,0:T(8,128)(2,1)S(1)} %bitcast.32, pred[4,2]{1,0:T(4,128)(4,1)S(1)} %copy.23), kind=kLoop, calls=%fused_computation | loop fusion | flops 1572864 | bytes 9437192 | tf_op jit(solution)/shard_map/jit(_where)/select_n | solution.py:468
  15.4 5.9 %collective-permute-start.1 = (bf16[4,96,256]{2,1,0:T(8,128)(2,1)S(1)}, bf16[4,96,256]{2,1,0:T(8,128)(2,1)S(1)}, u32[]{:S(2)}, u32[]{:S(2)}) collective-permute-start(bf16[4,96,256]{2,1,0:T(8,128)(2,1)S(1)} %get-tuple-element.40), channel_id=1, source_target_pairs={{1,0},{2,1},{3,2},{4,3},{5,4},{6,5},{7,6},{0,7},{9,8},{10,9},{11,1... | collective-permute-start | bytes 589832 | tf_op jit(solution)/shard_map/ppermute | solution.py:383
  21.3 5.9 %join_conv.1 = (bf16[4,6,96,256]{3,2,1,0:T(8,128)(2,1)S(1)}, f32[4,6,96,256]{3,2,1,0:T(8,128)S(1)}, f32[4,96,256]{2,1,0:T(8,128)S(1)}, f32[4,96,256]{2,1,0:T(8,128)S(1)}) custom-call(bf16[4,8,192,256]{3,2,1,0:T(8,128)(2,1)S(1)} %bitcast.19, bf16[4,8,96,256]{3,2,1,0:T(8,128)(2,1)S(1)} %bitcast.25, bf16[288,864]{1,0:T(8,128)(2,1)S(1)} %get-tuple-element.36.w), custom_call_target="tpu_custom_call" | custom-call | flops 4076863488 | bytes 7864320 | tf_op jit(solution)/shard_map/join_conv/pallas_call | solution.py:417
  27.2 3.5 %collective-permute-done.2.above = bf16[4,96,256]{2,1,0:T(8,128)(2,1)S(1)} collective-permute-done((bf16[4,96,256]{2,1,0:T(8,128)(2,1)S(1)}, bf16[4,96,256]{2,1,0:T(8,128)(2,1)S(1)}, u32[]{:S(2)}, u32[]{:S(2)}) %collective-permute-start.2) | collective-permute-done | bytes 196640 | tf_op jit(solution)/shard_map/ppermute | solution.py:384
  30.9 2.1 %collective-permute-start.4 = (bf16[4,96,256]{2,1,0:T(8,128)(2,1)S(1)}, bf16[4,96,256]{2,1,0:T(8,128)(2,1)S(1)}, u32[]{:S(2)}, u32[]{:S(2)}) collective-permute-start(bf16[4,96,256]{2,1,0:T(8,128)(2,1)S(1)} %get-tuple-element.42.ht), channel_id=1, source_target_pairs={{1,0},{2,1},{3,2},{4,3},{5,4},{6,5},{7,6},{0,7},{9,8},{10,9},{11,1... | collective-permute-start | bytes 589832 | tf_op jit(solution)/shard_map/ppermute | solution.py:383
  33.0 3.9 %out_conv.1 = (bf16[4,6,96,256]{3,2,1,0:T(8,128)(2,1)S(1)}, bf16[4,6,96,256]{3,2,1,0:T(8,128)(2,1)S(1)}, f32[4,96,256]{2,1,0:T(8,128)S(1)}, f32[4,96,256]{2,1,0:T(8,128)S(1)}) custom-call(s32[8]{0:T(128)S(1)} %copy-done.4, f32[32]{0:T(128)S(1)} %copy-done.5, s32[1]{0:T(128)} %bitcast.1.group, bf16[4,6,96,256]{3,2,1,0:T(8,128)(2,1)S(1)} %get-tuple-element.37.hm, ...), custom_call_target="tpu_custom_call" | custom-call | flops 1358954496 | bytes 7864320 | tf_op jit(solution)/shard_map/out_conv/pallas_call | solution.py:417
  37.0 4.4 %collective-permute-done.3.above = bf16[4,96,256]{2,1,0:T(8,128)(2,1)S(1)} collective-permute-done((bf16[4,96,256]{2,1,0:T(8,128)(2,1)S(1)}, bf16[4,96,256]{2,1,0:T(8,128)(2,1)S(1)}, u32[]{:S(2)}, u32[]{:S(2)}) %collective-permute-start.3) | collective-permute-done | bytes 196640 | tf_op jit(solution)/shard_map/ppermute | solution.py:384
  42.6 2.0 %collective-permute-start.6 = (bf16[4,96,256]{2,1,0:T(8,128)(2,1)S(1)}, bf16[4,96,256]{2,1,0:T(8,128)(2,1)S(1)}, u32[]{:S(2)}, u32[]{:S(2)}) collective-permute-start(bf16[4,96,256]{2,1,0:T(8,128)(2,1)S(1)} %get-tuple-element.48.rt), channel_id=1, source_target_pairs={{1,0},{2,1},{3,2},{4,3},{5,4},{6,5},{7,6},{0,7},{9,8},{10,9},{11,1... | collective-permute-start | bytes 589832 | tf_op jit(solution)/shard_map/ppermute | solution.py:383
  44.7 3.7 %out_grad.1.og = f32[288,288]{1,0:T(8,128)S(1)} custom-call(bf16[4,6,96,256]{3,2,1,0:T(8,128)(2,1)S(1)} %get-tuple-element.37.hm, bf16[4,96,256]{2,1,0:T(8,128)(2,1)S(1)} %get-tuple-element.42.ht, bf16[4,96,256]{2,1,0:T(8,128)(2,1)S(1)} %get-tuple-element.43.hb, bf16[4,6,96,256]{3,2,1,0:T(8,128)(2,1)S(1)} %get-tuple-element.45.rm, ...), custom_call_target="tpu_custom_call" | custom-call | flops 1358954496 | bytes 7864320 | tf_op jit(solution)/shard_map/out_grad/pallas_call | solution.py:417
  48.3 3.4 %back_conv.1 = (bf16[4,6,96,256]{3,2,1,0:T(8,128)(2,1)S(1)}, f32[4,96,256]{2,1,0:T(8,128)S(1)}, f32[4,96,256]{2,1,0:T(8,128)S(1)}) custom-call(bf16[4,6,96,256]{3,2,1,0:T(8,128)(2,1)S(1)} %get-tuple-element.45.rm, bf16[4,96,256]{2,1,0:T(8,128)(2,1)S(1)} %get-tuple-element.48.rt, bf16[4,96,256]{2,1,0:T(8,128)(2,1)S(1)} %get-tuple-element.49.rb, ...), custom_call_target="tpu_custom_call" | custom-call | flops 1358954496 | bytes 7864320 | tf_op jit(solution)/shard_map/back_conv/pallas_call | solution.py:417
  53.8 3.3 %collective-permute-start.8 = (bf16[4,96,256]{2,1,0:T(8,128)(2,1)S(1)}, bf16[4,96,256]{2,1,0:T(8,128)(2,1)S(1)}, u32[]{:S(2)}, u32[]{:S(2)}) collective-permute-start(bf16[4,96,256]{2,1,0:T(8,128)(2,1)S(1)} %get-tuple-element.58.gt), channel_id=1, source_target_pairs={{1,0},{2,1},{3,2},{4,3},{5,4},{6,5},{7,6},{0,7},{9,8},{10,9},{11,1... | collective-permute-start | bytes 589832 | tf_op jit(solution)/shard_map/ppermute | solution.py:383
  57.1 6.7 %grads.1.packed_in = f32[2688,128]{1,0:T(8,128)S(1)} custom-call(s32[1]{0:T(128)} %bitcast.tile, bf16[4,6,96,256]{3,2,1,0:T(8,128)(2,1)S(1)} %get-tuple-element.52.gm, bf16[4,96,256]{2,1,0:T(8,128)(2,1)S(1)} %get-tuple-element.58.gt, bf16[4,96,256]{2,1,0:T(8,128)(2,1)S(1)} %get-tuple-element.59.gb, bf16[4,8,192,256]{3,2,1,0:T(8,128)(2,1)S(1)} %bitcast.20, ...), custom_call_target="tpu_custom_call" | custom-call | flops 4076863488 | bytes 15728640 | tf_op jit(solution)/shard_map/grads/pallas_call | solution.py:417
  63.8 1.7 %collective-permute-done.7.above = bf16[4,96,256]{2,1,0:T(8,128)(2,1)S(1)} collective-permute-done((bf16[4,96,256]{2,1,0:T(8,128)(2,1)S(1)}, bf16[4,96,256]{2,1,0:T(8,128)(2,1)S(1)}, u32[]{:S(2)}, u32[]{:S(2)}) %collective-permute-start.7) | collective-permute-done | bytes 196640 | tf_op jit(solution)/shard_map/ppermute | solution.py:384
  66.6 1.6 %collective-permute-done.9 = bf16[1344,128]{1,0:T(8,128)(2,1)S(1)} collective-permute-done((bf16[1344,128]{1,0:T(8,128)(2,1)S(1)}, bf16[1344,128]{1,0:T(8,128)(2,1)S(1)}, u32[]{:S(2)}, u32[]{:S(2)}) %collective-permute-start.9) | collective-permute-done | bytes 344096 | tf_op jit(solution)/shard_map/ppermute | solution.py:571
  73.3 1.5 %collective-permute-done.10 = bf16[336,128]{1,0:T(8,128)(2,1)S(1)} collective-permute-done((bf16[336,128]{1,0:T(8,128)(2,1)S(1)}, bf16[336,128]{1,0:T(8,128)(2,1)S(1)}, u32[]{:S(2)}, u32[]{:S(2)}) %collective-permute-start.10) | collective-permute-done | bytes 86048 | tf_op jit(solution)/shard_map/ppermute | solution.py:576
  77.2 2.5 %maximum_bitcast_fusion = bf16[4,96,8,256]{3,2,1,0:T(8,128)(2,1)} fusion(bf16[4,1,96,256]{3,1,2,0:T(2,128)(2,1)S(1)} %copy.29, bf16[4,6,96,256]{3,1,2,0:T(8,128)(2,1)S(1)} %copy.28, bf16[4,1,96,256]{3,1,2,0:T(2,128)(2,1)S(1)} %copy.27), kind=kLoop, calls=%fused_computation.1 | loop fusion | flops 4718592 | bytes 3145728 | tf_op jit(solution)/shard_map/transpose | solution.py:543
  79.6 2.8 %collective-permute-done.13 = bf16[336,128]{1,0:T(8,128)(2,1)S(1)} collective-permute-done((bf16[336,128]{1,0:T(8,128)(2,1)S(1)}, bf16[336,128]{1,0:T(8,128)(2,1)S(1)}, u32[]{:S(2)}, u32[]{:S(2)}) %collective-permute-start.13) | collective-permute-done | bytes 86048 | tf_op jit(solution)/shard_map/ppermute | solution.py:576
  84.0 2.0 %collective-permute-start.14 = (bf16[336,128]{1,0:T(8,128)(2,1)S(1)}, bf16[336,128]{1,0:T(8,128)(2,1)S(1)}, u32[]{:S(2)}, u32[]{:S(2)}) collective-permute-start(bf16[336,128]{1,0:T(8,128)(2,1)S(1)} %add_convert_fusion), channel_id=1, source_target_pairs={{0,1},{1,0},{2,3},{3,2},{4,5},{5,4},{6,7},{7,6},{8,9},{9,8},{10,11... | collective-permute-start | bytes 258056 | tf_op jit(solution)/shard_map/ppermute | solution.py:576
  86.0 2.8 %collective-permute-done.14 = bf16[336,128]{1,0:T(8,128)(2,1)S(1)} collective-permute-done((bf16[336,128]{1,0:T(8,128)(2,1)S(1)}, bf16[336,128]{1,0:T(8,128)(2,1)S(1)}, u32[]{:S(2)}, u32[]{:S(2)}) %collective-permute-start.14) | collective-permute-done | bytes 86048 | tf_op jit(solution)/shard_map/ppermute | solution.py:576
  89.0 1.6 %collective-permute-done.17.got = bf16[1344,128]{1,0:T(8,128)(2,1)S(1)} collective-permute-done((bf16[1344,128]{1,0:T(8,128)(2,1)S(1)}, bf16[1344,128]{1,0:T(8,128)(2,1)S(1)}, u32[]{:S(2)}, u32[]{:S(2)}) %collective-permute-start.17) | collective-permute-done | bytes 344096 | tf_op jit(solution)/shard_map/ppermute | solution.py:592
  90.6 1.6 %unpack.1 = (f32[3,3,96,288]{3,2,1,0:T(8,128)}, f32[3,3,96,96]{3,2,1,0:T(8,128)}) custom-call(s32[1]{0:T(128)} %bitcast.1.group, s32[1]{0:T(128)} %bitcast.tile, bf16[1344,128]{1,0:T(8,128)(2,1)S(1)} %constant_dynamic-update-slice_fusion.own, bf16[1344,128]{1,0:T(8,128)(2,1)S(1)} %collective-permute-done.17.got), custom_call_target="tpu_custom_call" | custom-call | bytes 2752512 | tf_op jit(solution)/shard_map/unpack/pallas_call | solution.py:417
  (56 shorter events, 16.5 us)
Async XLA Ops:
  0.6 5.2 %copy-start.2 = (s32[8,2]{0,1:T(2,128)S(1)}, s32[8,2]{0,1:T(2,128)}, u32[]{:S(2)}) copy-start(s32[8,2]{0,1:T(2,128)} %param.10) | copy-start | bytes 196
  0.6 5.2 %copy-start.3 = (s32[32]{0:T(128)S(1)}, s32[32]{0:T(128)}, u32[]{:S(2)}) copy-start(s32[32]{0:T(128)} %slots.3) | copy-start | bytes 388
  5.2 6.3 %collective-permute-start = (bf16[8,96,8,256]{3,2,1,0:T(8,128)(2,1)}, bf16[8,96,8,256]{3,2,1,0:T(8,128)(2,1)}, u32[]{:S(2)}, u32[]{:S(2)}) collective-permute-start(bf16[8,96,8,256]{3,2,1,0:T(8,128)(2,1)} %gather_out.1), channel_id=1, source_target_pairs={{0,8},{8,0},{1,9},{9,1},{2,10},{10,2},{3,11},{11,3},{4,12},{12,4},... | collective-permute-start | bytes 9437192 | tf_op jit(solution)/shard_map/ppermute | solution.py:462
  8.5 2.3 %copy-start.1 = (bf16[3,3,96,96]{3,2,1,0:T(8,128)(2,1)S(1)}, bf16[3,3,96,96]{3,2,1,0:T(8,128)(2,1)}, u32[]{:S(2)}) copy-start(bf16[3,3,96,96]{3,2,1,0:T(8,128)(2,1)} %param.15) | copy-start | bytes 497668
  9.0 1.9 %copy-start = (bf16[3,3,96,288]{3,2,1,0:T(8,128)(2,1)S(1)}, bf16[3,3,96,288]{3,2,1,0:T(8,128)(2,1)}, u32[]{:S(2)}) copy-start(bf16[3,3,96,288]{3,2,1,0:T(8,128)(2,1)} %param.14) | copy-start | bytes 1492996
  15.4 11.8 %collective-permute-start.1 = (bf16[4,96,256]{2,1,0:T(8,128)(2,1)S(1)}, bf16[4,96,256]{2,1,0:T(8,128)(2,1)S(1)}, u32[]{:S(2)}, u32[]{:S(2)}) collective-permute-start(bf16[4,96,256]{2,1,0:T(8,128)(2,1)S(1)} %get-tuple-element.40), channel_id=1, source_target_pairs={{1,0},{2,1},{3,2},{4,3},{5,4},{6,5},{7,6},{0,7},{9,8},{10,9},{11,1... | collective-permute-start | bytes 589832 | tf_op jit(solution)/shard_map/ppermute | solution.py:383
  21.3 9.4 %collective-permute-start.2 = (bf16[4,96,256]{2,1,0:T(8,128)(2,1)S(1)}, bf16[4,96,256]{2,1,0:T(8,128)(2,1)S(1)}, u32[]{:S(2)}, u32[]{:S(2)}) collective-permute-start(bf16[4,96,256]{2,1,0:T(8,128)(2,1)S(1)} %get-tuple-element.41), channel_id=1, source_target_pairs={{0,1},{1,2},{2,3},{3,4},{4,5},{5,6},{6,7},{7,0},{8,9},{9,10},{10,1... | collective-permute-start | bytes 589832 | tf_op jit(solution)/shard_map/ppermute | solution.py:384
  21.3 11.7 %copy-start.4 = (s32[8]{0:T(128)S(1)}, s32[8]{0:T(128)}, u32[]{:S(2)}) copy-start(s32[8]{0:T(128)} %numbers.3) | copy-start | bytes 100
  21.3 11.7 %copy-start.5 = (f32[32]{0:T(128)S(1)}, f32[32]{0:T(128)}, u32[]{:S(2)}) copy-start(f32[32]{0:T(128)} %rates.3) | copy-start | bytes 388
  30.9 6.0 %collective-permute-start.4 = (bf16[4,96,256]{2,1,0:T(8,128)(2,1)S(1)}, bf16[4,96,256]{2,1,0:T(8,128)(2,1)S(1)}, u32[]{:S(2)}, u32[]{:S(2)}) collective-permute-start(bf16[4,96,256]{2,1,0:T(8,128)(2,1)S(1)} %get-tuple-element.42.ht), channel_id=1, source_target_pairs={{1,0},{2,1},{3,2},{4,3},{5,4},{6,5},{7,6},{0,7},{9,8},{10,9},{11,1... | collective-permute-start | bytes 589832 | tf_op jit(solution)/shard_map/ppermute | solution.py:383
  33.0 8.4 %collective-permute-start.3 = (bf16[4,96,256]{2,1,0:T(8,128)(2,1)S(1)}, bf16[4,96,256]{2,1,0:T(8,128)(2,1)S(1)}, u32[]{:S(2)}, u32[]{:S(2)}) collective-permute-start(bf16[4,96,256]{2,1,0:T(8,128)(2,1)S(1)} %get-tuple-element.43.hb), channel_id=1, source_target_pairs={{0,1},{1,2},{2,3},{3,4},{4,5},{5,6},{6,7},{7,0},{8,9},{9,10},{10,1... | collective-permute-start | bytes 589832 | tf_op jit(solution)/shard_map/ppermute | solution.py:384
  42.6 10.6 %collective-permute-start.6 = (bf16[4,96,256]{2,1,0:T(8,128)(2,1)S(1)}, bf16[4,96,256]{2,1,0:T(8,128)(2,1)S(1)}, u32[]{:S(2)}, u32[]{:S(2)}) collective-permute-start(bf16[4,96,256]{2,1,0:T(8,128)(2,1)S(1)} %get-tuple-element.48.rt), channel_id=1, source_target_pairs={{1,0},{2,1},{3,2},{4,3},{5,4},{6,5},{7,6},{0,7},{9,8},{10,9},{11,1... | collective-permute-start | bytes 589832 | tf_op jit(solution)/shard_map/ppermute | solution.py:383
  44.6 8.6 %collective-permute-start.5 = (bf16[4,96,256]{2,1,0:T(8,128)(2,1)S(1)}, bf16[4,96,256]{2,1,0:T(8,128)(2,1)S(1)}, u32[]{:S(2)}, u32[]{:S(2)}) collective-permute-start(bf16[4,96,256]{2,1,0:T(8,128)(2,1)S(1)} %get-tuple-element.49.rb), channel_id=1, source_target_pairs={{0,1},{1,2},{2,3},{3,4},{4,5},{5,6},{6,7},{7,0},{8,9},{9,10},{10,1... | collective-permute-start | bytes 589832 | tf_op jit(solution)/shard_map/ppermute | solution.py:384
  53.8 10.0 %collective-permute-start.8 = (bf16[4,96,256]{2,1,0:T(8,128)(2,1)S(1)}, bf16[4,96,256]{2,1,0:T(8,128)(2,1)S(1)}, u32[]{:S(2)}, u32[]{:S(2)}) collective-permute-start(bf16[4,96,256]{2,1,0:T(8,128)(2,1)S(1)} %get-tuple-element.58.gt), channel_id=1, source_target_pairs={{1,0},{2,1},{3,2},{4,3},{5,4},{6,5},{7,6},{0,7},{9,8},{10,9},{11,1... | collective-permute-start | bytes 589832 | tf_op jit(solution)/shard_map/ppermute | solution.py:383
  57.1 8.4 %collective-permute-start.7 = (bf16[4,96,256]{2,1,0:T(8,128)(2,1)S(1)}, bf16[4,96,256]{2,1,0:T(8,128)(2,1)S(1)}, u32[]{:S(2)}, u32[]{:S(2)}) collective-permute-start(bf16[4,96,256]{2,1,0:T(8,128)(2,1)S(1)} %get-tuple-element.59.gb), channel_id=1, source_target_pairs={{0,1},{1,2},{2,3},{3,4},{4,5},{5,6},{6,7},{7,0},{8,9},{9,10},{10,1... | collective-permute-start | bytes 589832 | tf_op jit(solution)/shard_map/ppermute | solution.py:384
  66.5 1.7 %collective-permute-start.9 = (bf16[1344,128]{1,0:T(8,128)(2,1)S(1)}, bf16[1344,128]{1,0:T(8,128)(2,1)S(1)}, u32[]{:S(2)}, u32[]{:S(2)}) collective-permute-start(bf16[1344,128]{1,0:T(8,128)(2,1)S(1)} %get-tuple-element.61), channel_id=1, source_target_pairs={{0,8},{8,0},{1,9},{9,1},{2,10},{10,2},{3,11},{11,3},{4,12},{12,4},... | collective-permute-start | bytes 1032200 | tf_op jit(solution)/shard_map/ppermute | solution.py:571
  68.4 6.4 %collective-permute-start.10 = (bf16[336,128]{1,0:T(8,128)(2,1)S(1)}, bf16[336,128]{1,0:T(8,128)(2,1)S(1)}, u32[]{:S(2)}, u32[]{:S(2)}) collective-permute-start(bf16[336,128]{1,0:T(8,128)(2,1)S(1)} %get-tuple-element.69), channel_id=1, source_target_pairs={{0,1},{1,0},{2,3},{3,2},{4,5},{5,4},{6,7},{7,6},{8,9},{9,8},{10,11... | collective-permute-start | bytes 258056 | tf_op jit(solution)/shard_map/ppermute | solution.py:576
  69.1 5.8 %collective-permute-start.12 = (bf16[336,128]{1,0:T(8,128)(2,1)S(1)}, bf16[336,128]{1,0:T(8,128)(2,1)S(1)}, u32[]{:S(2)}, u32[]{:S(2)}) collective-permute-start(bf16[336,128]{1,0:T(8,128)(2,1)S(1)} %get-tuple-element.70), channel_id=1, source_target_pairs={{0,3},{1,2},{2,1},{3,0},{4,7},{5,6},{6,5},{7,4},{8,11},{9,10},{10,... | collective-permute-start | bytes 258056 | tf_op jit(solution)/shard_map/ppermute | solution.py:576
  70.5 5.5 %collective-permute-start.11 = (bf16[336,128]{1,0:T(8,128)(2,1)S(1)}, bf16[336,128]{1,0:T(8,128)(2,1)S(1)}, u32[]{:S(2)}, u32[]{:S(2)}) collective-permute-start(bf16[336,128]{1,0:T(8,128)(2,1)S(1)} %get-tuple-element.71), channel_id=1, source_target_pairs={{0,2},{1,3},{2,0},{3,1},{4,6},{5,7},{6,4},{7,5},{8,10},{9,11},{10,... | collective-permute-start | bytes 258056 | tf_op jit(solution)/shard_map/ppermute | solution.py:576
  76.1 6.4 %collective-permute-start.13 = (bf16[336,128]{1,0:T(8,128)(2,1)S(1)}, bf16[336,128]{1,0:T(8,128)(2,1)S(1)}, u32[]{:S(2)}, u32[]{:S(2)}) collective-permute-start(bf16[336,128]{1,0:T(8,128)(2,1)S(1)} %add_convert_fusion.1), channel_id=1, source_target_pairs={{0,4},{1,5},{2,6},{3,7},{4,0},{5,1},{6,2},{7,3},{8,12},{9,13},{10,... | collective-permute-start | bytes 258056 | tf_op jit(solution)/shard_map/ppermute | solution.py:576
  82.5 6.4 %collective-permute-start.16 = (bf16[336,128]{1,0:T(8,128)(2,1)S(1)}, bf16[336,128]{1,0:T(8,128)(2,1)S(1)}, u32[]{:S(2)}, u32[]{:S(2)}) collective-permute-start(bf16[336,128]{1,0:T(8,128)(2,1)S(1)} %add_convert_fusion), channel_id=1, source_target_pairs={{0,3},{1,2},{2,1},{3,0},{4,7},{5,6},{6,5},{7,4},{8,11},{9,10},{10,... | collective-permute-start | bytes 258056 | tf_op jit(solution)/shard_map/ppermute | solution.py:576
  83.6 5.3 %collective-permute-start.15 = (bf16[336,128]{1,0:T(8,128)(2,1)S(1)}, bf16[336,128]{1,0:T(8,128)(2,1)S(1)}, u32[]{:S(2)}, u32[]{:S(2)}) collective-permute-start(bf16[336,128]{1,0:T(8,128)(2,1)S(1)} %add_convert_fusion), channel_id=1, source_target_pairs={{0,2},{1,3},{2,0},{3,1},{4,6},{5,7},{6,4},{7,5},{8,10},{9,11},{10,... | collective-permute-start | bytes 258056 | tf_op jit(solution)/shard_map/ppermute | solution.py:576
  84.0 4.8 %collective-permute-start.14 = (bf16[336,128]{1,0:T(8,128)(2,1)S(1)}, bf16[336,128]{1,0:T(8,128)(2,1)S(1)}, u32[]{:S(2)}, u32[]{:S(2)}) collective-permute-start(bf16[336,128]{1,0:T(8,128)(2,1)S(1)} %add_convert_fusion), channel_id=1, source_target_pairs={{0,1},{1,0},{2,3},{3,2},{4,5},{5,4},{6,7},{7,6},{8,9},{9,8},{10,11... | collective-permute-start | bytes 258056 | tf_op jit(solution)/shard_map/ppermute | solution.py:576
  88.9 1.7 %collective-permute-start.17 = (bf16[1344,128]{1,0:T(8,128)(2,1)S(1)}, bf16[1344,128]{1,0:T(8,128)(2,1)S(1)}, u32[]{:S(2)}, u32[]{:S(2)}) collective-permute-start(bf16[1344,128]{1,0:T(8,128)(2,1)S(1)} %constant_dynamic-update-slice_fusion.own), channel_id=1, source_target_pairs={{0,8},{8,0},{1,9},{9,1},{2,10},{10,2},{3,11},{11,3},{4,12},{12,4},... | collective-permute-start | bytes 1032200 | tf_op jit(solution)/shard_map/ppermute | solution.py:592

commit v4 on v3

--- a/solution.py
+++ b/solution.py
@@ -157,21 +157,22 @@
 
 
 def output_body(
-    numbers, rates, group, hm, ht, hb, xc, w, recon, residual, top, bottom, *, cells, frames
+    numbers, rates, group, hm, ht, hb, xc, w, recon, residual, top, bottom, scales,
+    *, cells, frames
 ):
     hidden = column(ht, hm, hb)
     sums = conv_rows(w[...], hidden, hm.shape[3])
     scale = frame_scale(numbers, rates, group, cells, pl.program_id(0), frames)
     top[0] = sums[0]
     bottom[0] = sums[-1]
+    scales[0] = jnp.full(scales.shape[1:], scale, F32)
     for r in range(1, len(sums) - 1):
         recon[0, r - 1] = sums[r].astype(BF16)
         residual[0, r - 1] = ((sums[r] - xc[0, r].astype(F32)) * scale).astype(BF16)
 
 
 def output_edge_body(
-    numbers, rates, group, tile, top, bottom, above, below, xc0, xc1, w, ct, cb, rt, rb,
-    *, cells, frames, count
+    tile, top, bottom, above, below, xc0, xc1, scales, w, ct, cb, rt, rb, *, count
 ):
     frames = top.shape[0]
     got = inside(tile, count, above[...], below[...])
@@ -180,10 +181,9 @@
         (got[1], 2, bottom, xc1, cb, rb),
     ):
         for b, x in enumerate(edge_sums(w, p, [g[b] for b in range(frames)])):
-            scale = frame_scale(numbers, rates, group, cells, b, frames)
             total = part[b] + x
             c[b] = total.astype(BF16)
-            r[b] = ((total - xc[b, 0].astype(F32)) * scale).astype(BF16)
+            r[b] = ((total - xc[b, 0].astype(F32)) * scales[b, :1, :]).astype(BF16)
 
 
 def slope_body(rm, rt, rb, slope, w, grad, top, bottom):
@@ -341,21 +341,22 @@
     keep[...] = packed[pl.ds(pl.multiple_of(g * half, 8), half), :]
 
 
-def unpack_body(group, tile, own, got, join, out, packed, *, near):
+def unpack_body(group, tile, *refs, near):
+    own, got, (join, out, packed) = refs[:near], refs[near : 2 * near], refs[2 * near :]
     channels = out.shape[2]
     joined = join.shape[3]
     rest = joined % 256
     head = joined - rest
     taps = 3 * channels
-    half = own.shape[0]
+    size = own[0].shape[0]
+    half = near * size
     g = group[0]
-    size = half // near
     me = lax.rem(tile[0], near)
     for k in range(near):
         at = (me ^ k) * size
         for held, x in ((g, own), (1 - g, got)):
-            packed[pl.ds(pl.multiple_of(held * half + at, 8), size), :] = x[
-                k * size : (k + 1) * size, :
+            packed[pl.ds(pl.multiple_of(held * half + at, 8), size), :] = x[k][
+                ...
             ].astype(F32)
     tail_at = 3 * taps * (head // LANES)
     tail = jnp.concatenate(
@@ -514,16 +515,16 @@
     h_above, h_below = swap_edges(ht, hb, "tile")
 
     rated = (frame_numbers, rate_weights, group_id)
-    outs = [mid_b, mid_b, line_f, line_f]
-    cm, rm, top, bottom = run(
+    outs = [mid_b, mid_b, line_f, line_f, struct((frames, 8, width), F32)]
+    cm, rm, top, bottom, scales = run(
         functools.partial(output_body, cells=cells, frames=frames), "out_conv", rated,
         (hm, ht, hb, xc, w2), [each(x) for x in (hm, ht, hb, xc)] + [whole(w2)],
         outs, [each(x) for x in outs], (frames,), conv_flops * channels, mid_bytes,
     )
     ct, cb, rt, rb = run(
-        functools.partial(output_edge_body, cells=cells, frames=frames, count=count),
-        "out_edge", rated + (tile_id,), (top, bottom, h_above, h_below, xc, xc, ok),
-        [whole(line_f)] * 4 + [row(xc, 0), row(xc, rows - 1), whole(ok)],
+        functools.partial(output_edge_body, count=count),
+        "out_edge", (tile_id,), (top, bottom, h_above, h_below, xc, xc, scales, ok),
+        [whole(line_f)] * 4 + [row(xc, 0), row(xc, rows - 1), whole(scales), whole(ok)],
         [line_b] * 4, [whole(line_b)] * 4, (1,), edge_flops, edge_bytes,
     )
     r_above, r_below = swap_edges(rt, rb, "tile")
@@ -588,11 +589,12 @@
         total = (total.astype(F32) + trade(total, mask).astype(F32)).astype(BF16)
         mask *= 2
     total, recon = lax.optimization_barrier((total, recon))
-    part = jnp.concatenate([total] + [trade(total, mask) for mask in range(1, near)], 0)
-    got = lax.ppermute(part, "frame", [(0, 1), (1, 0)])
+    pieces = [total] + [trade(total, mask) for mask in range(1, near)]
+    others = [lax.ppermute(x, "frame", [(0, 1), (1, 0)]) for x in pieces]
     outs = [struct(join_kernel.shape, F32), struct(out_kernel.shape, F32)]
     join_total, out_total = run(
-        functools.partial(unpack_body, near=near), "unpack", (group_id, tile_id), (part, got), [whole(half_s)] * 2,
+        functools.partial(unpack_body, near=near), "unpack", (group_id, tile_id), (*pieces, *others),
+        [whole(x) for x in pieces + others],
         outs, [whole(x) for x in outs], (1,), 0, 8 * packed_s.size,
         (pltpu.VMEM(packed_s.shape, F32),),
     )

time: 92.6 us -> 91.6 us (0.989)
    unnamed x16 -> x13, local copies, waits for them, and re-layouts: 1.9 us -> 1.87 us
  transfers between devices with their start and end apart: 18 -> 21, of which waited for: 12 -> 16; matrix products, arithmetic and copies ran while one was open for 7% -> 7% of each run, Pallas kernels for 29% -> 29%
where the time goes in v4:
time: 91.6 us; the launch traced here: 91 us
  Pallas kernels  36.1 us (39%)
  starting transfers between devices  22.6 us (25%)
  waiting for transfers between devices  22.1 us (24%)
  other arithmetic  5.9 us (6%)
  local copies, waits for them, and re-layouts  3.42 us (4%)
  between operations  0.93 us (1%)
    pallas_call x14, Pallas kernels, run(): call(body, name, flops, nbytes, vmem, grid_spec=pltpu.PrefetchScalarGridS...  36.1 us
    ppermute x4, starting transfers between devices, swap_edges(): below = lax.ppermute(up, axis, [((i + 1) % count, i) for i in range(count)])  13.1 us
    ppermute x4, waiting for transfers between devices, swap_edges(): lax.ppermute(down, axis, [(i, (i + 1) % count) for i in range(count)])  9.53 us
    ppermute x7, starting transfers between devices, trade(): return lax.ppermute(x, 'tile', [(i, i ^ mask) for i in range(count)])  8.22 us
    ppermute x7, waiting for transfers between devices, trade(): return lax.ppermute(x, 'tile', [(i, i ^ mask) for i in range(count)])  8.03 us
    select_n x1, other arithmetic, on_device(): jnp.where(held[:, :, None, None, None], own.reshape(frames, 2, channels,...  3.09 us
    transpose x1, other arithmetic, on_device(): jnp.concatenate([ct[:, None], cm, cb[:, None]], 1).transpose(0, 2, 1, 3)  2.45 us
    unnamed x13, local copies, waits for them, and re-layouts  1.87 us
  transfers between devices with their start and end apart: 21, of which 16 were waited for; matrix products, arithmetic and copies ran while one was open for 7% of the time, Pallas kernels for 29%

profile of v4, /device:TPU:0, one launch (start us, length us, event | category | flops | bytes accessed | tf_op | source)
XLA Modules:
  0.0 91.0 jit_solution(17994821140430089425)
XLA Ops:
  0.7 4.3 %gather_out.1 = bf16[8,96,8,256]{3,2,1,0:T(8,128)(2,1)} custom-call(s32[2,8]{1,0:T(2,128)} %bitcast.39, s32[32]{0:T(128)} %slots.3, s32[1]{0:T(128)} %bitcast.1.group, bf16[16,96,8,256]{3,2,1,0:T(8,128)(2,1)} %refs.3), custom_call_target="tpu_custom_call" | custom-call | bytes 6291456 | tf_op jit(solution)/shard_map/gather_out/pallas_call | solution.py:418
  5.7 2.7 %gather_own.1 = bf16[8,96,8,256]{3,2,1,0:T(8,128)(2,1)S(1)} custom-call(s32[2,8]{1,0:T(2,128)S(1)} %bitcast.40, s32[32]{0:T(128)S(1)} %copy-done.3, s32[1]{0:T(128)} %bitcast.1.group, bf16[16,96,8,256]{3,2,1,0:T(8,128)(2,1)} %refs.3), custom_call_target="tpu_custom_call" | custom-call | bytes 6291456 | tf_op jit(solution)/shard_map/gather_own/pallas_call | solution.py:418
  8.9 1.8 %copy.33 = bf16[4,96,8,256]{3,1,2,0:T(8,128)(2,1)S(1)} copy(bf16[4,96,8,256]{3,2,1,0:T(8,128)(2,1)} %param.9) | data formatting | bytes 3145728 | tf_op args[1]
  11.3 3.1 %copy_select_fusion = bf16[4,2,96,8,256]{4,2,1,3,0:T(8,128)(2,1)S(1)} fusion(bf16[4,2,96,8,256]{4,3,2,1,0:T(8,128)(2,1)} %bitcast.4, bf16[4,2,96,8,256]{4,3,2,1,0:T(8,128)(2,1)S(1)} %bitcast.32, pred[4,2]{1,0:T(4,128)(4,1)S(1)} %copy.23), kind=kLoop, calls=%fused_computation | loop fusion | flops 1572864 | bytes 9437192 | tf_op jit(solution)/shard_map/jit(_where)/select_n | solution.py:469
  15.3 5.8 %collective-permute-start.1 = (bf16[4,96,256]{2,1,0:T(8,128)(2,1)S(1)}, bf16[4,96,256]{2,1,0:T(8,128)(2,1)S(1)}, u32[]{:S(2)}, u32[]{:S(2)}) collective-permute-start(bf16[4,96,256]{2,1,0:T(8,128)(2,1)S(1)} %get-tuple-element.41), channel_id=1, source_target_pairs={{1,0},{2,1},{3,2},{4,3},{5,4},{6,5},{7,6},{0,7},{9,8},{10,9},{11,1... | collective-permute-start | bytes 589832 | tf_op jit(solution)/shard_map/ppermute | solution.py:384
  21.1 5.9 %join_conv.1 = (bf16[4,6,96,256]{3,2,1,0:T(8,128)(2,1)S(1)}, f32[4,6,96,256]{3,2,1,0:T(8,128)S(1)}, f32[4,96,256]{2,1,0:T(8,128)S(1)}, f32[4,96,256]{2,1,0:T(8,128)S(1)}) custom-call(bf16[4,8,192,256]{3,2,1,0:T(8,128)(2,1)S(1)} %bitcast.19, bf16[4,8,96,256]{3,2,1,0:T(8,128)(2,1)S(1)} %bitcast.25, bf16[288,864]{1,0:T(8,128)(2,1)S(1)} %get-tuple-element.37.w), custom_call_target="tpu_custom_call" | custom-call | flops 4076863488 | bytes 7864320 | tf_op jit(solution)/shard_map/join_conv/pallas_call | solution.py:418
  27.0 3.5 %collective-permute-done.2.above = bf16[4,96,256]{2,1,0:T(8,128)(2,1)S(1)} collective-permute-done((bf16[4,96,256]{2,1,0:T(8,128)(2,1)S(1)}, bf16[4,96,256]{2,1,0:T(8,128)(2,1)S(1)}, u32[]{:S(2)}, u32[]{:S(2)}) %collective-permute-start.2) | collective-permute-done | bytes 196640 | tf_op jit(solution)/shard_map/ppermute | solution.py:385
  30.8 2.1 %collective-permute-start.4 = (bf16[4,96,256]{2,1,0:T(8,128)(2,1)S(1)}, bf16[4,96,256]{2,1,0:T(8,128)(2,1)S(1)}, u32[]{:S(2)}, u32[]{:S(2)}) collective-permute-start(bf16[4,96,256]{2,1,0:T(8,128)(2,1)S(1)} %get-tuple-element.43.ht), channel_id=1, source_target_pairs={{1,0},{2,1},{3,2},{4,3},{5,4},{6,5},{7,6},{0,7},{9,8},{10,9},{11,1... | collective-permute-start | bytes 589832 | tf_op jit(solution)/shard_map/ppermute | solution.py:384
  32.9 3.9 %out_conv.1 = (bf16[4,6,96,256]{3,2,1,0:T(8,128)(2,1)S(1)}, bf16[4,6,96,256]{3,2,1,0:T(8,128)(2,1)S(1)}, f32[4,96,256]{2,1,0:T(8,128)S(1)}, f32[4,96,256]{2,1,0:T(8,128)S(1)}, f32[4,8,256]{2,1,0:T(8,128)S(1)}) custom-call(s32[8]{0:T(128)S(1)} %copy-done.4, f32[32]{0:T(128)S(1)} %copy-done.5, s32[1]{0:T(128)} %bitcast.1.group, ...), custom_call_target="tpu_custom_call" | custom-call | flops 1358954496 | bytes 7864320 | tf_op jit(solution)/shard_map/out_conv/pallas_call | solution.py:418
  36.8 4.4 %collective-permute-done.3.above = bf16[4,96,256]{2,1,0:T(8,128)(2,1)S(1)} collective-permute-done((bf16[4,96,256]{2,1,0:T(8,128)(2,1)S(1)}, bf16[4,96,256]{2,1,0:T(8,128)(2,1)S(1)}, u32[]{:S(2)}, u32[]{:S(2)}) %collective-permute-start.3) | collective-permute-done | bytes 196640 | tf_op jit(solution)/shard_map/ppermute | solution.py:385
  41.9 2.0 %collective-permute-start.6 = (bf16[4,96,256]{2,1,0:T(8,128)(2,1)S(1)}, bf16[4,96,256]{2,1,0:T(8,128)(2,1)S(1)}, u32[]{:S(2)}, u32[]{:S(2)}) collective-permute-start(bf16[4,96,256]{2,1,0:T(8,128)(2,1)S(1)} %get-tuple-element.50.rt), channel_id=1, source_target_pairs={{1,0},{2,1},{3,2},{4,3},{5,4},{6,5},{7,6},{0,7},{9,8},{10,9},{11,1... | collective-permute-start | bytes 589832 | tf_op jit(solution)/shard_map/ppermute | solution.py:384
  44.0 3.7 %out_grad.1.og = f32[288,288]{1,0:T(8,128)S(1)} custom-call(bf16[4,6,96,256]{3,2,1,0:T(8,128)(2,1)S(1)} %get-tuple-element.38.hm, bf16[4,96,256]{2,1,0:T(8,128)(2,1)S(1)} %get-tuple-element.43.ht, bf16[4,96,256]{2,1,0:T(8,128)(2,1)S(1)} %get-tuple-element.44.hb, bf16[4,6,96,256]{3,2,1,0:T(8,128)(2,1)S(1)} %get-tuple-element.46.rm, ...), custom_call_target="tpu_custom_call" | custom-call | flops 1358954496 | bytes 7864320 | tf_op jit(solution)/shard_map/out_grad/pallas_call | solution.py:418
  47.7 3.4 %back_conv.1 = (bf16[4,6,96,256]{3,2,1,0:T(8,128)(2,1)S(1)}, f32[4,96,256]{2,1,0:T(8,128)S(1)}, f32[4,96,256]{2,1,0:T(8,128)S(1)}) custom-call(bf16[4,6,96,256]{3,2,1,0:T(8,128)(2,1)S(1)} %get-tuple-element.46.rm, bf16[4,96,256]{2,1,0:T(8,128)(2,1)S(1)} %get-tuple-element.50.rt, bf16[4,96,256]{2,1,0:T(8,128)(2,1)S(1)} %get-tuple-element.51.rb, ...), custom_call_target="tpu_custom_call" | custom-call | flops 1358954496 | bytes 7864320 | tf_op jit(solution)/shard_map/back_conv/pallas_call | solution.py:418
  51.0 1.4 %collective-permute-done.6.below = bf16[4,96,256]{2,1,0:T(8,128)(2,1)S(1)} collective-permute-done((bf16[4,96,256]{2,1,0:T(8,128)(2,1)S(1)}, bf16[4,96,256]{2,1,0:T(8,128)(2,1)S(1)}, u32[]{:S(2)}, u32[]{:S(2)}) %collective-permute-start.6) | collective-permute-done | bytes 196640 | tf_op jit(solution)/shard_map/ppermute | solution.py:384
  53.2 3.2 %collective-permute-start.8 = (bf16[4,96,256]{2,1,0:T(8,128)(2,1)S(1)}, bf16[4,96,256]{2,1,0:T(8,128)(2,1)S(1)}, u32[]{:S(2)}, u32[]{:S(2)}) collective-permute-start(bf16[4,96,256]{2,1,0:T(8,128)(2,1)S(1)} %get-tuple-element.60.gt), channel_id=1, source_target_pairs={{1,0},{2,1},{3,2},{4,3},{5,4},{6,5},{7,6},{0,7},{9,8},{10,9},{11,1... | collective-permute-start | bytes 589832 | tf_op jit(solution)/shard_map/ppermute | solution.py:384
  56.4 6.7 %grads.1.packed_in = f32[2688,128]{1,0:T(8,128)S(1)} custom-call(s32[1]{0:T(128)} %bitcast.tile, bf16[4,6,96,256]{3,2,1,0:T(8,128)(2,1)S(1)} %get-tuple-element.54.gm, bf16[4,96,256]{2,1,0:T(8,128)(2,1)S(1)} %get-tuple-element.60.gt, bf16[4,96,256]{2,1,0:T(8,128)(2,1)S(1)} %get-tuple-element.61.gb, bf16[4,8,192,256]{3,2,1,0:T(8,128)(2,1)S(1)} %bitcast.20, ...), custom_call_target="tpu_custom_call" | custom-call | flops 4076863488 | bytes 15728640 | tf_op jit(solution)/shard_map/grads/pallas_call | solution.py:418
  63.1 1.7 %collective-permute-done.7.above = bf16[4,96,256]{2,1,0:T(8,128)(2,1)S(1)} collective-permute-done((bf16[4,96,256]{2,1,0:T(8,128)(2,1)S(1)}, bf16[4,96,256]{2,1,0:T(8,128)(2,1)S(1)}, u32[]{:S(2)}, u32[]{:S(2)}) %collective-permute-start.7) | collective-permute-done | bytes 196640 | tf_op jit(solution)/shard_map/ppermute | solution.py:385
  65.9 1.6 %collective-permute-done.9 = bf16[1344,128]{1,0:T(8,128)(2,1)S(1)} collective-permute-done((bf16[1344,128]{1,0:T(8,128)(2,1)S(1)}, bf16[1344,128]{1,0:T(8,128)(2,1)S(1)}, u32[]{:S(2)}, u32[]{:S(2)}) %collective-permute-start.9) | collective-permute-done | bytes 344096 | tf_op jit(solution)/shard_map/ppermute | solution.py:572
  72.5 1.5 %collective-permute-done.10 = bf16[336,128]{1,0:T(8,128)(2,1)S(1)} collective-permute-done((bf16[336,128]{1,0:T(8,128)(2,1)S(1)}, bf16[336,128]{1,0:T(8,128)(2,1)S(1)}, u32[]{:S(2)}, u32[]{:S(2)}) %collective-permute-start.10) | collective-permute-done | bytes 86048 | tf_op jit(solution)/shard_map/ppermute | solution.py:577
  76.5 2.5 %maximum_bitcast_fusion = bf16[4,96,8,256]{3,2,1,0:T(8,128)(2,1)} fusion(bf16[4,1,96,256]{3,1,2,0:T(2,128)(2,1)S(1)} %copy.29, bf16[4,6,96,256]{3,1,2,0:T(8,128)(2,1)S(1)} %copy.28, bf16[4,1,96,256]{3,1,2,0:T(2,128)(2,1)S(1)} %copy.27), kind=kLoop, calls=%fused_computation.1 | loop fusion | flops 4718592 | bytes 3145728 | tf_op jit(solution)/shard_map/transpose | solution.py:544
  78.9 2.8 %collective-permute-done.13 = bf16[336,128]{1,0:T(8,128)(2,1)S(1)} collective-permute-done((bf16[336,128]{1,0:T(8,128)(2,1)S(1)}, bf16[336,128]{1,0:T(8,128)(2,1)S(1)}, u32[]{:S(2)}, u32[]{:S(2)}) %collective-permute-start.13) | collective-permute-done | bytes 86048 | tf_op jit(solution)/shard_map/ppermute | solution.py:577
  83.3 2.0 %collective-permute-start.14 = (bf16[336,128]{1,0:T(8,128)(2,1)S(1)}, bf16[336,128]{1,0:T(8,128)(2,1)S(1)}, u32[]{:S(2)}, u32[]{:S(2)}) collective-permute-start(bf16[336,128]{1,0:T(8,128)(2,1)S(1)} %add_convert_fusion.refs_0_), channel_id=1, source_target_pairs={{0,1},{1,0},{2,3},{3,2},{4,5},{5,4},{6,7},{7,6},{8,9},{9,8},{10,11... | collective-permute-start | bytes 258056 | tf_op jit(solution)/shard_map/ppermute | solution.py:577
  85.3 1.9 %collective-permute-done.16.refs_3_ = bf16[336,128]{1,0:T(8,128)(2,1)S(1)} collective-permute-done((bf16[336,128]{1,0:T(8,128)(2,1)S(1)}, bf16[336,128]{1,0:T(8,128)(2,1)S(1)}, u32[]{:S(2)}, u32[]{:S(2)}) %collective-permute-start.16) | collective-permute-done | bytes 86048 | tf_op jit(solution)/shard_map/ppermute | solution.py:577
  89.4 1.6 %unpack.1 = (f32[3,3,96,288]{3,2,1,0:T(8,128)}, f32[3,3,96,96]{3,2,1,0:T(8,128)}) custom-call(s32[1]{0:T(128)} %bitcast.1.group, s32[1]{0:T(128)} %bitcast.tile, bf16[336,128]{1,0:T(8,128)(2,1)S(1)} %add_convert_fusion.refs_0_, bf16[336,128]{1,0:T(8,128)(2,1)S(1)} %collective-permute-done.14.refs_1_, bf16[336,128]{1,0:T(8,128)(2,1)S(1)} %collective-permute-done.15.refs_2_, ...), custom_call_target="tpu_custom_call" | custom-call | bytes 2752512 | tf_op jit(solution)/shard_map/unpack/pallas_call | solution.py:418
  (58 shorter events, 16.6 us)
Async XLA Ops:
  0.6 5.1 %copy-start.2 = (s32[8,2]{0,1:T(2,128)S(1)}, s32[8,2]{0,1:T(2,128)}, u32[]{:S(2)}) copy-start(s32[8,2]{0,1:T(2,128)} %param.10) | copy-start | bytes 196
  5.0 6.3 %collective-permute-start = (bf16[8,96,8,256]{3,2,1,0:T(8,128)(2,1)}, bf16[8,96,8,256]{3,2,1,0:T(8,128)(2,1)}, u32[]{:S(2)}, u32[]{:S(2)}) collective-permute-start(bf16[8,96,8,256]{3,2,1,0:T(8,128)(2,1)} %gather_out.1), channel_id=1, source_target_pairs={{0,8},{8,0},{1,9},{9,1},{2,10},{10,2},{3,11},{11,3},{4,12},{12,4},... | collective-permute-start | bytes 9437192 | tf_op jit(solution)/shard_map/ppermute | solution.py:463
  15.3 11.7 %collective-permute-start.1 = (bf16[4,96,256]{2,1,0:T(8,128)(2,1)S(1)}, bf16[4,96,256]{2,1,0:T(8,128)(2,1)S(1)}, u32[]{:S(2)}, u32[]{:S(2)}) collective-permute-start(bf16[4,96,256]{2,1,0:T(8,128)(2,1)S(1)} %get-tuple-element.41), channel_id=1, source_target_pairs={{1,0},{2,1},{3,2},{4,3},{5,4},{6,5},{7,6},{0,7},{9,8},{10,9},{11,1... | collective-permute-start | bytes 589832 | tf_op jit(solution)/shard_map/ppermute | solution.py:384
  21.1 9.4 %collective-permute-start.2 = (bf16[4,96,256]{2,1,0:T(8,128)(2,1)S(1)}, bf16[4,96,256]{2,1,0:T(8,128)(2,1)S(1)}, u32[]{:S(2)}, u32[]{:S(2)}) collective-permute-start(bf16[4,96,256]{2,1,0:T(8,128)(2,1)S(1)} %get-tuple-element.42), channel_id=1, source_target_pairs={{0,1},{1,2},{2,3},{3,4},{4,5},{5,6},{6,7},{7,0},{8,9},{9,10},{10,1... | collective-permute-start | bytes 589832 | tf_op jit(solution)/shard_map/ppermute | solution.py:385
  21.1 11.7 %copy-start.4 = (s32[8]{0:T(128)S(1)}, s32[8]{0:T(128)}, u32[]{:S(2)}) copy-start(s32[8]{0:T(128)} %numbers.1) | copy-start | bytes 100
  21.1 11.7 %copy-start.5 = (f32[32]{0:T(128)S(1)}, f32[32]{0:T(128)}, u32[]{:S(2)}) copy-start(f32[32]{0:T(128)} %rates.1) | copy-start | bytes 388
  30.8 6.0 %collective-permute-start.4 = (bf16[4,96,256]{2,1,0:T(8,128)(2,1)S(1)}, bf16[4,96,256]{2,1,0:T(8,128)(2,1)S(1)}, u32[]{:S(2)}, u32[]{:S(2)}) collective-permute-start(bf16[4,96,256]{2,1,0:T(8,128)(2,1)S(1)} %get-tuple-element.43.ht), channel_id=1, source_target_pairs={{1,0},{2,1},{3,2},{4,3},{5,4},{6,5},{7,6},{0,7},{9,8},{10,9},{11,1... | collective-permute-start | bytes 589832 | tf_op jit(solution)/shard_map/ppermute | solution.py:384
  32.9 8.4 %collective-permute-start.3 = (bf16[4,96,256]{2,1,0:T(8,128)(2,1)S(1)}, bf16[4,96,256]{2,1,0:T(8,128)(2,1)S(1)}, u32[]{:S(2)}, u32[]{:S(2)}) collective-permute-start(bf16[4,96,256]{2,1,0:T(8,128)(2,1)S(1)} %get-tuple-element.44.hb), channel_id=1, source_target_pairs={{0,1},{1,2},{2,3},{3,4},{4,5},{5,6},{6,7},{7,0},{8,9},{9,10},{10,1... | collective-permute-start | bytes 589832 | tf_op jit(solution)/shard_map/ppermute | solution.py:385
  41.9 10.6 %collective-permute-start.6 = (bf16[4,96,256]{2,1,0:T(8,128)(2,1)S(1)}, bf16[4,96,256]{2,1,0:T(8,128)(2,1)S(1)}, u32[]{:S(2)}, u32[]{:S(2)}) collective-permute-start(bf16[4,96,256]{2,1,0:T(8,128)(2,1)S(1)} %get-tuple-element.50.rt), channel_id=1, source_target_pairs={{1,0},{2,1},{3,2},{4,3},{5,4},{6,5},{7,6},{0,7},{9,8},{10,9},{11,1... | collective-permute-start | bytes 589832 | tf_op jit(solution)/shard_map/ppermute | solution.py:384
  43.9 8.6 %collective-permute-start.5 = (bf16[4,96,256]{2,1,0:T(8,128)(2,1)S(1)}, bf16[4,96,256]{2,1,0:T(8,128)(2,1)S(1)}, u32[]{:S(2)}, u32[]{:S(2)}) collective-permute-start(bf16[4,96,256]{2,1,0:T(8,128)(2,1)S(1)} %get-tuple-element.51.rb), channel_id=1, source_target_pairs={{0,1},{1,2},{2,3},{3,4},{4,5},{5,6},{6,7},{7,0},{8,9},{9,10},{10,1... | collective-permute-start | bytes 589832 | tf_op jit(solution)/shard_map/ppermute | solution.py:385
  53.2 10.0 %collective-permute-start.8 = (bf16[4,96,256]{2,1,0:T(8,128)(2,1)S(1)}, bf16[4,96,256]{2,1,0:T(8,128)(2,1)S(1)}, u32[]{:S(2)}, u32[]{:S(2)}) collective-permute-start(bf16[4,96,256]{2,1,0:T(8,128)(2,1)S(1)} %get-tuple-element.60.gt), channel_id=1, source_target_pairs={{1,0},{2,1},{3,2},{4,3},{5,4},{6,5},{7,6},{0,7},{9,8},{10,9},{11,1... | collective-permute-start | bytes 589832 | tf_op jit(solution)/shard_map/ppermute | solution.py:384
  56.4 8.4 %collective-permute-start.7 = (bf16[4,96,256]{2,1,0:T(8,128)(2,1)S(1)}, bf16[4,96,256]{2,1,0:T(8,128)(2,1)S(1)}, u32[]{:S(2)}, u32[]{:S(2)}) collective-permute-start(bf16[4,96,256]{2,1,0:T(8,128)(2,1)S(1)} %get-tuple-element.61.gb), channel_id=1, source_target_pairs={{0,1},{1,2},{2,3},{3,4},{4,5},{5,6},{6,7},{7,0},{8,9},{9,10},{10,1... | collective-permute-start | bytes 589832 | tf_op jit(solution)/shard_map/ppermute | solution.py:385
  65.8 1.7 %collective-permute-start.9 = (bf16[1344,128]{1,0:T(8,128)(2,1)S(1)}, bf16[1344,128]{1,0:T(8,128)(2,1)S(1)}, u32[]{:S(2)}, u32[]{:S(2)}) collective-permute-start(bf16[1344,128]{1,0:T(8,128)(2,1)S(1)} %get-tuple-element.63), channel_id=1, source_target_pairs={{0,8},{8,0},{1,9},{9,1},{2,10},{10,2},{3,11},{11,3},{4,12},{12,4},... | collective-permute-start | bytes 1032200 | tf_op jit(solution)/shard_map/ppermute | solution.py:572
  67.6 6.4 %collective-permute-start.10 = (bf16[336,128]{1,0:T(8,128)(2,1)S(1)}, bf16[336,128]{1,0:T(8,128)(2,1)S(1)}, u32[]{:S(2)}, u32[]{:S(2)}) collective-permute-start(bf16[336,128]{1,0:T(8,128)(2,1)S(1)} %get-tuple-element.71), channel_id=1, source_target_pairs={{0,1},{1,0},{2,3},{3,2},{4,5},{5,4},{6,7},{7,6},{8,9},{9,8},{10,11... | collective-permute-start | bytes 258056 | tf_op jit(solution)/shard_map/ppermute | solution.py:577
  68.4 5.8 %collective-permute-start.12 = (bf16[336,128]{1,0:T(8,128)(2,1)S(1)}, bf16[336,128]{1,0:T(8,128)(2,1)S(1)}, u32[]{:S(2)}, u32[]{:S(2)}) collective-permute-start(bf16[336,128]{1,0:T(8,128)(2,1)S(1)} %get-tuple-element.72), channel_id=1, source_target_pairs={{0,3},{1,2},{2,1},{3,0},{4,7},{5,6},{6,5},{7,4},{8,11},{9,10},{10,... | collective-permute-start | bytes 258056 | tf_op jit(solution)/shard_map/ppermute | solution.py:577
  69.8 5.5 %collective-permute-start.11 = (bf16[336,128]{1,0:T(8,128)(2,1)S(1)}, bf16[336,128]{1,0:T(8,128)(2,1)S(1)}, u32[]{:S(2)}, u32[]{:S(2)}) collective-permute-start(bf16[336,128]{1,0:T(8,128)(2,1)S(1)} %get-tuple-element.73), channel_id=1, source_target_pairs={{0,2},{1,3},{2,0},{3,1},{4,6},{5,7},{6,4},{7,5},{8,10},{9,11},{10,... | collective-permute-start | bytes 258056 | tf_op jit(solution)/shard_map/ppermute | solution.py:577
  75.4 6.4 %collective-permute-start.13 = (bf16[336,128]{1,0:T(8,128)(2,1)S(1)}, bf16[336,128]{1,0:T(8,128)(2,1)S(1)}, u32[]{:S(2)}, u32[]{:S(2)}) collective-permute-start(bf16[336,128]{1,0:T(8,128)(2,1)S(1)} %add_convert_fusion.1), channel_id=1, source_target_pairs={{0,4},{1,5},{2,6},{3,7},{4,0},{5,1},{6,2},{7,3},{8,12},{9,13},{10,... | collective-permute-start | bytes 258056 | tf_op jit(solution)/shard_map/ppermute | solution.py:577
  81.8 5.5 %collective-permute-start.16 = (bf16[336,128]{1,0:T(8,128)(2,1)S(1)}, bf16[336,128]{1,0:T(8,128)(2,1)S(1)}, u32[]{:S(2)}, u32[]{:S(2)}) collective-permute-start(bf16[336,128]{1,0:T(8,128)(2,1)S(1)} %add_convert_fusion.refs_0_), channel_id=1, source_target_pairs={{0,3},{1,2},{2,1},{3,0},{4,7},{5,6},{6,5},{7,4},{8,11},{9,10},{10,... | collective-permute-start | bytes 258056 | tf_op jit(solution)/shard_map/ppermute | solution.py:577
  82.9 4.5 %collective-permute-start.15 = (bf16[336,128]{1,0:T(8,128)(2,1)S(1)}, bf16[336,128]{1,0:T(8,128)(2,1)S(1)}, u32[]{:S(2)}, u32[]{:S(2)}) collective-permute-start(bf16[336,128]{1,0:T(8,128)(2,1)S(1)} %add_convert_fusion.refs_0_), channel_id=1, source_target_pairs={{0,2},{1,3},{2,0},{3,1},{4,6},{5,7},{6,4},{7,5},{8,10},{9,11},{10,... | collective-permute-start | bytes 258056 | tf_op jit(solution)/shard_map/ppermute | solution.py:577
  83.3 4.8 %collective-permute-start.14 = (bf16[336,128]{1,0:T(8,128)(2,1)S(1)}, bf16[336,128]{1,0:T(8,128)(2,1)S(1)}, u32[]{:S(2)}, u32[]{:S(2)}) collective-permute-start(bf16[336,128]{1,0:T(8,128)(2,1)S(1)} %add_convert_fusion.refs_0_), channel_id=1, source_target_pairs={{0,1},{1,0},{2,3},{3,2},{4,5},{5,4},{6,7},{7,6},{8,9},{9,8},{10,11... | collective-permute-start | bytes 258056 | tf_op jit(solution)/shard_map/ppermute | solution.py:577
  85.3 2.8 %collective-permute-start.17 = (bf16[336,128]{1,0:T(8,128)(2,1)S(1)}, bf16[336,128]{1,0:T(8,128)(2,1)S(1)}, u32[]{:S(2)}, u32[]{:S(2)}) collective-permute-start(bf16[336,128]{1,0:T(8,128)(2,1)S(1)} %add_convert_fusion.refs_0_), channel_id=1, source_target_pairs={{0,8},{8,0},{1,9},{9,1},{2,10},{10,2},{3,11},{11,3},{4,12},{12,4},... | collective-permute-start | bytes 258056 | tf_op jit(solution)/shard_map/ppermute | solution.py:593
  87.2 1.3 %collective-permute-start.20 = (bf16[336,128]{1,0:T(8,128)(2,1)S(1)}, bf16[336,128]{1,0:T(8,128)(2,1)S(1)}, u32[]{:S(2)}, u32[]{:S(2)}) collective-permute-start(bf16[336,128]{1,0:T(8,128)(2,1)S(1)} %collective-permute-done.16.refs_3_), channel_id=1, source_target_pairs={{0,8},{8,0},{1,9},{9,1},{2,10},{10,2},{3,11},{11,3},{4,12},{12,4},... | collective-permute-start | bytes 258056 | tf_op jit(solution)/shard_map/ppermute | solution.py:593
  87.4 1.3 %collective-permute-start.19 = (bf16[336,128]{1,0:T(8,128)(2,1)S(1)}, bf16[336,128]{1,0:T(8,128)(2,1)S(1)}, u32[]{:S(2)}, u32[]{:S(2)}) collective-permute-start(bf16[336,128]{1,0:T(8,128)(2,1)S(1)} %collective-permute-done.15.refs_2_), channel_id=1, source_target_pairs={{0,8},{8,0},{1,9},{9,1},{2,10},{10,2},{3,11},{11,3},{4,12},{12,4},... | collective-permute-start | bytes 258056 | tf_op jit(solution)/shard_map/ppermute | solution.py:593
  88.1 1.3 %collective-permute-start.18 = (bf16[336,128]{1,0:T(8,128)(2,1)S(1)}, bf16[336,128]{1,0:T(8,128)(2,1)S(1)}, u32[]{:S(2)}, u32[]{:S(2)}) collective-permute-start(bf16[336,128]{1,0:T(8,128)(2,1)S(1)} %collective-permute-done.14.refs_1_), channel_id=1, source_target_pairs={{0,8},{8,0},{1,9},{9,1},{2,10},{10,2},{3,11},{11,3},{4,12},{12,4},... | collective-permute-start | bytes 258056 | tf_op jit(solution)/shard_map/ppermute | solution.py:593
  (3 other events, 9.2 us)

commit v5 on v4

--- a/solution.py
+++ b/solution.py
@@ -551,7 +551,7 @@
     g_above, g_below = swap_edges(gt, gb, "tile")
 
     near = 4 if count % 4 == 0 else count
-    unit = 16 * 2 * near
+    unit = 8 * 2 * near
     packed_rows = 3 * taps * (joined + channels) // LANES
     packed_s = struct((pl.cdiv(packed_rows, unit) * unit, LANES), F32)
     half_s = struct((packed_s.shape[0] // 2, LANES), F32)

time: 91.6 us -> 91.3 us (level)
  no operation moved by 1% of the time
where the time goes in v5:
time: 91.3 us; the launch traced here: 90.9 us
  Pallas kernels  36 us (39%)
  starting transfers between devices  22.6 us (25%)
  waiting for transfers between devices  22.1 us (24%)
  other arithmetic  5.9 us (6%)
  local copies, waits for them, and re-layouts  3.43 us (4%)
  between operations  0.92 us (1%)
    pallas_call x14, Pallas kernels, run(): call(body, name, flops, nbytes, vmem, grid_spec=pltpu.PrefetchScalarGridS...  36 us
    ppermute x4, starting transfers between devices, swap_edges(): below = lax.ppermute(up, axis, [((i + 1) % count, i) for i in range(count)])  13.3 us
    ppermute x4, waiting for transfers between devices, swap_edges(): lax.ppermute(down, axis, [(i, (i + 1) % count) for i in range(count)])  9.56 us
    ppermute x7, starting transfers between devices, trade(): return lax.ppermute(x, 'tile', [(i, i ^ mask) for i in range(count)])  8.23 us
    ppermute x7, waiting for transfers between devices, trade(): return lax.ppermute(x, 'tile', [(i, i ^ mask) for i in range(count)])  7.87 us
    select_n x1, other arithmetic, on_device(): jnp.where(held[:, :, None, None, None], own.reshape(frames, 2, channels,...  3.09 us
    transpose x1, other arithmetic, on_device(): jnp.concatenate([ct[:, None], cm, cb[:, None]], 1).transpose(0, 2, 1, 3)  2.45 us
    unnamed x13, local copies, waits for them, and re-layouts  1.87 us
  transfers between devices with their start and end apart: 21, of which 16 were waited for; matrix products, arithmetic and copies ran while one was open for 7% of the time, Pallas kernels for 29%

profile of v5, /device:TPU:0, one launch (start us, length us, event | category | flops | bytes accessed | tf_op | source)
XLA Modules:
  0.0 90.9 jit_solution(1379699534598400615)
XLA Ops:
  0.7 4.5 %gather_out.1 = bf16[8,96,8,256]{3,2,1,0:T(8,128)(2,1)} custom-call(s32[2,8]{1,0:T(2,128)} %bitcast.39, s32[32]{0:T(128)} %slots.3, s32[1]{0:T(128)} %bitcast.1.group, bf16[16,96,8,256]{3,2,1,0:T(8,128)(2,1)} %refs.3), custom_call_target="tpu_custom_call" | custom-call | bytes 6291456 | tf_op jit(solution)/shard_map/gather_out/pallas_call | solution.py:418
  5.7 2.6 %gather_own.1 = bf16[8,96,8,256]{3,2,1,0:T(8,128)(2,1)S(1)} custom-call(s32[2,8]{1,0:T(2,128)S(1)} %bitcast.40, s32[32]{0:T(128)S(1)} %copy-done.3, s32[1]{0:T(128)} %bitcast.1.group, bf16[16,96,8,256]{3,2,1,0:T(8,128)(2,1)} %refs.3), custom_call_target="tpu_custom_call" | custom-call | bytes 6291456 | tf_op jit(solution)/shard_map/gather_own/pallas_call | solution.py:418
  8.7 1.8 %copy.33 = bf16[4,96,8,256]{3,1,2,0:T(8,128)(2,1)S(1)} copy(bf16[4,96,8,256]{3,2,1,0:T(8,128)(2,1)} %param.9) | data formatting | bytes 3145728 | tf_op args[1]
  11.3 3.1 %copy_select_fusion = bf16[4,2,96,8,256]{4,2,1,3,0:T(8,128)(2,1)S(1)} fusion(bf16[4,2,96,8,256]{4,3,2,1,0:T(8,128)(2,1)} %bitcast.4, bf16[4,2,96,8,256]{4,3,2,1,0:T(8,128)(2,1)S(1)} %bitcast.32, pred[4,2]{1,0:T(4,128)(4,1)S(1)} %copy.23), kind=kLoop, calls=%fused_computation | loop fusion | flops 1572864 | bytes 9437192 | tf_op jit(solution)/shard_map/jit(_where)/select_n | solution.py:469
  15.2 6.0 %collective-permute-start.1 = (bf16[4,96,256]{2,1,0:T(8,128)(2,1)S(1)}, bf16[4,96,256]{2,1,0:T(8,128)(2,1)S(1)}, u32[]{:S(2)}, u32[]{:S(2)}) collective-permute-start(bf16[4,96,256]{2,1,0:T(8,128)(2,1)S(1)} %get-tuple-element.41), channel_id=1, source_target_pairs={{1,0},{2,1},{3,2},{4,3},{5,4},{6,5},{7,6},{0,7},{9,8},{10,9},{11,1... | collective-permute-start | bytes 589832 | tf_op jit(solution)/shard_map/ppermute | solution.py:384
  21.2 5.9 %join_conv.1 = (bf16[4,6,96,256]{3,2,1,0:T(8,128)(2,1)S(1)}, f32[4,6,96,256]{3,2,1,0:T(8,128)S(1)}, f32[4,96,256]{2,1,0:T(8,128)S(1)}, f32[4,96,256]{2,1,0:T(8,128)S(1)}) custom-call(bf16[4,8,192,256]{3,2,1,0:T(8,128)(2,1)S(1)} %bitcast.19, bf16[4,8,96,256]{3,2,1,0:T(8,128)(2,1)S(1)} %bitcast.25, bf16[288,864]{1,0:T(8,128)(2,1)S(1)} %get-tuple-element.37.w), custom_call_target="tpu_custom_call" | custom-call | flops 4076863488 | bytes 7864320 | tf_op jit(solution)/shard_map/join_conv/pallas_call | solution.py:418
  27.1 3.5 %collective-permute-done.2.above = bf16[4,96,256]{2,1,0:T(8,128)(2,1)S(1)} collective-permute-done((bf16[4,96,256]{2,1,0:T(8,128)(2,1)S(1)}, bf16[4,96,256]{2,1,0:T(8,128)(2,1)S(1)}, u32[]{:S(2)}, u32[]{:S(2)}) %collective-permute-start.2) | collective-permute-done | bytes 196640 | tf_op jit(solution)/shard_map/ppermute | solution.py:385
  30.9 2.1 %collective-permute-start.4 = (bf16[4,96,256]{2,1,0:T(8,128)(2,1)S(1)}, bf16[4,96,256]{2,1,0:T(8,128)(2,1)S(1)}, u32[]{:S(2)}, u32[]{:S(2)}) collective-permute-start(bf16[4,96,256]{2,1,0:T(8,128)(2,1)S(1)} %get-tuple-element.43.ht), channel_id=1, source_target_pairs={{1,0},{2,1},{3,2},{4,3},{5,4},{6,5},{7,6},{0,7},{9,8},{10,9},{11,1... | collective-permute-start | bytes 589832 | tf_op jit(solution)/shard_map/ppermute | solution.py:384
  33.0 3.9 %out_conv.1 = (bf16[4,6,96,256]{3,2,1,0:T(8,128)(2,1)S(1)}, bf16[4,6,96,256]{3,2,1,0:T(8,128)(2,1)S(1)}, f32[4,96,256]{2,1,0:T(8,128)S(1)}, f32[4,96,256]{2,1,0:T(8,128)S(1)}, f32[4,8,256]{2,1,0:T(8,128)S(1)}) custom-call(s32[8]{0:T(128)S(1)} %copy-done.4, f32[32]{0:T(128)S(1)} %copy-done.5, s32[1]{0:T(128)} %bitcast.1.group, ...), custom_call_target="tpu_custom_call" | custom-call | flops 1358954496 | bytes 7864320 | tf_op jit(solution)/shard_map/out_conv/pallas_call | solution.py:418
  36.9 4.4 %collective-permute-done.3.above = bf16[4,96,256]{2,1,0:T(8,128)(2,1)S(1)} collective-permute-done((bf16[4,96,256]{2,1,0:T(8,128)(2,1)S(1)}, bf16[4,96,256]{2,1,0:T(8,128)(2,1)S(1)}, u32[]{:S(2)}, u32[]{:S(2)}) %collective-permute-start.3) | collective-permute-done | bytes 196640 | tf_op jit(solution)/shard_map/ppermute | solution.py:385
  42.0 2.0 %collective-permute-start.6 = (bf16[4,96,256]{2,1,0:T(8,128)(2,1)S(1)}, bf16[4,96,256]{2,1,0:T(8,128)(2,1)S(1)}, u32[]{:S(2)}, u32[]{:S(2)}) collective-permute-start(bf16[4,96,256]{2,1,0:T(8,128)(2,1)S(1)} %get-tuple-element.50.rt), channel_id=1, source_target_pairs={{1,0},{2,1},{3,2},{4,3},{5,4},{6,5},{7,6},{0,7},{9,8},{10,9},{11,1... | collective-permute-start | bytes 589832 | tf_op jit(solution)/shard_map/ppermute | solution.py:384
  44.1 3.7 %out_grad.1.og = f32[288,288]{1,0:T(8,128)S(1)} custom-call(bf16[4,6,96,256]{3,2,1,0:T(8,128)(2,1)S(1)} %get-tuple-element.38.hm, bf16[4,96,256]{2,1,0:T(8,128)(2,1)S(1)} %get-tuple-element.43.ht, bf16[4,96,256]{2,1,0:T(8,128)(2,1)S(1)} %get-tuple-element.44.hb, bf16[4,6,96,256]{3,2,1,0:T(8,128)(2,1)S(1)} %get-tuple-element.46.rm, ...), custom_call_target="tpu_custom_call" | custom-call | flops 1358954496 | bytes 7864320 | tf_op jit(solution)/shard_map/out_grad/pallas_call | solution.py:418
  47.8 3.4 %back_conv.1 = (bf16[4,6,96,256]{3,2,1,0:T(8,128)(2,1)S(1)}, f32[4,96,256]{2,1,0:T(8,128)S(1)}, f32[4,96,256]{2,1,0:T(8,128)S(1)}) custom-call(bf16[4,6,96,256]{3,2,1,0:T(8,128)(2,1)S(1)} %get-tuple-element.46.rm, bf16[4,96,256]{2,1,0:T(8,128)(2,1)S(1)} %get-tuple-element.50.rt, bf16[4,96,256]{2,1,0:T(8,128)(2,1)S(1)} %get-tuple-element.51.rb, ...), custom_call_target="tpu_custom_call" | custom-call | flops 1358954496 | bytes 7864320 | tf_op jit(solution)/shard_map/back_conv/pallas_call | solution.py:418
  51.2 1.4 %collective-permute-done.6.below = bf16[4,96,256]{2,1,0:T(8,128)(2,1)S(1)} collective-permute-done((bf16[4,96,256]{2,1,0:T(8,128)(2,1)S(1)}, bf16[4,96,256]{2,1,0:T(8,128)(2,1)S(1)}, u32[]{:S(2)}, u32[]{:S(2)}) %collective-permute-start.6) | collective-permute-done | bytes 196640 | tf_op jit(solution)/shard_map/ppermute | solution.py:384
  53.3 3.3 %collective-permute-start.8 = (bf16[4,96,256]{2,1,0:T(8,128)(2,1)S(1)}, bf16[4,96,256]{2,1,0:T(8,128)(2,1)S(1)}, u32[]{:S(2)}, u32[]{:S(2)}) collective-permute-start(bf16[4,96,256]{2,1,0:T(8,128)(2,1)S(1)} %get-tuple-element.60.gt), channel_id=1, source_target_pairs={{1,0},{2,1},{3,2},{4,3},{5,4},{6,5},{7,6},{0,7},{9,8},{10,9},{11,1... | collective-permute-start | bytes 589832 | tf_op jit(solution)/shard_map/ppermute | solution.py:384
  56.5 6.7 %grads.1.packed_in = f32[2624,128]{1,0:T(8,128)S(1)} custom-call(s32[1]{0:T(128)} %bitcast.tile, bf16[4,6,96,256]{3,2,1,0:T(8,128)(2,1)S(1)} %get-tuple-element.54.gm, bf16[4,96,256]{2,1,0:T(8,128)(2,1)S(1)} %get-tuple-element.60.gt, bf16[4,96,256]{2,1,0:T(8,128)(2,1)S(1)} %get-tuple-element.61.gb, bf16[4,8,192,256]{3,2,1,0:T(8,128)(2,1)S(1)} %bitcast.20, ...), custom_call_target="tpu_custom_call" | custom-call | flops 4076863488 | bytes 15728640 | tf_op jit(solution)/shard_map/grads/pallas_call | solution.py:418
  63.2 1.7 %collective-permute-done.7.above = bf16[4,96,256]{2,1,0:T(8,128)(2,1)S(1)} collective-permute-done((bf16[4,96,256]{2,1,0:T(8,128)(2,1)S(1)}, bf16[4,96,256]{2,1,0:T(8,128)(2,1)S(1)}, u32[]{:S(2)}, u32[]{:S(2)}) %collective-permute-start.7) | collective-permute-done | bytes 196640 | tf_op jit(solution)/shard_map/ppermute | solution.py:385
  66.1 1.6 %collective-permute-done.9 = bf16[1312,128]{1,0:T(8,128)(2,1)S(1)} collective-permute-done((bf16[1312,128]{1,0:T(8,128)(2,1)S(1)}, bf16[1312,128]{1,0:T(8,128)(2,1)S(1)}, u32[]{:S(2)}, u32[]{:S(2)}) %collective-permute-start.9) | collective-permute-done | bytes 335904 | tf_op jit(solution)/shard_map/ppermute | solution.py:572
  68.5 1.4 %collective-permute-start.12 = (bf16[328,128]{1,0:T(8,128)(2,1)S(1)}, bf16[328,128]{1,0:T(8,128)(2,1)S(1)}, u32[]{:S(2)}, u32[]{:S(2)}) collective-permute-start(bf16[328,128]{1,0:T(8,128)(2,1)S(1)} %get-tuple-element.72), channel_id=1, source_target_pairs={{0,3},{1,2},{2,1},{3,0},{4,7},{5,6},{6,5},{7,4},{8,11},{9,10},{10,... | collective-permute-start | bytes 251912 | tf_op jit(solution)/shard_map/ppermute | solution.py:577
  76.5 2.5 %maximum_bitcast_fusion = bf16[4,96,8,256]{3,2,1,0:T(8,128)(2,1)} fusion(bf16[4,1,96,256]{3,1,2,0:T(2,128)(2,1)S(1)} %copy.29, bf16[4,6,96,256]{3,1,2,0:T(8,128)(2,1)S(1)} %copy.28, bf16[4,1,96,256]{3,1,2,0:T(2,128)(2,1)S(1)} %copy.27), kind=kLoop, calls=%fused_computation.1 | loop fusion | flops 4718592 | bytes 3145728 | tf_op jit(solution)/shard_map/transpose | solution.py:544
  79.0 2.8 %collective-permute-done.13 = bf16[328,128]{1,0:T(8,128)(2,1)S(1)} collective-permute-done((bf16[328,128]{1,0:T(8,128)(2,1)S(1)}, bf16[328,128]{1,0:T(8,128)(2,1)S(1)}, u32[]{:S(2)}, u32[]{:S(2)}) %collective-permute-start.13) | collective-permute-done | bytes 84000 | tf_op jit(solution)/shard_map/ppermute | solution.py:577
  83.4 1.9 %collective-permute-start.14 = (bf16[328,128]{1,0:T(8,128)(2,1)S(1)}, bf16[328,128]{1,0:T(8,128)(2,1)S(1)}, u32[]{:S(2)}, u32[]{:S(2)}) collective-permute-start(bf16[328,128]{1,0:T(8,128)(2,1)S(1)} %add_convert_fusion.refs_0_), channel_id=1, source_target_pairs={{0,1},{1,0},{2,3},{3,2},{4,5},{5,4},{6,7},{7,6},{8,9},{9,8},{10,11... | collective-permute-start | bytes 251912 | tf_op jit(solution)/shard_map/ppermute | solution.py:577
  85.3 1.9 %collective-permute-done.16.refs_3_ = bf16[328,128]{1,0:T(8,128)(2,1)S(1)} collective-permute-done((bf16[328,128]{1,0:T(8,128)(2,1)S(1)}, bf16[328,128]{1,0:T(8,128)(2,1)S(1)}, u32[]{:S(2)}, u32[]{:S(2)}) %collective-permute-start.16) | collective-permute-done | bytes 84000 | tf_op jit(solution)/shard_map/ppermute | solution.py:577
  89.4 1.6 %unpack.1 = (f32[3,3,96,288]{3,2,1,0:T(8,128)}, f32[3,3,96,96]{3,2,1,0:T(8,128)}) custom-call(s32[1]{0:T(128)} %bitcast.1.group, s32[1]{0:T(128)} %bitcast.tile, bf16[328,128]{1,0:T(8,128)(2,1)S(1)} %add_convert_fusion.refs_0_, bf16[328,128]{1,0:T(8,128)(2,1)S(1)} %collective-permute-done.14.refs_1_, bf16[328,128]{1,0:T(8,128)(2,1)S(1)} %collective-permute-done.15.refs_2_, ...), custom_call_target="tpu_custom_call" | custom-call | bytes 2686976 | tf_op jit(solution)/shard_map/unpack/pallas_call | solution.py:418
  (58 shorter events, 16.6 us)
Async XLA Ops:
  0.6 5.0 %copy-start.2 = (s32[8,2]{0,1:T(2,128)S(1)}, s32[8,2]{0,1:T(2,128)}, u32[]{:S(2)}) copy-start(s32[8,2]{0,1:T(2,128)} %param.10) | copy-start | bytes 196
  5.1 6.2 %collective-permute-start = (bf16[8,96,8,256]{3,2,1,0:T(8,128)(2,1)}, bf16[8,96,8,256]{3,2,1,0:T(8,128)(2,1)}, u32[]{:S(2)}, u32[]{:S(2)}) collective-permute-start(bf16[8,96,8,256]{3,2,1,0:T(8,128)(2,1)} %gather_out.1), channel_id=1, source_target_pairs={{0,8},{8,0},{1,9},{9,1},{2,10},{10,2},{3,11},{11,3},{4,12},{12,4},... | collective-permute-start | bytes 9437192 | tf_op jit(solution)/shard_map/ppermute | solution.py:463
  15.2 11.9 %collective-permute-start.1 = (bf16[4,96,256]{2,1,0:T(8,128)(2,1)S(1)}, bf16[4,96,256]{2,1,0:T(8,128)(2,1)S(1)}, u32[]{:S(2)}, u32[]{:S(2)}) collective-permute-start(bf16[4,96,256]{2,1,0:T(8,128)(2,1)S(1)} %get-tuple-element.41), channel_id=1, source_target_pairs={{1,0},{2,1},{3,2},{4,3},{5,4},{6,5},{7,6},{0,7},{9,8},{10,9},{11,1... | collective-permute-start | bytes 589832 | tf_op jit(solution)/shard_map/ppermute | solution.py:384
  21.2 9.4 %collective-permute-start.2 = (bf16[4,96,256]{2,1,0:T(8,128)(2,1)S(1)}, bf16[4,96,256]{2,1,0:T(8,128)(2,1)S(1)}, u32[]{:S(2)}, u32[]{:S(2)}) collective-permute-start(bf16[4,96,256]{2,1,0:T(8,128)(2,1)S(1)} %get-tuple-element.42), channel_id=1, source_target_pairs={{0,1},{1,2},{2,3},{3,4},{4,5},{5,6},{6,7},{7,0},{8,9},{9,10},{10,1... | collective-permute-start | bytes 589832 | tf_op jit(solution)/shard_map/ppermute | solution.py:385
  21.2 11.8 %copy-start.4 = (s32[8]{0:T(128)S(1)}, s32[8]{0:T(128)}, u32[]{:S(2)}) copy-start(s32[8]{0:T(128)} %numbers.1) | copy-start | bytes 100
  21.2 11.8 %copy-start.5 = (f32[32]{0:T(128)S(1)}, f32[32]{0:T(128)}, u32[]{:S(2)}) copy-start(f32[32]{0:T(128)} %rates.1) | copy-start | bytes 388
  30.9 6.0 %collective-permute-start.4 = (bf16[4,96,256]{2,1,0:T(8,128)(2,1)S(1)}, bf16[4,96,256]{2,1,0:T(8,128)(2,1)S(1)}, u32[]{:S(2)}, u32[]{:S(2)}) collective-permute-start(bf16[4,96,256]{2,1,0:T(8,128)(2,1)S(1)} %get-tuple-element.43.ht), channel_id=1, source_target_pairs={{1,0},{2,1},{3,2},{4,3},{5,4},{6,5},{7,6},{0,7},{9,8},{10,9},{11,1... | collective-permute-start | bytes 589832 | tf_op jit(solution)/shard_map/ppermute | solution.py:384
  33.0 8.4 %collective-permute-start.3 = (bf16[4,96,256]{2,1,0:T(8,128)(2,1)S(1)}, bf16[4,96,256]{2,1,0:T(8,128)(2,1)S(1)}, u32[]{:S(2)}, u32[]{:S(2)}) collective-permute-start(bf16[4,96,256]{2,1,0:T(8,128)(2,1)S(1)} %get-tuple-element.44.hb), channel_id=1, source_target_pairs={{0,1},{1,2},{2,3},{3,4},{4,5},{5,6},{6,7},{7,0},{8,9},{9,10},{10,1... | collective-permute-start | bytes 589832 | tf_op jit(solution)/shard_map/ppermute | solution.py:385
  42.0 10.6 %collective-permute-start.6 = (bf16[4,96,256]{2,1,0:T(8,128)(2,1)S(1)}, bf16[4,96,256]{2,1,0:T(8,128)(2,1)S(1)}, u32[]{:S(2)}, u32[]{:S(2)}) collective-permute-start(bf16[4,96,256]{2,1,0:T(8,128)(2,1)S(1)} %get-tuple-element.50.rt), channel_id=1, source_target_pairs={{1,0},{2,1},{3,2},{4,3},{5,4},{6,5},{7,6},{0,7},{9,8},{10,9},{11,1... | collective-permute-start | bytes 589832 | tf_op jit(solution)/shard_map/ppermute | solution.py:384
  44.0 8.6 %collective-permute-start.5 = (bf16[4,96,256]{2,1,0:T(8,128)(2,1)S(1)}, bf16[4,96,256]{2,1,0:T(8,128)(2,1)S(1)}, u32[]{:S(2)}, u32[]{:S(2)}) collective-permute-start(bf16[4,96,256]{2,1,0:T(8,128)(2,1)S(1)} %get-tuple-element.51.rb), channel_id=1, source_target_pairs={{0,1},{1,2},{2,3},{3,4},{4,5},{5,6},{6,7},{7,0},{8,9},{9,10},{10,1... | collective-permute-start | bytes 589832 | tf_op jit(solution)/shard_map/ppermute | solution.py:385
  53.3 10.0 %collective-permute-start.8 = (bf16[4,96,256]{2,1,0:T(8,128)(2,1)S(1)}, bf16[4,96,256]{2,1,0:T(8,128)(2,1)S(1)}, u32[]{:S(2)}, u32[]{:S(2)}) collective-permute-start(bf16[4,96,256]{2,1,0:T(8,128)(2,1)S(1)} %get-tuple-element.60.gt), channel_id=1, source_target_pairs={{1,0},{2,1},{3,2},{4,3},{5,4},{6,5},{7,6},{0,7},{9,8},{10,9},{11,1... | collective-permute-start | bytes 589832 | tf_op jit(solution)/shard_map/ppermute | solution.py:384
  56.5 8.4 %collective-permute-start.7 = (bf16[4,96,256]{2,1,0:T(8,128)(2,1)S(1)}, bf16[4,96,256]{2,1,0:T(8,128)(2,1)S(1)}, u32[]{:S(2)}, u32[]{:S(2)}) collective-permute-start(bf16[4,96,256]{2,1,0:T(8,128)(2,1)S(1)} %get-tuple-element.61.gb), channel_id=1, source_target_pairs={{0,1},{1,2},{2,3},{3,4},{4,5},{5,6},{6,7},{7,0},{8,9},{9,10},{10,1... | collective-permute-start | bytes 589832 | tf_op jit(solution)/shard_map/ppermute | solution.py:385
  65.9 1.7 %collective-permute-start.9 = (bf16[1312,128]{1,0:T(8,128)(2,1)S(1)}, bf16[1312,128]{1,0:T(8,128)(2,1)S(1)}, u32[]{:S(2)}, u32[]{:S(2)}) collective-permute-start(bf16[1312,128]{1,0:T(8,128)(2,1)S(1)} %get-tuple-element.63), channel_id=1, source_target_pairs={{0,8},{8,0},{1,9},{9,1},{2,10},{10,2},{3,11},{11,3},{4,12},{12,4},... | collective-permute-start | bytes 1007624 | tf_op jit(solution)/shard_map/ppermute | solution.py:572
  67.8 6.3 %collective-permute-start.10 = (bf16[328,128]{1,0:T(8,128)(2,1)S(1)}, bf16[328,128]{1,0:T(8,128)(2,1)S(1)}, u32[]{:S(2)}, u32[]{:S(2)}) collective-permute-start(bf16[328,128]{1,0:T(8,128)(2,1)S(1)} %get-tuple-element.71), channel_id=1, source_target_pairs={{0,1},{1,0},{2,3},{3,2},{4,5},{5,4},{6,7},{7,6},{8,9},{9,8},{10,11... | collective-permute-start | bytes 251912 | tf_op jit(solution)/shard_map/ppermute | solution.py:577
  68.5 5.8 %collective-permute-start.12 = (bf16[328,128]{1,0:T(8,128)(2,1)S(1)}, bf16[328,128]{1,0:T(8,128)(2,1)S(1)}, u32[]{:S(2)}, u32[]{:S(2)}) collective-permute-start(bf16[328,128]{1,0:T(8,128)(2,1)S(1)} %get-tuple-element.72), channel_id=1, source_target_pairs={{0,3},{1,2},{2,1},{3,0},{4,7},{5,6},{6,5},{7,4},{8,11},{9,10},{10,... | collective-permute-start | bytes 251912 | tf_op jit(solution)/shard_map/ppermute | solution.py:577
  69.9 5.4 %collective-permute-start.11 = (bf16[328,128]{1,0:T(8,128)(2,1)S(1)}, bf16[328,128]{1,0:T(8,128)(2,1)S(1)}, u32[]{:S(2)}, u32[]{:S(2)}) collective-permute-start(bf16[328,128]{1,0:T(8,128)(2,1)S(1)} %get-tuple-element.73), channel_id=1, source_target_pairs={{0,2},{1,3},{2,0},{3,1},{4,6},{5,7},{6,4},{7,5},{8,10},{9,11},{10,... | collective-permute-start | bytes 251912 | tf_op jit(solution)/shard_map/ppermute | solution.py:577
  75.4 6.3 %collective-permute-start.13 = (bf16[328,128]{1,0:T(8,128)(2,1)S(1)}, bf16[328,128]{1,0:T(8,128)(2,1)S(1)}, u32[]{:S(2)}, u32[]{:S(2)}) collective-permute-start(bf16[328,128]{1,0:T(8,128)(2,1)S(1)} %add_convert_fusion.1), channel_id=1, source_target_pairs={{0,4},{1,5},{2,6},{3,7},{4,0},{5,1},{6,2},{7,3},{8,12},{9,13},{10,... | collective-permute-start | bytes 251912 | tf_op jit(solution)/shard_map/ppermute | solution.py:577
  81.7 5.4 %collective-permute-start.16 = (bf16[328,128]{1,0:T(8,128)(2,1)S(1)}, bf16[328,128]{1,0:T(8,128)(2,1)S(1)}, u32[]{:S(2)}, u32[]{:S(2)}) collective-permute-start(bf16[328,128]{1,0:T(8,128)(2,1)S(1)} %add_convert_fusion.refs_0_), channel_id=1, source_target_pairs={{0,3},{1,2},{2,1},{3,0},{4,7},{5,6},{6,5},{7,4},{8,11},{9,10},{10,... | collective-permute-start | bytes 251912 | tf_op jit(solution)/shard_map/ppermute | solution.py:577
  82.9 4.5 %collective-permute-start.15 = (bf16[328,128]{1,0:T(8,128)(2,1)S(1)}, bf16[328,128]{1,0:T(8,128)(2,1)S(1)}, u32[]{:S(2)}, u32[]{:S(2)}) collective-permute-start(bf16[328,128]{1,0:T(8,128)(2,1)S(1)} %add_convert_fusion.refs_0_), channel_id=1, source_target_pairs={{0,2},{1,3},{2,0},{3,1},{4,6},{5,7},{6,4},{7,5},{8,10},{9,11},{10,... | collective-permute-start | bytes 251912 | tf_op jit(solution)/shard_map/ppermute | solution.py:577
  83.4 4.7 %collective-permute-start.14 = (bf16[328,128]{1,0:T(8,128)(2,1)S(1)}, bf16[328,128]{1,0:T(8,128)(2,1)S(1)}, u32[]{:S(2)}, u32[]{:S(2)}) collective-permute-start(bf16[328,128]{1,0:T(8,128)(2,1)S(1)} %add_convert_fusion.refs_0_), channel_id=1, source_target_pairs={{0,1},{1,0},{2,3},{3,2},{4,5},{5,4},{6,7},{7,6},{8,9},{9,8},{10,11... | collective-permute-start | bytes 251912 | tf_op jit(solution)/shard_map/ppermute | solution.py:577
  85.3 2.8 %collective-permute-start.17 = (bf16[328,128]{1,0:T(8,128)(2,1)S(1)}, bf16[328,128]{1,0:T(8,128)(2,1)S(1)}, u32[]{:S(2)}, u32[]{:S(2)}) collective-permute-start(bf16[328,128]{1,0:T(8,128)(2,1)S(1)} %add_convert_fusion.refs_0_), channel_id=1, source_target_pairs={{0,8},{8,0},{1,9},{9,1},{2,10},{10,2},{3,11},{11,3},{4,12},{12,4},... | collective-permute-start | bytes 251912 | tf_op jit(solution)/shard_map/ppermute | solution.py:593
  87.2 1.3 %collective-permute-start.20 = (bf16[328,128]{1,0:T(8,128)(2,1)S(1)}, bf16[328,128]{1,0:T(8,128)(2,1)S(1)}, u32[]{:S(2)}, u32[]{:S(2)}) collective-permute-start(bf16[328,128]{1,0:T(8,128)(2,1)S(1)} %collective-permute-done.16.refs_3_), channel_id=1, source_target_pairs={{0,8},{8,0},{1,9},{9,1},{2,10},{10,2},{3,11},{11,3},{4,12},{12,4},... | collective-permute-start | bytes 251912 | tf_op jit(solution)/shard_map/ppermute | solution.py:593
  87.4 1.3 %collective-permute-start.19 = (bf16[328,128]{1,0:T(8,128)(2,1)S(1)}, bf16[328,128]{1,0:T(8,128)(2,1)S(1)}, u32[]{:S(2)}, u32[]{:S(2)}) collective-permute-start(bf16[328,128]{1,0:T(8,128)(2,1)S(1)} %collective-permute-done.15.refs_2_), channel_id=1, source_target_pairs={{0,8},{8,0},{1,9},{9,1},{2,10},{10,2},{3,11},{11,3},{4,12},{12,4},... | collective-permute-start | bytes 251912 | tf_op jit(solution)/shard_map/ppermute | solution.py:593
  88.1 1.3 %collective-permute-start.18 = (bf16[328,128]{1,0:T(8,128)(2,1)S(1)}, bf16[328,128]{1,0:T(8,128)(2,1)S(1)}, u32[]{:S(2)}, u32[]{:S(2)}) collective-permute-start(bf16[328,128]{1,0:T(8,128)(2,1)S(1)} %collective-permute-done.14.refs_1_), channel_id=1, source_target_pairs={{0,8},{8,0},{1,9},{9,1},{2,10},{10,2},{3,11},{11,3},{4,12},{12,4},... | collective-permute-start | bytes 251912 | tf_op jit(solution)/shard_map/ppermute | solution.py:593
  (3 other events, 9.2 us)
